TPU v7x, 32 devices: a whole 2x2x4 slice. The times are simulated.
32 devices in a mesh: gx: 8 (over z, core), gy: 4 (over y, x).
Axes of the slice: x: 2, y: 2, z: 4, core: 2. Of those that a mesh axis runs over, the one named last changes fastest.
Arguments:
- density: float32 [256, 256, 256], P('gx', 'gy'), may hold values from 0.05 to 2
Outputs:
- potential: float32 [256, 256, 256], P('gx', 'gy')
- energy: float32 [], replicated
All inputs are finite; a program needn't handle non-finite values.
Results may differ from a plain program's by a relative error of at most 0.00005.
Values sent between devices are 32-bit elements.
No kernel may reach another device: no remote copies, remote signals or barrier semaphores. Data moves between devices by JAX's collectives and lax.ppermute only.
A program may use at most 128 MiB of HBM per device.

v0:
```python
import math

import jax
import jax.numpy as jnp
from jax import lax
from jax.sharding import PartitionSpec as P

spacing = 1.0
highest = lax.Precision.HIGHEST
pbe_kappa = 0.804
pbe_mu = 0.2195149727645171
pbe_beta = 0.06672455060314922
pbe_gamma = 0.031090690869654894
pw_coef = 0.0310907
pw_alpha = 0.2137
pw_first = 7.5957
pw_second = 3.5876
pw_third = 1.6382
pw_fourth = 0.49294


def xc_energy(electrons, grad_sq):
    k_fermi = jnp.cbrt(3.0 * math.pi**2 * electrons)
    exch_unif = -0.75 * k_fermi / math.pi
    s_square = grad_sq / (4.0 * k_fermi**2 * electrons**2)
    enhance = 1.0 + pbe_kappa - pbe_kappa / (1.0 + pbe_mu * s_square / pbe_kappa)
    wigner = jnp.cbrt(3.0 / (4.0 * math.pi * electrons))
    root_rs = jnp.sqrt(wigner)
    series = (
        2.0
        * pw_coef
        * (
            pw_first * root_rs
            + pw_second * wigner
            + pw_third * wigner * root_rs
            + pw_fourth * wigner**2
        )
    )
    corr_unif = -2.0 * pw_coef * (1.0 + pw_alpha * wigner) * jnp.log(1.0 + 1.0 / series)
    screen_sq = 4.0 * k_fermi / math.pi
    t_square = grad_sq / (4.0 * screen_sq * electrons**2)
    factor = pbe_beta / pbe_gamma / jnp.expm1(-corr_unif / pbe_gamma)
    scaled = factor * t_square
    gradient_term = pbe_gamma * jnp.log(
        1.0 + pbe_beta / pbe_gamma * t_square * (1.0 + scaled) / (1.0 + scaled + scaled**2)
    )
    return electrons * (exch_unif * enhance + corr_unif + gradient_term)


def summed_energy(electrons, grad_sq):
    return jnp.sum(xc_energy(electrons, grad_sq))


def total_energy(energy_local, cells):
    return lax.psum(energy_local, ("gx", "gy")) / float(cells)


def wavenum(index, count):
    signed = jnp.where(index < count // 2, index, index - count)
    signed = jnp.where(index == count // 2, 0, signed)
    return signed.astype(jnp.float32) * (2.0 * math.pi / (count * spacing))


def dft_tables(count, order):
    columns = jnp.arange(count, dtype=jnp.int32)
    phase = (order[:, None] * columns[None, :] % count).astype(jnp.float32) * (
        2.0 * math.pi / count
    )
    return (jnp.cos(phase), jnp.sin(phase))


def deriv_matrix(count):
    positions = jnp.arange(count, dtype=jnp.int32)
    cosine, sine = dft_tables(count, positions)
    waves = wavenum(positions, count)
    first = jnp.dot(cosine.T * waves[None, :], sine, precision=highest)
    second = jnp.dot(sine.T * waves[None, :], cosine, precision=highest)
    return (first - second) / float(count)


def body(density):
    count_gx = lax.axis_size("gx")
    count_gy = lax.axis_size("gy")
    rows_x, rows_y, count_z = density.shape
    count_x = rows_x * count_gx
    count_y = rows_y * count_gy
    deriv_x = deriv_matrix(count_x)
    deriv_y = deriv_matrix(count_y)
    deriv_z = deriv_matrix(count_z)

    def line_x(piece):
        flat = piece.reshape(piece.shape[0], piece.shape[1] * piece.shape[2])
        result = jnp.dot(deriv_x, flat, precision=highest)
        return result.reshape(piece.shape)

    def line_y(piece):
        turned = jnp.swapaxes(piece, 0, 1)
        flat = turned.reshape(turned.shape[0], turned.shape[1] * turned.shape[2])
        result = jnp.dot(deriv_y, flat, precision=highest).reshape(turned.shape)
        return jnp.swapaxes(result, 0, 1)

    def along_x(field):
        lines = line_x(lax.all_to_all(field, "gx", split_axis=2, concat_axis=0, tiled=True))
        return lax.all_to_all(lines, "gx", split_axis=0, concat_axis=2, tiled=True)

    def along_y(field):
        lines = line_y(lax.all_to_all(field, "gy", split_axis=2, concat_axis=1, tiled=True))
        return lax.all_to_all(lines, "gy", split_axis=1, concat_axis=2, tiled=True)

    def along_z(field):
        flat = field.reshape(field.shape[0] * field.shape[1], field.shape[2])
        result = jnp.dot(flat, deriv_z.T, precision=highest)
        return result.reshape(field.shape)

    gradients = [along_x(density), along_y(density), along_z(density)]
    grad_sq = (
        gradients[0] * gradients[0] + gradients[1] * gradients[1] + gradients[2] * gradients[2]
    )
    energy_local, partials = jax.value_and_grad(summed_energy, argnums=(0, 1))(density, grad_sq)
    d_dens, d_grad = partials
    fluxes = [2.0 * d_grad * gradient for gradient in gradients]
    divergence = along_x(fluxes[0]) + along_y(fluxes[1]) + along_z(fluxes[2])
    potential = d_dens - divergence
    return (potential, total_energy(energy_local, count_x * count_y * count_z))


def solution(mesh):
    in_specs = (P("gx", "gy", None),)
    out_specs = (P("gx", "gy", None), P())
    return jax.shard_map(body, mesh=mesh, in_specs=in_specs, out_specs=out_specs, check_vma=False)
```

profile of v0, /device:TPU:0, one launch (start us, length us, event | category | flops | bytes accessed | tf_op | source)
XLA Modules:
  0.0 536.8 jit_solution(16059502869179916569)
XLA Ops:
  0.6 5.5 %copy.31 = f32[32,64,256]{1,0,2:T(8,128)} copy(f32[32,64,256]{2,1,0:T(8,128)} %param.1) | data formatting | bytes 4194304 | tf_op args[0]
  6.2 5.5 %reshape.56 = f32[4,1,131072]{2,1,0:T(1,128)} reshape(f32[256,32,64]{2,1,0:T(8,128)} %bitcast.101) | data formatting | bytes 4194304
  11.6 5.2 all-to-all-start.2
  16.8 7.2 %reshape.60 = f32[8,1,65536]{2,1,0:T(1,128)} reshape(f32[256,32,64]{2,1,0:T(8,128)} %bitcast.102) | data formatting | bytes 4194304
  24.1 17.6 %all-to-all-done.2 = f32[4,1,131072]{2,1,0:T(1,128)S(1)} async-done(((f32[4,1,131072]{2,1,0:T(1,128)}), f32[4,1,131072]{2,1,0:T(1,128)S(1)}, u32[]{:S(2)}, u32[]{:S(2)}) %all-to-all-start.2) | async-done | bytes 2097184 | tf_op jit(solution)/shard_map/all_to_all | solution.py:107
  50.3 7.7 %reduce = f32[4,131072]{1,0:T(4,128)S(1)} reduce(f32[4,1,131072]{2,1,0:T(1,128)} %copy-done.2, f32[]{:T(128)} %broadcast.365), dimensions={1}, to_apply=%all_to_all.107.reduce_sub_computation | reduce | bytes 4194308 | tf_op jit(solution)/shard_map/all_to_all | solution.py:107
  61.9 7.1 %copy.71 = f32[32,64,4,64]{1,2,3,0:T(4,128)} copy(f32[32,64,4,64]{1,0,3,2:T(8,128)} %bitcast.112) | data formatting | bytes 4194304 | tf_op jit(solution)/shard_map/all_to_all | solution.py:107
  76.3 5.5 %copy.42 = f32[32,256,64]{2,0,1:T(8,128)} copy(f32[32,256,64]{1,2,0:T(8,128)} %fusion.18) | data formatting | bytes 4194304 | tf_op jit(solution)/shard_map/transpose | solution.py:100
  81.9 5.5 %reshape.58 = f32[4,1,131072]{2,1,0:T(1,128)} reshape(f32[256,32,64]{2,1,0:T(8,128)} %bitcast.106) | data formatting | bytes 4194304
  87.4 8.5 %all-to-all-done = f32[8,1,65536]{2,1,0:T(1,128)} async-done(((f32[8,1,65536]{2,1,0:T(1,128)}), f32[8,1,65536]{2,1,0:T(1,128)}, u32[]{:S(2)}, u32[]{:S(2)}) %all-to-all-start) | async-done | bytes 2097184 | tf_op jit(solution)/shard_map/all_to_all | solution.py:103
  100.6 7.2 %reduce.2 = f32[8,65536]{1,0:T(8,128)S(1)} reduce(f32[8,1,65536]{2,1,0:T(1,128)} %all-to-all-done, f32[]{:T(128)} %broadcast.365), dimensions={1}, to_apply=%all_to_all.100.reduce_sub_computation | reduce | bytes 4194308 | tf_op jit(solution)/shard_map/all_to_all | solution.py:103
  111.4 7.0 %copy.33 = f32[8,32,64,32]{3,2,1,0:T(8,128)} copy(f32[8,32,64,32]{2,1,3,0:T(8,128)} %bitcast.104) | data formatting | bytes 4194304 | tf_op jit(solution)/shard_map/all_to_all | solution.py:103
  118.4 6.4 %reshape.49 = f32[256,2048]{1,0:T(8,128)S(1)} reshape(f32[8,32,64,32]{3,2,1,0:T(8,128)} %copy.33) | data formatting | bytes 4194304 | tf_op jit(solution)/shard_map/reshape | solution.py:92
  135.9 7.2 %reshape.62 = f32[8,1,65536]{2,1,0:T(1,128)} reshape(f32[256,32,64]{2,1,0:T(8,128)} %bitcast.107) | data formatting | bytes 4194304
  154.0 9.0 %reduce.1 = f32[4,131072]{1,0:T(4,128)} reduce(f32[4,1,131072]{2,1,0:T(1,128)} %all-to-all-done.3, f32[]{:T(128)} %broadcast.365), dimensions={1}, to_apply=%all_to_all.111.reduce_sub_computation | reduce | bytes 4194308 | tf_op jit(solution)/shard_map/all_to_all | solution.py:108
  163.0 5.5 %reshape.59 = f32[256,32,64]{2,1,0:T(8,128)} reshape(f32[4,131072]{1,0:T(4,128)} %reduce.1) | data formatting | bytes 4194304
  168.5 6.9 %copy.70 = f32[32,4,64,64]{3,1,2,0:T(4,128)} copy(f32[32,4,64,64]{3,0,2,1:T(8,128)} %bitcast.114) | data formatting | bytes 4194304 | tf_op jit(solution)/shard_map/all_to_all | solution.py:108
  175.3 5.5 %all_to_all.114 = f32[32,64,256]{2,1,0:T(8,128)} reshape(f32[32,64,4,64]{3,2,1,0:T(4,128)} %bitcast.115) | data formatting | bytes 4194304 | tf_op jit(solution)/shard_map/all_to_all | solution.py:108
  180.8 15.9 %all-to-all-done.1 = f32[8,1,65536]{2,1,0:T(1,128)} async-done(((f32[8,1,65536]{2,1,0:T(1,128)}), f32[8,1,65536]{2,1,0:T(1,128)}, u32[]{:S(2)}, u32[]{:S(2)}) %all-to-all-start.1) | async-done | bytes 2097184 | tf_op jit(solution)/shard_map/all_to_all | solution.py:104
  196.7 8.5 %reduce.3 = f32[8,65536]{1,0:T(8,128)} reduce(f32[8,1,65536]{2,1,0:T(1,128)} %all-to-all-done.1, f32[]{:T(128)} %broadcast.365), dimensions={1}, to_apply=%all_to_all.103.reduce_sub_computation | reduce | bytes 4194308 | tf_op jit(solution)/shard_map/all_to_all | solution.py:104
  218.9 11.6 %multiply_reduce_fusion = (f32[]{:T(128)}, f32[32,64,256]{2,1,0:T(8,128)S(1)}) fusion(f32[32,64,256]{2,1,0:T(8,128)S(1)} %copy-done, f32[32,64,256]{2,1,0:T(8,128)} %bitcast.128, f32[32,64,256]{2,1,0:T(8,128)} %all_to_all.114, f32[32,64,256]{2,1,0:T(8,128)} %copy.38), kind=kLoop, calls=%fused_computation.15 | loop fusion | flops 28311552 | bytes 10485764 | tf_op jit(solution)/shard_map/jvp()/reduce_sum | solution.py:51
  230.5 12.0 %fusion.60 = (f32[32,64,256]{2,1,0:T(8,128)}, f32[32,64,256]{2,1,0:T(8,128)}, f32[32,64,256]{2,1,0:T(8,128)}) fusion(f32[32,64,256]{2,1,0:T(8,128)S(1)} %copy-done.1, f32[32,64,256]{2,1,0:T(8,128)S(1)} %get-tuple-element.3, f32[32,64,256]{2,1,0:T(8,128)S(1)} %copy-done), kind=kLoop, calls=%fused_computation.85 | loop fusion | flops 37748736 | bytes 12582912 | tf_op jit(solution)/shard_map/mul | solution.py:121
  242.5 5.5 %copy.53 = f32[32,64,256]{1,0,2:T(8,128)} copy(f32[32,64,256]{2,1,0:T(8,128)} %get-tuple-element.4) | data formatting | bytes 4194304 | tf_op jit(solution)/shard_map/mul | solution.py:121
  248.0 5.5 %reshape.68 = f32[4,1,131072]{2,1,0:T(1,128)} reshape(f32[256,32,64]{2,1,0:T(8,128)} %bitcast.108) | data formatting | bytes 4194304
  262.0 5.5 %copy.46 = f32[32,64,256]{1,0,2:T(8,128)} copy(f32[32,64,256]{2,1,0:T(8,128)} %mul.496) | data formatting | bytes 4194304 | tf_op jit(solution)/shard_map/mul | solution.py:121
  267.5 7.2 %reshape.64 = f32[8,1,65536]{2,1,0:T(1,128)} reshape(f32[256,32,64]{2,1,0:T(8,128)} %bitcast.109) | data formatting | bytes 4194304
  274.7 8.5 %all-to-all-done.6 = f32[4,1,131072]{2,1,0:T(1,128)} async-done(((f32[4,1,131072]{2,1,0:T(1,128)}), f32[4,1,131072]{2,1,0:T(1,128)}, u32[]{:S(2)}, u32[]{:S(2)}) %all-to-all-start.6) | async-done | bytes 2097184 | tf_op jit(solution)/shard_map/all_to_all | solution.py:107
  287.7 9.0 %reduce.6 = f32[4,131072]{1,0:T(4,128)} reduce(f32[4,1,131072]{2,1,0:T(1,128)} %all-to-all-done.6, f32[]{:T(128)} %broadcast.365), dimensions={1}, to_apply=%all_to_all.122.reduce_sub_computation | reduce | bytes 4194308 | tf_op jit(solution)/shard_map/all_to_all | solution.py:107
  296.8 5.5 %reshape.69 = f32[256,32,64]{2,1,0:T(8,128)} reshape(f32[4,131072]{1,0:T(4,128)} %reduce.6) | data formatting | bytes 4194304
  302.2 6.9 %copy.69 = f32[32,64,4,64]{1,2,3,0:T(4,128)} copy(f32[32,64,4,64]{1,0,3,2:T(8,128)} %bitcast.118) | data formatting | bytes 4194304 | tf_op jit(solution)/shard_map/all_to_all | solution.py:107
  309.1 5.7 %all_to_all.125 = f32[32,256,64]{1,2,0:T(8,128)} reshape(f32[32,4,64,64]{2,1,3,0:T(4,128)} %bitcast.119) | data formatting | bytes 4194304 | tf_op jit(solution)/shard_map/all_to_all | solution.py:107
  319.5 5.5 %copy.55 = f32[32,256,64]{2,0,1:T(8,128)} copy(f32[32,256,64]{1,2,0:T(8,128)} %fusion.21) | data formatting | bytes 4194304 | tf_op jit(solution)/shard_map/transpose | solution.py:100
  325.0 5.5 %reshape.70 = f32[4,1,131072]{2,1,0:T(1,128)} reshape(f32[256,32,64]{2,1,0:T(8,128)} %bitcast.110) | data formatting | bytes 4194304
  330.5 6.2 %all-to-all-done.4 = f32[8,1,65536]{2,1,0:T(1,128)} async-done(((f32[8,1,65536]{2,1,0:T(1,128)}), f32[8,1,65536]{2,1,0:T(1,128)}, u32[]{:S(2)}, u32[]{:S(2)}) %all-to-all-start.4) | async-done | bytes 2097184 | tf_op jit(solution)/shard_map/all_to_all | solution.py:103
  341.2 8.5 %reduce.4 = f32[8,65536]{1,0:T(8,128)} reduce(f32[8,1,65536]{2,1,0:T(1,128)} %all-to-all-done.4, f32[]{:T(128)} %broadcast.365), dimensions={1}, to_apply=%all_to_all.115.reduce_sub_computation | reduce | bytes 4194308 | tf_op jit(solution)/shard_map/all_to_all | solution.py:103
  349.7 5.2 reshape.65
  355.0 7.0 %copy.48 = f32[8,32,64,32]{3,2,1,0:T(8,128)} copy(f32[8,32,64,32]{2,1,3,0:T(8,128)} %bitcast.105) | data formatting | bytes 4194304 | tf_op jit(solution)/shard_map/all_to_all | solution.py:103
  361.9 7.5 %reshape.53 = f32[256,2048]{1,0:T(8,128)} reshape(f32[8,32,64,32]{3,2,1,0:T(8,128)} %copy.48) | data formatting | bytes 4194304 | tf_op jit(solution)/shard_map/reshape | solution.py:92
  372.5 5.6 %fusion.5 = f32[256,64,32]{0,1,2:T(8,128)} fusion(f32[64,32,256]{2,1,0:T(8,128)} %bitcast.127, f32[256,256]{1,0:T(8,128)S(1)} %fusion.26), kind=kOutput, calls=%fused_computation.11 | convolution fusion | flops 1610612736 | bytes 4456448 | tf_op jit(solution)/shard_map/dot_general | solution.py:93
  378.1 5.5 %copy.51 = f32[256,64,32]{1,2,0:T(8,128)} copy(f32[256,64,32]{0,1,2:T(8,128)} %fusion.5) | data formatting | bytes 4194304 | tf_op jit(solution)/shard_map/dot_general | solution.py:93
  383.6 7.2 %reshape.66 = f32[8,1,65536]{2,1,0:T(1,128)} reshape(f32[256,32,64]{2,1,0:T(8,128)} %bitcast.111) | data formatting | bytes 4194304
  395.2 69.7 %psum.7 = f32[]{:T(128)} all-reduce(f32[]{:T(128)} %get-tuple-element.2), channel_id=1, replica_groups=mesh['gx'=8,'gy'=4] {'gx','gy'}, use_global_device_ids=true, to_apply=%region_1.2 | all-reduce | flops 1 | bytes 8 | tf_op jit(solution)/shard_map/psum | solution.py:55
  465.6 9.0 %reduce.7 = f32[4,131072]{1,0:T(4,128)} reduce(f32[4,1,131072]{2,1,0:T(1,128)} %all-to-all-done.7, f32[]{:T(128)} %broadcast.365), dimensions={1}, to_apply=%all_to_all.126.reduce_sub_computation | reduce | bytes 4194308 | tf_op jit(solution)/shard_map/all_to_all | solution.py:108
  474.6 5.5 %reshape.71 = f32[256,32,64]{2,1,0:T(8,128)} reshape(f32[4,131072]{1,0:T(4,128)} %reduce.7) | data formatting | bytes 4194304
  480.1 6.9 %copy.68 = f32[32,4,64,64]{3,1,2,0:T(4,128)} copy(f32[32,4,64,64]{3,0,2,1:T(8,128)} %bitcast.120) | data formatting | bytes 4194304 | tf_op jit(solution)/shard_map/all_to_all | solution.py:108
  486.9 5.5 %all_to_all.129 = f32[32,64,256]{2,1,0:T(8,128)} reshape(f32[32,64,4,64]{3,2,1,0:T(4,128)} %bitcast.121) | data formatting | bytes 4194304 | tf_op jit(solution)/shard_map/all_to_all | solution.py:108
  492.4 8.5 %reduce.5 = f32[8,65536]{1,0:T(8,128)} reduce(f32[8,1,65536]{2,1,0:T(1,128)} %all-to-all-done.5, f32[]{:T(128)} %broadcast.365), dimensions={1}, to_apply=%all_to_all.118.reduce_sub_computation | reduce | bytes 4194308 | tf_op jit(solution)/shard_map/all_to_all | solution.py:104
  514.6 20.8 %add_subtract_fusion = f32[32,64,256]{2,1,0:T(8,128)} fusion(f32[32,64,256]{2,1,0:T(8,128)} %copy.57, f32[32,64,256]{2,1,0:T(8,128)} %all_to_all.129, f32[32,64,256]{2,1,0:T(8,128)S(1)} %copy-done, f32[32,64,256]{2,1,0:T(8,128)} %copy-done.3, f32[32,64,256]{2,1,0:T(8,128)} %get-tuple-element.6, f32[32,64,256]{2,1,0:T(8,128)} %get-tuple-element.5, ...), kind=kOutput, calls=%fused_computation.16 | convolution fusion | flops 1688731648 | bytes 17039360 | tf_op jit(solution)/shard_map/dot_general | solution.py:112
  (40 shorter events, 107.2 us)
Async XLA Ops:
  11.6 30.1 %all-to-all-start.2 = ((f32[4,1,131072]{2,1,0:T(1,128)}), f32[4,1,131072]{2,1,0:T(1,128)S(1)}, u32[]{:S(2)}, u32[]{:S(2)}) async-start(f32[4,1,131072]{2,1,0:T(1,128)} %reshape.56), calls=%async_computation.2 | async-start | bytes 4194304 | tf_op jit(solution)/shard_map/all_to_all | solution.py:107
  41.7 5.2 copy-start.2
  41.7 54.2 %all-to-all-start = ((f32[8,1,65536]{2,1,0:T(1,128)}), f32[8,1,65536]{2,1,0:T(1,128)}, u32[]{:S(2)}, u32[]{:S(2)}) async-start(f32[8,1,65536]{2,1,0:T(1,128)} %reshape.60), calls=%async_computation | async-start | bytes 4194304 | tf_op jit(solution)/shard_map/all_to_all | solution.py:103
  95.9 47.3 %all-to-all-start.3 = ((f32[4,1,131072]{2,1,0:T(1,128)}), f32[4,1,131072]{2,1,0:T(1,128)}, u32[]{:S(2)}, u32[]{:S(2)}) async-start(f32[4,1,131072]{2,1,0:T(1,128)} %reshape.58), calls=%async_computation.3 | async-start | bytes 4194304 | tf_op jit(solution)/shard_map/all_to_all | solution.py:108
  143.2 4.5 copy-start
  143.2 53.5 %all-to-all-start.1 = ((f32[8,1,65536]{2,1,0:T(1,128)}), f32[8,1,65536]{2,1,0:T(1,128)}, u32[]{:S(2)}, u32[]{:S(2)}) async-start(f32[8,1,65536]{2,1,0:T(1,128)} %reshape.62), calls=%async_computation.1 | async-start | bytes 4194304 | tf_op jit(solution)/shard_map/all_to_all | solution.py:104
  218.9 11.6 %copy-start.1 = (f32[32,64,256]{2,1,0:T(8,128)S(1)}, f32[32,64,256]{2,1,0:T(8,128)}, u32[]{:S(2)}) copy-start(f32[32,64,256]{2,1,0:T(8,128)} %all_to_all.114) | copy-start | bytes 6291460
  230.5 12.0 %copy-start.3 = (f32[32,64,256]{2,1,0:T(8,128)}, f32[32,64,256]{2,1,0:T(8,128)S(1)}, u32[]{:S(2)}) copy-start(f32[32,64,256]{2,1,0:T(8,128)S(1)} %get-tuple-element.3) | copy-start | bytes 6291460
  253.6 29.6 %all-to-all-start.6 = ((f32[4,1,131072]{2,1,0:T(1,128)}), f32[4,1,131072]{2,1,0:T(1,128)}, u32[]{:S(2)}, u32[]{:S(2)}) async-start(f32[4,1,131072]{2,1,0:T(1,128)} %reshape.68), calls=%async_computation.6 | async-start | bytes 4194304 | tf_op jit(solution)/shard_map/all_to_all | solution.py:107
  283.2 53.6 %all-to-all-start.4 = ((f32[8,1,65536]{2,1,0:T(1,128)}), f32[8,1,65536]{2,1,0:T(1,128)}, u32[]{:S(2)}, u32[]{:S(2)}) async-start(f32[8,1,65536]{2,1,0:T(1,128)} %reshape.64), calls=%async_computation.4 | async-start | bytes 4194304 | tf_op jit(solution)/shard_map/all_to_all | solution.py:103
  336.8 54.1 %all-to-all-start.7 = ((f32[4,1,131072]{2,1,0:T(1,128)}), f32[4,1,131072]{2,1,0:T(1,128)}, u32[]{:S(2)}, u32[]{:S(2)}) async-start(f32[4,1,131072]{2,1,0:T(1,128)} %reshape.70), calls=%async_computation.7 | async-start | bytes 4194304 | tf_op jit(solution)/shard_map/all_to_all | solution.py:108
  390.8 101.5 %all-to-all-start.5 = ((f32[8,1,65536]{2,1,0:T(1,128)}), f32[8,1,65536]{2,1,0:T(1,128)}, u32[]{:S(2)}, u32[]{:S(2)}) async-start(f32[8,1,65536]{2,1,0:T(1,128)} %reshape.66), calls=%async_computation.5 | async-start | bytes 4194304 | tf_op jit(solution)/shard_map/all_to_all | solution.py:104
where the time goes:
time: 543 us; the launch traced here: 537 us
  local copies, waits for them, and re-layouts  230 us (42%)
  other arithmetic  95 us (17%)
  blocking collectives  69.7 us (13%)
  waiting for transfers between devices  56.8 us (10%)
  matrix products  44.7 us (8%)
  starting transfers between devices  37.4 us (7%)
    unnamed x25, local copies, waits for them, and re-layouts  96 us
    psum x1, blocking collectives, total_energy(): return lax.psum(energy_local, ('gx', 'gy')) / float(cells)  69.7 us
    all_to_all x2, waiting for transfers between devices, along_y(): lax.all_to_all(field, 'gy', split_axis=2, concat_axis=1, tiled=True)  26.2 us
    all_to_all x4, local copies, waits for them, and re-layouts, along_y(): return lax.all_to_all(lines, 'gy', split_axis=1, concat_axis=2, tiled=True)  24.6 us
    all_to_all x5, local copies, waits for them, and re-layouts, along_y(): lax.all_to_all(field, 'gy', split_axis=2, concat_axis=1, tiled=True)  24.3 us
    dot_general x2, matrix products, along_z(): result = jnp.dot(flat, deriv_z.T, precision=highest)  24 us
    all_to_all x2, other arithmetic, along_y(): return lax.all_to_all(lines, 'gy', split_axis=1, concat_axis=2, tiled=True)  18 us
    all_to_all x4, local copies, waits for them, and re-layouts, along_x(): return lax.all_to_all(lines, 'gx', split_axis=0, concat_axis=2, tiled=True)  17.2 us
  transfers between devices with their start and end apart: 8, of which 5 were waited for; matrix products, arithmetic and copies ran while one was open for 44% of the time, Pallas kernels for 0%

commit v1 on v0

--- a/solution.py
+++ b/solution.py
@@ -2,11 +2,14 @@
 
 import jax
 import jax.numpy as jnp
+import numpy as np
 from jax import lax
+from jax.experimental import pallas as pl
+from jax.experimental.pallas import tpu as pltpu
 from jax.sharding import PartitionSpec as P
 
+
 spacing = 1.0
-highest = lax.Precision.HIGHEST
 pbe_kappa = 0.804
 pbe_mu = 0.2195149727645171
 pbe_beta = 0.06672455060314922
@@ -17,6 +20,413 @@
 pw_second = 3.5876
 pw_third = 1.6382
 pw_fourth = 0.49294
+
+LANES = 128
+ROWS = 8
+
+
+def deriv_matrix(count):
+    index = np.arange(count)
+    signed = np.where(index < count // 2, index, index - count)
+    signed = np.where(index == count // 2, 0, signed)
+    waves = signed * (2.0 * math.pi / (count * spacing))
+    return np.fft.ifft(1j * waves[:, None] * np.fft.fft(np.eye(count), axis=0), axis=0).real
+
+
+def split_matrix(count):
+    matrix = deriv_matrix(count)
+    high = matrix.astype(jnp.bfloat16)
+    low = (matrix - high.astype(np.float64)).astype(jnp.bfloat16)
+    return jnp.asarray(high), jnp.asarray(low)
+
+
+def halves(field):
+    high = field.astype(jnp.bfloat16)
+    return high, (field - high.astype(jnp.float32)).astype(jnp.bfloat16)
+
+
+def dot(left, right):
+    return jnp.dot(left, right, preferred_element_type=jnp.float32)
+
+
+def matrix_times(high, low, field):
+    f_high, f_low = halves(field)
+    return dot(high, f_high) + (dot(high, f_low) + dot(low, f_high))
+
+
+def times_matrix(field, high, low):
+    f_high, f_low = halves(field)
+    return dot(f_high, high) + (dot(f_low, high) + dot(f_high, low))
+
+
+def xc_partials(n, g):
+    c_fermi = (3.0 * math.pi**2) ** (1.0 / 3.0)
+    c_wigner = (3.0 / (4.0 * math.pi)) ** (1.0 / 3.0)
+    c_ratio = pbe_beta / pbe_gamma
+    v = jnp.exp(jnp.log(n) * (-1.0 / 6.0))
+    v2 = v * v
+    v4 = v2 * v2
+    n13 = n * v4
+    v8 = v4 * v4
+    v14 = v8 * v4 * v2
+    ex = n13 * (-0.75 * c_fermi / math.pi)
+    s_scale = (v14 * v2) * (1.0 / (4.0 * c_fermi**2))
+    s2 = g * s_scale
+    r_x = 1.0 / (pbe_kappa + pbe_mu * s2)
+    fx = (1.0 + pbe_kappa) - pbe_kappa**2 * r_x
+    dfx = (pbe_mu * pbe_kappa**2) * (r_x * r_x)
+    rs = c_wigner * v2
+    root = math.sqrt(c_wigner) * v
+    q_series = (2.0 * pw_coef) * (
+        root * (pw_first + pw_third * rs) + rs * (pw_second + pw_fourth * rs)
+    )
+    q_slope = (2.0 * pw_coef) * (
+        root * (0.5 * pw_first + 1.5 * pw_third * rs) + rs * (pw_second + (2.0 * pw_fourth) * rs)
+    )
+    r_q = 1.0 / (q_series * (q_series + 1.0))
+    log_q = jnp.log(1.0 + (q_series + 1.0) * r_q)
+    lead = (2.0 * pw_coef) * (1.0 + pw_alpha * rs)
+    ec = -lead * log_q
+    nd = (-1.0 / 3.0) * (lead * q_slope * r_q - (2.0 * pw_coef * pw_alpha) * rs * log_q)
+    t_scale = v14 * (math.pi / (16.0 * c_fermi))
+    t2 = g * t_scale
+    grown = jnp.exp(ec * (-1.0 / pbe_gamma))
+    r_e = 1.0 / (grown - 1.0)
+    factor = c_ratio * r_e
+    q = factor * t2
+    den = 1.0 + q + q * q
+    full = den + c_ratio * t2 * (1.0 + q)
+    r_d = 1.0 / (den * full)
+    h = pbe_gamma * jnp.log(full * full * r_d)
+    h_t = pbe_beta * (1.0 + 2.0 * q) * r_d
+    h_p = (-pbe_beta) * (t2 * t2) * (q * (2.0 + q)) * r_d
+    energy = n * (ex * fx + ec + h)
+    d_grad = n * (ex * dfx * s_scale + h_t * t_scale)
+    d_dens = (
+        ex * ((4.0 / 3.0) * fx - (8.0 / 3.0) * (s2 * dfx))
+        + ec
+        + h
+        + nd * (1.0 + h_p * factor * grown * r_e * (1.0 / pbe_gamma))
+        - (7.0 / 3.0) * t2 * h_t
+    )
+    return energy, d_dens, d_grad
+
+
+def slot(axis, step, size, width):
+    return pl.multiple_of(lax.rem(lax.axis_index(axis) + step, size) * width, width)
+
+
+def whole(shape):
+    return pl.BlockSpec(shape, lambda s: (0,) * len(shape))
+
+
+def call(kernel, ins, outs, in_specs=None, scratch=(), flops=1 << 28):
+    specs = [whole(a.shape) for a in ins]
+    for position, spec in (in_specs or {}).items():
+        specs[position] = spec
+    return pl.pallas_call(
+        kernel,
+        grid=(1,),
+        in_specs=specs,
+        out_specs=[whole(o) for o in outs],
+        out_shape=[jax.ShapeDtypeStruct(o, jnp.float32) for o in outs],
+        scratch_shapes=list(scratch),
+        cost_estimate=pl.CostEstimate(
+            flops=flops,
+            bytes_accessed=sum(4 * math.prod(o) for o in outs) + sum(4 * a.size for a in ins),
+            transcendentals=0,
+        ),
+    )(*ins)
+
+
+class Plan:
+    def __init__(self, shape):
+        self.gx, self.gy = lax.axis_size("gx"), lax.axis_size("gy")
+        self.rx, self.ry, self.z = shape
+        self.yc = self.ry // self.gx
+        self.sx = self.rx // self.gy
+
+    @staticmethod
+    def fits(shape, gx, gy):
+        rx, ry, z = shape
+        return ry % (ROWS * gx) == 0 and ry // gx == ROWS and rx % gy == 0 and (rx // gy) % 2 == 0 and z % (2 * LANES) == 0 and rx % ROWS == 0
+
+
+def pack_x(plan, density, chunk, lanes):
+    def kernel(n_ref, *outs):
+        for t, out in enumerate(outs):
+            rows = pl.ds(slot("gx", t, plan.gx, plan.yc), plan.yc)
+            out[...] = n_ref[:, rows, :].reshape(plan.rx * plan.yc, lanes)
+
+    spec = pl.BlockSpec((plan.rx, plan.ry, lanes), lambda s: (0, 0, chunk))
+    return call(kernel, [density], [(plan.rx * plan.yc, lanes)] * plan.gx, {0: spec}, flops=1 << 20)
+
+
+def pack_y(plan, density):
+    def kernel(n_ref, *outs):
+        for t, out in enumerate(outs):
+            out[...] = n_ref[pl.ds(slot("gy", t, plan.gy, plan.sx), plan.sx)]
+
+    return call(kernel, [density], [(plan.sx, plan.ry, plan.z)] * plan.gy, flops=1 << 20)
+
+
+def rotate(pieces, axis, size):
+    arrived = [pieces[0]] + [None] * (size - 1)
+    for t in sorted(range(1, size), key=lambda t: abs(2 * t - size)):
+        pairs = [(i, (i + t) % size) for i in range(size)]
+        arrived[size - t] = lax.ppermute(pieces[t], axis, pairs)
+    return arrived
+
+
+def after(arrays, token):
+    return lax.optimization_barrier((list(arrays), token))[0]
+
+
+def deriv_x(plan, matrix, pieces, lanes, with_energy):
+    gx, rx, yc = plan.gx, plan.rx, plan.yc
+
+    def kernel(high_ref, low_ref, *refs):
+        ins, outs = refs[:gx], refs[gx : 2 * gx]
+        high, low = high_ref[...], low_ref[...]
+        for y in range(0, yc, 2):
+            columns = [
+                jnp.concatenate([p[pl.ds(y + k, rx, stride=yc), :] for p in ins], axis=0)
+                for k in range(2)
+            ]
+            result = matrix_times(high, low, jnp.concatenate(columns, axis=1))
+            for k in range(2):
+                for t, out in enumerate(outs):
+                    out[pl.ds(y + k, rx, stride=yc), :] = result[
+                        t * rx : (t + 1) * rx, k * lanes : (k + 1) * lanes
+                    ]
+        if with_energy:
+            energy_ref, ordered = refs[2 * gx :]
+            for t, p in enumerate(ins):
+                ordered[pl.ds(slot("gx", t, gx, ROWS), ROWS), :] = p[rx * yc :, :]
+            total = ordered[:ROWS, :]
+            for t in range(1, gx):
+                total = total + ordered[t * ROWS : (t + 1) * ROWS, :]
+            energy_ref[...] = total
+
+    outs = [(rx * yc, lanes)] * gx
+    scratch = []
+    if with_energy:
+        outs = outs + [(ROWS, lanes)]
+        scratch = [pltpu.VMEM((gx * ROWS, lanes), jnp.float32)]
+    return call(kernel, [*matrix, *pieces], outs, scratch=scratch)
+
+
+def deriv_y(plan, matrix, pieces, lanes, energy=None):
+    gy, sx, ry = plan.gy, plan.sx, plan.ry
+    together = max(1, 2 * LANES // lanes)
+    extra = 0 if energy is None else 1
+
+    def kernel(high_ref, low_ref, *refs):
+        ins, outs = refs[extra : extra + gy], refs[extra + gy :]
+        high, low = high_ref[...], low_ref[...]
+        for x in range(0, sx, together):
+            columns = [
+                jnp.concatenate([p[x + k] for p in ins], axis=0) for k in range(together)
+            ]
+            field = columns[0] if together == 1 else jnp.concatenate(columns, axis=1)
+            result = matrix_times(high, low, field)
+            for k in range(together):
+                for t, out in enumerate(outs):
+                    out[x + k] = result[t * ry : (t + 1) * ry, k * lanes : (k + 1) * lanes]
+        if extra:
+            for out in outs:
+                out[sx] = jnp.zeros((ry, lanes), jnp.float32)
+                out[sx, :ROWS, :] = refs[0][...]
+
+    ins = [*matrix] + ([energy] if extra else []) + list(pieces)
+    return call(kernel, ins, [(sx + extra, ry, lanes)] * gy)
+
+
+def rows_call(kernel, rows, ins, widths, out_width, resident):
+    block = rows // 4
+    return pl.pallas_call(
+        kernel,
+        grid=(4,),
+        in_specs=[pl.BlockSpec(m.shape, lambda s: (0, 0)) for m in resident]
+        + [pl.BlockSpec((block, w), lambda s: (s, 0)) for w in widths],
+        out_specs=pl.BlockSpec((block, out_width), lambda s: (s, 0)),
+        out_shape=jax.ShapeDtypeStruct((rows, out_width), jnp.float32),
+        cost_estimate=pl.CostEstimate(flops=1 << 28, bytes_accessed=1 << 22, transcendentals=0),
+    )(*resident, *ins)
+
+
+def deriv_z(plan, matrix, field):
+    def kernel(high_ref, low_ref, f_ref, out_ref):
+        out_ref[...] = -times_matrix(f_ref[...], high_ref[...], low_ref[...])
+
+    rows = plan.rx * plan.ry
+    flat = field.reshape(rows, plan.z)
+    return rows_call(kernel, rows, [flat], [plan.z], plan.z, matrix).reshape(field.shape)
+
+
+def less_deriv_z(plan, matrix, d_dens, flux):
+    def kernel(high_ref, low_ref, *refs):
+        count = len(flux)
+        dens = jnp.concatenate([r[...] for r in refs[:count]], axis=1)
+        field = jnp.concatenate([r[...] for r in refs[count : 2 * count]], axis=1)
+        refs[-1][...] = dens + times_matrix(field, high_ref[...], low_ref[...])
+
+    rows = plan.rx * plan.ry
+    flat = [a.reshape(rows, a.shape[2]) for a in (*d_dens, *flux)]
+    widths = [a.shape[1] for a in flat]
+    out = rows_call(kernel, rows, flat, widths, plan.z, matrix)
+    return out.reshape(plan.rx, plan.ry, plan.z)
+
+
+def pointwise(plan, density, grad_z, grad_y, grad_x, chunk, lanes, before):
+    gx, gy, rx, ry, yc, sx = plan.gx, plan.gy, plan.rx, plan.ry, plan.yc, plan.sx
+    extra = 0 if before is None else 1
+
+    def kernel(*refs):
+        n_ref, gz_ref = refs[0], refs[1]
+        gy_refs = refs[2 : 2 + gy]
+        gx_refs = refs[2 + gy : 2 + gy + gx]
+        refs = refs[2 + gy + gx :]
+        if extra:
+            before_ref, refs = refs[0], refs[1:]
+        fx_refs, fy_refs = refs[:gx], refs[gx : gx + gy]
+        fz_ref, dd_ref, energy_ref = refs[gx + gy :]
+        total = jnp.zeros((yc, lanes), jnp.float32)
+        for part in range(gy):
+            base = slot("gy", part, gy, sx)
+
+            def step(inner, total, part=part, base=base):
+                x = base + inner
+                for t in range(gx):
+                    rows = pl.ds(slot("gx", t, gx, yc), yc)
+                    n = n_ref[x, rows, :]
+                    d_x = gx_refs[t][x]
+                    d_y = gy_refs[part][inner, rows, :]
+                    d_z = gz_ref[x, rows, :]
+                    f, d_dens, d_grad = xc_partials(n, d_x * d_x + d_y * d_y + d_z * d_z)
+                    twice = 2.0 * d_grad
+                    fx_refs[t][x] = twice * d_x
+                    fy_refs[part][inner, rows, :] = twice * d_y
+                    fz_ref[x, rows, :] = twice * d_z
+                    dd_ref[x, rows, :] = d_dens
+                    total = total + f
+                return total
+
+            total = lax.fori_loop(0, sx, step, total)
+        if extra:
+            total = total + before_ref[...]
+            for out in fx_refs:
+                out[rx] = total
+        energy_ref[...] = total
+
+    block = pl.BlockSpec((rx, ry, lanes), lambda s: (0, 0, chunk))
+    y_block = pl.BlockSpec((sx, ry, lanes), lambda s: (0, 0, chunk))
+    specs = {0: block, 1: block} | {2 + t: y_block for t in range(gy)}
+    ins = [density, grad_z, *grad_y, *[p.reshape(rx, yc, lanes) for p in grad_x]]
+    if extra:
+        ins.append(before)
+    outs = [(rx + extra, yc, lanes)] * gx + [(sx, ry, lanes)] * gy
+    outs += [(rx, ry, lanes)] * 2 + [(yc, lanes)]
+    out = call(kernel, ins, outs, specs, flops=1 << 32)
+    flux_x = [p.reshape((rx + extra) * yc, lanes) for p in out[:gx]]
+    return flux_x, out[gx : gx + gy], out[gx + gy], out[gx + gy + 1], out[gx + gy + 2]
+
+
+def finish(plan, base, div_x, div_y, lanes, cells):
+    gx, gy, rx, ry, yc, sx = plan.gx, plan.gy, plan.rx, plan.ry, plan.yc, plan.sx
+    chunks = len(div_x)
+
+    def kernel(base_ref, *refs):
+        x_refs = [refs[c * gx : (c + 1) * gx] for c in range(chunks)]
+        refs = refs[chunks * gx :]
+        y_refs = [refs[c * gy : (c + 1) * gy] for c in range(chunks)]
+        out_ref, energy_ref, ordered = refs[chunks * gy :]
+        for part in range(gy):
+            start = slot("gy", part, gy, sx)
+
+            def step(inner, carry, part=part, start=start):
+                x = start + inner
+                for c in range(chunks):
+                    where = slice(c * lanes, (c + 1) * lanes)
+                    for t in range(gx):
+                        rows = pl.ds(slot("gx", t, gx, yc), yc)
+                        out_ref[x, rows, where] = base_ref[x, rows, where] - (
+                            x_refs[c][t][x] + y_refs[c][part][inner, rows, :]
+                        )
+                return carry
+
+            lax.fori_loop(0, sx, step, 0)
+        for t, p in enumerate(y_refs[-1]):
+            ordered[pl.ds(slot("gy", t, gy, ROWS), ROWS), :] = p[sx, :ROWS, :]
+        total = ordered[:ROWS, :]
+        for t in range(1, gy):
+            total = total + ordered[t * ROWS : (t + 1) * ROWS, :]
+        energy_ref[...] = total
+
+    ins = [base]
+    for c in range(chunks):
+        ins += [p.reshape(rx, yc, lanes) for p in div_x[c]]
+    for c in range(chunks):
+        ins += list(div_y[c])
+    outs = [(rx, ry, plan.z), (ROWS, lanes)]
+    scratch = [pltpu.VMEM((gy * ROWS, lanes), jnp.float32)]
+    out, energy = call(kernel, ins, outs, scratch=scratch, flops=1 << 24)
+    return out, jnp.sum(energy) / float(cells)
+
+
+def body(density):
+    return tiled_body(density)
+
+
+def tiled_body(density):
+    plan = Plan(density.shape)
+    gx, gy = plan.gx, plan.gy
+    count_x, count_y, count_z = plan.rx * gx, plan.ry * gy, plan.z
+    matrix_x, matrix_y, matrix_z = split_matrix(count_x), split_matrix(count_y), split_matrix(count_z)
+    chunks = 2
+    lanes = plan.z // chunks
+
+    out = pack_x(plan, density, 0, lanes)
+    dens_x = [rotate(out, "gx", gx)]
+    out = pack_y(plan, *after([density], out[0]))
+    dens_y = rotate(out, "gy", gy)
+    for c in range(1, chunks):
+        out = pack_x(plan, *after([density], out[0]), c, lanes)
+        dens_x.append(rotate(out, "gx", gx))
+    grad_z = deriv_z(plan, matrix_z, *after([density], out[0]))
+    out = deriv_y(plan, matrix_y, after(dens_y, grad_z), plan.z)
+    grad_y = rotate(out, "gy", gy)
+    grad_x = []
+    for c in range(chunks):
+        pieces = after(dens_x[c], out[0])
+        out = deriv_x(plan, matrix_x, pieces, lanes, False)
+        grad_x.append(rotate(out, "gx", gx))
+
+    token, energy = out[0], None
+    flux_x, flux_y, flux_z, d_dens = [], [], [], []
+    for c in range(chunks):
+        before = energy if c == chunks - 1 else None
+        pieces = after(grad_x[c], token)
+        f_x, f_y, f_z, dd, energy = pointwise(
+            plan, density, grad_z, grad_y, pieces, c, lanes, before
+        )
+        token = energy
+        flux_x.append(rotate(f_x, "gx", gx))
+        flux_y.append(rotate(f_y, "gy", gy))
+        flux_z.append(f_z)
+        d_dens.append(dd)
+    base = less_deriv_z(plan, matrix_z, d_dens, flux_z)
+    token = base
+    div_x, div_y = [], []
+    for c in range(chunks):
+        last = c == chunks - 1
+        out = deriv_x(plan, matrix_x, after(flux_x[c], token), lanes, last)
+        div_x.append(rotate(out[:gx], "gx", gx))
+        summed = out[gx] if last else None
+        out = deriv_y(plan, matrix_y, after(flux_y[c], out[0]), lanes, summed)
+        div_y.append(rotate(out, "gy", gy))
+        token = out[0]
+    return finish(plan, base, div_x, div_y, lanes, count_x * count_y * count_z)
 
 
 def xc_energy(electrons, grad_sq):
@@ -69,34 +479,34 @@
     return (jnp.cos(phase), jnp.sin(phase))
 
 
-def deriv_matrix(count):
+def plain_matrix(count):
     positions = jnp.arange(count, dtype=jnp.int32)
     cosine, sine = dft_tables(count, positions)
     waves = wavenum(positions, count)
-    first = jnp.dot(cosine.T * waves[None, :], sine, precision=highest)
-    second = jnp.dot(sine.T * waves[None, :], cosine, precision=highest)
+    first = jnp.dot(cosine.T * waves[None, :], sine, precision=lax.Precision.HIGHEST)
+    second = jnp.dot(sine.T * waves[None, :], cosine, precision=lax.Precision.HIGHEST)
     return (first - second) / float(count)
 
 
-def body(density):
+def plain_body(density):
     count_gx = lax.axis_size("gx")
     count_gy = lax.axis_size("gy")
     rows_x, rows_y, count_z = density.shape
     count_x = rows_x * count_gx
     count_y = rows_y * count_gy
-    deriv_x = deriv_matrix(count_x)
-    deriv_y = deriv_matrix(count_y)
-    deriv_z = deriv_matrix(count_z)
+    deriv_x = plain_matrix(count_x)
+    deriv_y = plain_matrix(count_y)
+    deriv_z = plain_matrix(count_z)
 
     def line_x(piece):
         flat = piece.reshape(piece.shape[0], piece.shape[1] * piece.shape[2])
-        result = jnp.dot(deriv_x, flat, precision=highest)
+        result = jnp.dot(deriv_x, flat, precision=lax.Precision.HIGHEST)
         return result.reshape(piece.shape)
 
     def line_y(piece):
         turned = jnp.swapaxes(piece, 0, 1)
         flat = turned.reshape(turned.shape[0], turned.shape[1] * turned.shape[2])
-        result = jnp.dot(deriv_y, flat, precision=highest).reshape(turned.shape)
+        result = jnp.dot(deriv_y, flat, precision=lax.Precision.HIGHEST).reshape(turned.shape)
         return jnp.swapaxes(result, 0, 1)
 
     def along_x(field):
@@ -109,7 +519,7 @@
 
     def along_z(field):
         flat = field.reshape(field.shape[0] * field.shape[1], field.shape[2])
-        result = jnp.dot(flat, deriv_z.T, precision=highest)
+        result = jnp.dot(flat, deriv_z.T, precision=lax.Precision.HIGHEST)
         return result.reshape(field.shape)
 
     gradients = [along_x(density), along_y(density), along_z(density)]
@@ -127,4 +537,18 @@
 def solution(mesh):
     in_specs = (P("gx", "gy", None),)
     out_specs = (P("gx", "gy", None), P())
-    return jax.shard_map(body, mesh=mesh, in_specs=in_specs, out_specs=out_specs, check_vma=False)
+
+    def run(density):
+        gx, gy = mesh.shape["gx"], mesh.shape["gy"]
+        x, y, z = density.shape
+        tiled = Plan.fits((x // gx, y // gy, z), gx, gy)
+        step = jax.shard_map(
+            body if tiled else plain_body,
+            mesh=mesh,
+            in_specs=in_specs,
+            out_specs=out_specs,
+            check_vma=False,
+        )
+        return step(density)
+
+    return run

time: 543 us -> 263 us (0.48)
  local copies, waits for them, and re-layouts: 230 us -> 4.18 us
  other arithmetic: 95 us -> 1.29 us
  blocking collectives: 69.7 us -> 0 us
  starting transfers between devices: 37.4 us -> 103 us
  Pallas kernels: 0 us -> 65.3 us
  matrix products: 44.7 us -> 0 us
  waiting for transfers between devices: 56.8 us -> 84.7 us
    ppermute x0 -> x74, starting transfers between devices: none -> 103 us  [rotate(): arrived[size - t] = lax.ppermute(pieces[t], axis, pairs)]
    unnamed x25 -> x176, local copies, waits for them, and re-layouts: 96 us -> 4.18 us
    ppermute x0 -> x74, waiting for transfers between devices: none -> 84.7 us  [rotate(): arrived[size - t] = lax.ppermute(pieces[t], axis, pairs)]
    all_to_all x15 -> x0, local copies, waits for them, and re-layouts: 80 us -> none  [the longest x4 24.6 us: along_y(): return lax.all_to_all(lines, 'gy', split_axis=1, concat_axis=2, tiled=True)]
    psum x1 -> x0, blocking collectives: 69.7 us -> none  [total_energy(): return lax.psum(energy_local, ('gx', 'gy')) / float(cells)]
    all_to_all x8 -> x0, other arithmetic: 67.5 us -> none  [the longest x2 18 us: along_y(): return lax.all_to_all(lines, 'gy', split_axis=1, concat_axis=2, tiled=True)]
    pallas_call x0 -> x15, Pallas kernels: none -> 65.3 us  [the longest x13 55.5 us: call(): pl.pallas_call(kernel, grid=(1,), in_specs=specs, out_specs=[whole(o) for...]
    all_to_all x8 -> x0, waiting for transfers between devices: 56.8 us -> none  [the longest x2 26.2 us: along_y(): lax.all_to_all(field, 'gy', split_axis=2, concat_axis=1, tiled=True)]
  transfers between devices with their start and end apart: 8 -> 74, of which waited for: 5 -> 23; matrix products, arithmetic and copies ran while one was open for 44% -> 0% of each run, Pallas kernels for 0% -> 21%
where the time goes in v1:
time: 263 us; the launch traced here: 262 us
  starting transfers between devices  103 us (39%)
  waiting for transfers between devices  84.7 us (32%)
  Pallas kernels  65.3 us (25%)
  local copies, waits for them, and re-layouts  4.18 us (2%)
  between operations  3.35 us (1%)
    ppermute x74, starting transfers between devices, rotate(): arrived[size - t] = lax.ppermute(pieces[t], axis, pairs)  103 us
    ppermute x74, waiting for transfers between devices, rotate(): arrived[size - t] = lax.ppermute(pieces[t], axis, pairs)  84.7 us
    pallas_call x13, Pallas kernels, call(): pl.pallas_call(kernel, grid=(1,), in_specs=specs, out_specs=[whole(o) for...  55.5 us
    pallas_call x2, Pallas kernels, rows_call(): pl.pallas_call(kernel, grid=(4,), in_specs=[pl.BlockSpec(m.shape, lambda...  9.81 us
  transfers between devices with their start and end apart: 74, of which 23 were waited for; matrix products, arithmetic and copies ran while one was open for 0% of the time, Pallas kernels for 21%

profile of v1, /device:TPU:0, one launch (start us, length us, event | category | flops | bytes accessed | tf_op | source)
XLA Modules:
  0.0 262.1 jit_solution(2110885213874423314)
XLA Ops:
  0.6 2.4 shard_map.86
  3.0 3.1 %shard_map.87 = (f32[8,64,256]{2,1,0:T(8,128)}, f32[8,64,256]{2,1,0:T(8,128)}, f32[8,64,256]{2,1,0:T(8,128)}, f32[8,64,256]{2,1,0:T(8,128)}) custom-call(f32[32,64,256]{2,1,0:T(8,128)} %refs_0_.3), custom_call_target="tpu_custom_call" | custom-call | flops 1048576 | bytes 4194304 | tf_op jit(solution)/shard_map/pallas_call | solution.py:127
  6.2 3.9 %collective-permute-start = (f32[8,64,256]{2,1,0:T(8,128)}, f32[8,64,256]{2,1,0:T(8,128)S(1)}, u32[]{:S(2)}, u32[]{:S(2)}) collective-permute-start(f32[8,64,256]{2,1,0:T(8,128)} %get-tuple-element.167), channel_id=1, source_target_pairs={{0,3},{1,0},{2,1},{3,2},{4,7},{5,4},{6,5},{7,6},{8,11},{9,8},{10,9... | collective-permute-start | bytes 1572872 | tf_op jit(solution)/shard_map/ppermute | solution.py:177
  11.2 2.2 collective-permute-start.6
  16.3 3.1 %collective-permute-start.8 = (f32[256,128]{1,0:T(8,128)S(1)}, f32[256,128]{1,0:T(8,128)S(1)}, u32[]{:S(2)}, u32[]{:S(2)}) collective-permute-start(f32[256,128]{1,0:T(8,128)S(1)} %copy-done.85), channel_id=1, source_target_pairs={{0,20},{4,24},{8,28},{12,0},{16,4},{20,8},{24,12},{28,16},{1,21},{... | collective-permute-start | bytes 393224 | tf_op jit(solution)/shard_map/ppermute | solution.py:177
  21.1 2.2 collective-permute-done.8.refs_3_
  25.1 6.1 %collective-permute-done.9.refs_4_ = f32[256,128]{1,0:T(8,128)S(1)} collective-permute-done((f32[256,128]{1,0:T(8,128)S(1)}, f32[256,128]{1,0:T(8,128)S(1)}, u32[]{:S(2)}, u32[]{:S(2)}) %collective-permute-start.9) | collective-permute-done | bytes 131104 | tf_op jit(solution)/shard_map/ppermute | solution.py:177
  31.1 2.1 collective-permute-start.11
  33.2 2.8 %collective-permute-start.12 = (f32[256,128]{1,0:T(8,128)S(1)}, f32[256,128]{1,0:T(8,128)S(1)}, u32[]{:S(2)}, u32[]{:S(2)}) collective-permute-start(f32[256,128]{1,0:T(8,128)S(1)} %copy-done.71), channel_id=1, source_target_pairs={{0,4},{4,8},{8,12},{12,16},{16,20},{20,24},{24,28},{28,0},{1,5},{5... | collective-permute-start | bytes 393224 | tf_op jit(solution)/shard_map/ppermute | solution.py:177
  36.0 2.4 shard_map.88
  38.4 2.4 collective-permute-start.20
  41.3 4.7 %shard_map.89 = f32[2048,256]{1,0:T(8,128)} custom-call(bf16[256,256]{1,0:T(8,128)(2,1)} %constant.9.clone.high_ref, bf16[256,256]{1,0:T(8,128)(2,1)} %constant.10.clone.low_ref, f32[2048,256]{1,0:T(8,128)} %bitcast.55), custom_call_target="tpu_custom_call" | custom-call | flops 268435456 | bytes 4194304 | tf_op jit(solution)/shard_map/pallas_call | solution.py:247
  46.1 4.0 %shard_map.90 = (f32[8,64,256]{2,1,0:T(8,128)}, f32[8,64,256]{2,1,0:T(8,128)}, f32[8,64,256]{2,1,0:T(8,128)}, f32[8,64,256]{2,1,0:T(8,128)}) custom-call(bf16[256,256]{1,0:T(8,128)(2,1)} %constant.9.clone.high_ref, bf16[256,256]{1,0:T(8,128)(2,1)} %constant.10.clone.low_ref, f32[8,64,256]{2,1,0:T(8,128)} %get-tuple-element.170.refs_0_, ...), custom_call_target="tpu_custom_call" | custom-call | flops 268435456 | bytes 4718592 | tf_op jit(solution)/shard_map/pallas_call | solution.py:127
  50.1 2.5 collective-permute-start.23
  53.3 3.0 %shard_map.91 = (f32[256,128]{1,0:T(8,128)}, f32[256,128]{1,0:T(8,128)}, f32[256,128]{1,0:T(8,128)}, f32[256,128]{1,0:T(8,128)}, f32[256,128]{1,0:T(8,128)}, /*i...) custom-call(bf16[256,256]{1,0:T(8,128)(2,1)} %constant.9.clone.high_ref, ...), custom_call_target="tpu_custom_call" | custom-call | flops 268435456 | bytes 2621440 | tf_op jit(solution)/shard_map/pallas_call | solution.py:127
  57.7 3.3 %collective-permute-start.13 = (f32[256,128]{1,0:T(8,128)}, f32[256,128]{1,0:T(8,128)S(1)}, u32[]{:S(2)}, u32[]{:S(2)}) collective-permute-start(f32[256,128]{1,0:T(8,128)} %get-tuple-element.194), channel_id=1, source_target_pairs={{0,28},{4,0},{8,4},{12,8},{16,12},{20,16},{24,20},{28,24},{1,29},{... | collective-permute-start | bytes 393224 | tf_op jit(solution)/shard_map/ppermute | solution.py:177
  61.1 6.0 %collective-permute-done.23.refs_4_ = f32[256,128]{1,0:T(8,128)S(1)} collective-permute-done((f32[256,128]{1,0:T(8,128)S(1)}, f32[256,128]{1,0:T(8,128)S(1)}, u32[]{:S(2)}, u32[]{:S(2)}) %collective-permute-start.23) | collective-permute-done | bytes 131104 | tf_op jit(solution)/shard_map/ppermute | solution.py:177
  67.1 3.4 %collective-permute-done.24.refs_5_ = f32[256,128]{1,0:T(8,128)S(1)} collective-permute-done((f32[256,128]{1,0:T(8,128)S(1)}, f32[256,128]{1,0:T(8,128)S(1)}, u32[]{:S(2)}, u32[]{:S(2)}) %collective-permute-start.24) | collective-permute-done | bytes 131104 | tf_op jit(solution)/shard_map/ppermute | solution.py:177
  70.5 2.4 collective-permute-start.3
  75.7 10.5 %collective-permute-done.16 = f32[256,128]{1,0:T(8,128)S(1)} collective-permute-done((f32[256,128]{1,0:T(8,128)}, f32[256,128]{1,0:T(8,128)S(1)}, u32[]{:S(2)}, u32[]{:S(2)}) %collective-permute-start.16) | collective-permute-done | bytes 131104 | tf_op jit(solution)/shard_map/ppermute | solution.py:177
  87.1 3.0 %shard_map.92 = (f32[256,128]{1,0:T(8,128)}, f32[256,128]{1,0:T(8,128)}, f32[256,128]{1,0:T(8,128)}, f32[256,128]{1,0:T(8,128)}, f32[256,128]{1,0:T(8,128)}, /*i...) custom-call(bf16[256,256]{1,0:T(8,128)(2,1)} %constant.9.clone.high_ref, ...), custom_call_target="tpu_custom_call" | custom-call | flops 268435456 | bytes 2621440 | tf_op jit(solution)/shard_map/pallas_call | solution.py:127
  90.1 4.1 %collective-permute-done.18 = f32[256,128]{1,0:T(8,128)S(1)} collective-permute-done((f32[256,128]{1,0:T(8,128)}, f32[256,128]{1,0:T(8,128)S(1)}, u32[]{:S(2)}, u32[]{:S(2)}) %collective-permute-start.18) | collective-permute-done | bytes 131104 | tf_op jit(solution)/shard_map/ppermute | solution.py:177
  94.8 3.4 %collective-permute-done.27 = f32[256,128]{1,0:T(8,128)S(1)} collective-permute-done((f32[256,128]{1,0:T(8,128)}, f32[256,128]{1,0:T(8,128)S(1)}, u32[]{:S(2)}, u32[]{:S(2)}) %collective-permute-start.27) | collective-permute-done | bytes 131104 | tf_op jit(solution)/shard_map/ppermute | solution.py:177
  102.3 2.5 collective-permute-start.32
  105.7 10.1 %shard_map.93 = (f32[32,8,128]{2,1,0:T(8,128)}, f32[32,8,128]{2,1,0:T(8,128)}, f32[32,8,128]{2,1,0:T(8,128)}, f32[32,8,128]{2,1,0:T(8,128)}, f32[32,8,128]{2,1,0...) custom-call(f32[32,64,256]{2,1,0:T(8,128)} %refs_0_.3, ...), custom_call_target="tpu_custom_call" | custom-call | flops 4294967296 | bytes 11538432 | tf_op jit(solution)/shard_map/pallas_call | solution.py:127
  115.9 2.9 %collective-permute-start.34 = (f32[256,128]{1,0:T(8,128)}, f32[256,128]{1,0:T(8,128)S(1)}, u32[]{:S(2)}, u32[]{:S(2)}) collective-permute-start(f32[256,128]{1,0:T(8,128)} %bitcast.110), channel_id=1, source_target_pairs={{0,28},{4,0},{8,4},{12,8},{16,12},{20,16},{24,20},{28,24},{1,29},{... | collective-permute-start | bytes 393224 | tf_op jit(solution)/shard_map/ppermute | solution.py:177
  123.4 2.4 collective-permute-done.35.refs_2_
  125.8 10.2 %shard_map.94 = (f32[33,8,128]{2,1,0:T(8,128)}, f32[33,8,128]{2,1,0:T(8,128)}, f32[33,8,128]{2,1,0:T(8,128)}, f32[33,8,128]{2,1,0:T(8,128)}, f32[33,8,128]{2,1,0...) custom-call(f32[32,64,256]{2,1,0:T(8,128)} %refs_0_.3, ...), custom_call_target="tpu_custom_call" | custom-call | flops 4294967296 | bytes 11575296 | tf_op jit(solution)/shard_map/pallas_call | solution.py:127
  136.1 3.6 %collective-permute-start.48 = (f32[264,128]{1,0:T(8,128)}, f32[264,128]{1,0:T(8,128)S(1)}, u32[]{:S(2)}, u32[]{:S(2)}) collective-permute-start(f32[264,128]{1,0:T(8,128)} %bitcast.87), channel_id=1, source_target_pairs={{0,28},{4,0},{8,4},{12,8},{16,12},{20,16},{24,20},{28,24},{1,29},{... | collective-permute-start | bytes 405512 | tf_op jit(solution)/shard_map/ppermute | solution.py:177
  143.8 10.2 %collective-permute-start.51 = (f32[264,128]{1,0:T(8,128)}, f32[264,128]{1,0:T(8,128)S(1)}, u32[]{:S(2)}, u32[]{:S(2)}) collective-permute-start(f32[264,128]{1,0:T(8,128)} %bitcast.84), channel_id=1, source_target_pairs={{0,16},{4,20},{8,24},{12,28},{16,0},{20,4},{24,8},{28,12},{1,17},{... | collective-permute-start | bytes 405512 | tf_op jit(solution)/shard_map/ppermute | solution.py:177
  154.0 5.1 %shard_map.95 = f32[2048,256]{1,0:T(8,128)} custom-call(bf16[256,256]{1,0:T(8,128)(2,1)} %constant.9.clone.high_ref, bf16[256,256]{1,0:T(8,128)(2,1)} %constant.10.clone.low_ref, f32[2048,128]{1,0:T(8,128)} %bitcast.60, f32[2048,128]{1,0:T(8,128)} %bitcast.62, f32[2048,128]{1,0:T(8,128)} %bitcast.59, f32[2048,128]{1,0:T(8,128)} %bitcast.61), custom_call_target="tpu_custom_call" | custom-call | flops 268435456 | bytes 4194304 | tf_op jit(solution)/shard_map/pallas_call | solution.py:247
  160.1 3.1 %shard_map.96 = (f32[256,128]{1,0:T(8,128)}, f32[256,128]{1,0:T(8,128)}, f32[256,128]{1,0:T(8,128)}, f32[256,128]{1,0:T(8,128)}, f32[256,128]{1,0:T(8,128)}, /*i...) custom-call(bf16[256,256]{1,0:T(8,128)(2,1)} %constant.9.clone.high_ref, ...), custom_call_target="tpu_custom_call" | custom-call | flops 268435456 | bytes 2621440 | tf_op jit(solution)/shard_map/pallas_call | solution.py:127
  163.2 2.8 %collective-permute-start.41 = (f32[256,128]{1,0:T(8,128)}, f32[256,128]{1,0:T(8,128)S(1)}, u32[]{:S(2)}, u32[]{:S(2)}) collective-permute-start(f32[256,128]{1,0:T(8,128)} %get-tuple-element.262), channel_id=1, source_target_pairs={{0,28},{4,0},{8,4},{12,8},{16,12},{20,16},{24,20},{28,24},{1,29},{... | collective-permute-start | bytes 393224 | tf_op jit(solution)/shard_map/ppermute | solution.py:177
  168.0 3.2 %collective-permute-start.55 = (f32[8,64,128]{2,1,0:T(8,128)}, f32[8,64,128]{2,1,0:T(8,128)S(1)}, u32[]{:S(2)}, u32[]{:S(2)}) collective-permute-start(f32[8,64,128]{2,1,0:T(8,128)} %get-tuple-element.278), channel_id=1, source_target_pairs={{0,3},{1,0},{2,1},{3,2},{4,7},{5,4},{6,5},{7,6},{8,11},{9,8},{10,9... | collective-permute-start | bytes 786440 | tf_op jit(solution)/shard_map/ppermute | solution.py:177
  176.4 8.0 %collective-permute-done.44 = f32[256,128]{1,0:T(8,128)S(1)} collective-permute-done((f32[256,128]{1,0:T(8,128)}, f32[256,128]{1,0:T(8,128)S(1)}, u32[]{:S(2)}, u32[]{:S(2)}) %collective-permute-start.44) | collective-permute-done | bytes 131104 | tf_op jit(solution)/shard_map/ppermute | solution.py:177
  184.4 2.0 collective-permute-start.68
  189.1 2.1 collective-permute-start.46
  191.9 2.9 %shard_map.97 = (f32[8,64,128]{2,1,0:T(8,128)}, f32[8,64,128]{2,1,0:T(8,128)}, f32[8,64,128]{2,1,0:T(8,128)}, f32[8,64,128]{2,1,0:T(8,128)}) custom-call(bf16[256,256]{1,0:T(8,128)(2,1)} %constant.9.clone.high_ref, bf16[256,256]{1,0:T(8,128)(2,1)} %constant.10.clone.low_ref, f32[8,64,128]{2,1,0:T(8,128)} %get-tuple-element.281.refs_0_, ...), custom_call_target="tpu_custom_call" | custom-call | flops 268435456 | bytes 2621440 | tf_op jit(solution)/shard_map/pallas_call | solution.py:127
  194.9 3.0 %shard_map.98 = (f32[256,128]{1,0:T(8,128)}, f32[256,128]{1,0:T(8,128)}, f32[256,128]{1,0:T(8,128)}, f32[256,128]{1,0:T(8,128)}, f32[256,128]{1,0:T(8,128)}, /*i...) custom-call(bf16[256,256]{1,0:T(8,128)(2,1)} %constant.9.clone.high_ref, ...), custom_call_target="tpu_custom_call" | custom-call | flops 268435456 | bytes 2658304 | tf_op jit(solution)/shard_map/pallas_call | solution.py:127
  197.9 2.9 %collective-permute-start.58 = (f32[256,128]{1,0:T(8,128)}, f32[256,128]{1,0:T(8,128)S(1)}, u32[]{:S(2)}, u32[]{:S(2)}) collective-permute-start(f32[256,128]{1,0:T(8,128)} %get-tuple-element.295), channel_id=1, source_target_pairs={{0,28},{4,0},{8,4},{12,8},{16,12},{20,16},{24,20},{28,24},{1,29},{... | collective-permute-start | bytes 393224 | tf_op jit(solution)/shard_map/ppermute | solution.py:177
  205.1 2.8 %collective-permute-done.59 = f32[256,128]{1,0:T(8,128)S(1)} collective-permute-done((f32[256,128]{1,0:T(8,128)}, f32[256,128]{1,0:T(8,128)S(1)}, u32[]{:S(2)}, u32[]{:S(2)}) %collective-permute-start.59) | collective-permute-done | bytes 131104 | tf_op jit(solution)/shard_map/ppermute | solution.py:177
  207.9 2.8 %collective-permute-done.60 = f32[256,128]{1,0:T(8,128)S(1)} collective-permute-done((f32[256,128]{1,0:T(8,128)}, f32[256,128]{1,0:T(8,128)S(1)}, u32[]{:S(2)}, u32[]{:S(2)}) %collective-permute-start.60) | collective-permute-done | bytes 131104 | tf_op jit(solution)/shard_map/ppermute | solution.py:177
  210.7 8.0 %collective-permute-start.64 = (f32[256,128]{1,0:T(8,128)}, f32[256,128]{1,0:T(8,128)S(1)}, u32[]{:S(2)}, u32[]{:S(2)}) collective-permute-start(f32[256,128]{1,0:T(8,128)} %get-tuple-element.301), channel_id=1, source_target_pairs={{0,4},{4,8},{8,12},{12,16},{16,20},{20,24},{24,28},{28,0},{1,5},{5... | collective-permute-start | bytes 393224 | tf_op jit(solution)/shard_map/ppermute | solution.py:177
  218.7 2.9 %shard_map.99 = (f32[9,64,128]{2,1,0:T(8,128)}, f32[9,64,128]{2,1,0:T(8,128)}, f32[9,64,128]{2,1,0:T(8,128)}, f32[9,64,128]{2,1,0:T(8,128)}) custom-call(bf16[256,256]{1,0:T(8,128)(2,1)} %constant.9.clone.high_ref, bf16[256,256]{1,0:T(8,128)(2,1)} %constant.10.clone.low_ref, f32[8,128]{1,0:T(8,128)} %get-tuple-element.305.refs_0_, ...), custom_call_target="tpu_custom_call" | custom-call | flops 268435456 | bytes 2756608 | tf_op jit(solution)/shard_map/pallas_call | solution.py:127
  223.1 2.8 %collective-permute-start.71 = (f32[9,64,128]{2,1,0:T(8,128)}, f32[9,64,128]{2,1,0:T(8,128)S(1)}, u32[]{:S(2)}, u32[]{:S(2)}) collective-permute-start(f32[9,64,128]{2,1,0:T(8,128)} %get-tuple-element.315), channel_id=1, source_target_pairs={{0,3},{1,0},{2,1},{3,2},{4,7},{5,4},{6,5},{7,6},{8,11},{9,8},{10,9... | collective-permute-start | bytes 884744 | tf_op jit(solution)/shard_map/ppermute | solution.py:177
  229.1 2.8 %collective-permute-start.67 = (f32[8,64,128]{2,1,0:T(8,128)}, f32[8,64,128]{2,1,0:T(8,128)S(1)}, u32[]{:S(2)}, u32[]{:S(2)}) collective-permute-start(f32[8,64,128]{2,1,0:T(8,128)} %get-tuple-element.304), channel_id=1, source_target_pairs={{0,1},{1,2},{2,3},{3,0},{4,5},{5,6},{6,7},{7,4},{8,9},{9,10},{10,1... | collective-permute-start | bytes 786440 | tf_op jit(solution)/shard_map/ppermute | solution.py:177
  231.9 20.5 %collective-permute-done.66.refs_18_ = f32[8,64,128]{2,1,0:T(8,128)S(1)} collective-permute-done((f32[8,64,128]{2,1,0:T(8,128)}, f32[8,64,128]{2,1,0:T(8,128)S(1)}, u32[]{:S(2)}, u32[]{:S(2)}) %collective-permute-start.66) | collective-permute-done | bytes 262176 | tf_op jit(solution)/shard_map/ppermute | solution.py:177
  253.6 5.5 %shard_map.100 = (f32[32,64,256]{2,1,0:T(8,128)}, f32[8,128]{1,0:T(8,128)}) custom-call(f32[32,64,256]{2,1,0:T(8,128)} %bitcast.56, f32[32,8,128]{2,1,0:T(8,128)} %bitcast.64, f32[32,8,128]{2,1,0:T(8,128)} %bitcast.65, f32[32,8,128]{2,1,0:T(8,128)} %bitcast.66, f32[32,8,128]{2,1,0:T(8,128)} %bitcast.67, f32[32,8,128]{2,1,0:T(8,128)} %bitcast.68, ...), custom_call_target="tpu_custom_call" | custom-call | flops 16777216 | bytes 8523776 | tf_op jit(solution)/shard_map/pallas_call | solution.py:127
  (292 shorter events, 50.7 us)
Async XLA Ops:
  6.2 32.2 %collective-permute-start = (f32[8,64,256]{2,1,0:T(8,128)}, f32[8,64,256]{2,1,0:T(8,128)S(1)}, u32[]{:S(2)}, u32[]{:S(2)}) collective-permute-start(f32[8,64,256]{2,1,0:T(8,128)} %get-tuple-element.167), channel_id=1, source_target_pairs={{0,3},{1,0},{2,1},{3,2},{4,7},{5,4},{6,5},{7,6},{8,11},{9,8},{10,9... | collective-permute-start | bytes 1572872 | tf_op jit(solution)/shard_map/ppermute | solution.py:177
  10.1 30.8 %collective-permute-start.1 = (f32[8,64,256]{2,1,0:T(8,128)}, f32[8,64,256]{2,1,0:T(8,128)S(1)}, u32[]{:S(2)}, u32[]{:S(2)}) collective-permute-start(f32[8,64,256]{2,1,0:T(8,128)} %get-tuple-element.168), channel_id=1, source_target_pairs={{0,2},{1,3},{2,0},{3,1},{4,6},{5,7},{6,4},{7,5},{8,10},{9,11},{10,... | collective-permute-start | bytes 1572872 | tf_op jit(solution)/shard_map/ppermute | solution.py:177
  10.6 30.7 %collective-permute-start.2 = (f32[8,64,256]{2,1,0:T(8,128)}, f32[8,64,256]{2,1,0:T(8,128)S(1)}, u32[]{:S(2)}, u32[]{:S(2)}) collective-permute-start(f32[8,64,256]{2,1,0:T(8,128)} %get-tuple-element.169), channel_id=1, source_target_pairs={{0,1},{1,2},{2,3},{3,0},{4,5},{5,6},{6,7},{7,4},{8,9},{9,10},{10,1... | collective-permute-start | bytes 1572872 | tf_op jit(solution)/shard_map/ppermute | solution.py:177
  31.1 19.0 %collective-permute-start.11 = (f32[256,128]{1,0:T(8,128)S(1)}, f32[256,128]{1,0:T(8,128)S(1)}, u32[]{:S(2)}, u32[]{:S(2)}) collective-permute-start(f32[256,128]{1,0:T(8,128)S(1)} %copy-done.75), channel_id=1, source_target_pairs={{0,8},{4,12},{8,16},{12,20},{16,24},{20,28},{24,0},{28,4},{1,9},{5... | collective-permute-start | bytes 393224 | tf_op jit(solution)/shard_map/ppermute | solution.py:177
  33.2 19.4 %collective-permute-start.12 = (f32[256,128]{1,0:T(8,128)S(1)}, f32[256,128]{1,0:T(8,128)S(1)}, u32[]{:S(2)}, u32[]{:S(2)}) collective-permute-start(f32[256,128]{1,0:T(8,128)S(1)} %copy-done.71), channel_id=1, source_target_pairs={{0,4},{4,8},{8,12},{12,16},{16,20},{20,24},{24,28},{28,0},{1,5},{5... | collective-permute-start | bytes 393224 | tf_op jit(solution)/shard_map/ppermute | solution.py:177
  38.4 17.9 %collective-permute-start.20 = (f32[256,128]{1,0:T(8,128)}, f32[256,128]{1,0:T(8,128)S(1)}, u32[]{:S(2)}, u32[]{:S(2)}) collective-permute-start(f32[256,128]{1,0:T(8,128)} %get-tuple-element.201), channel_id=1, source_target_pairs={{0,28},{4,0},{8,4},{12,8},{16,12},{20,16},{24,20},{28,24},{1,29},{... | collective-permute-start | bytes 393224 | tf_op jit(solution)/shard_map/ppermute | solution.py:177
  40.9 16.6 %collective-permute-start.21 = (f32[256,128]{1,0:T(8,128)}, f32[256,128]{1,0:T(8,128)S(1)}, u32[]{:S(2)}, u32[]{:S(2)}) collective-permute-start(f32[256,128]{1,0:T(8,128)} %get-tuple-element.202), channel_id=1, source_target_pairs={{0,24},{4,28},{8,0},{12,4},{16,8},{20,12},{24,16},{28,20},{1,25},{... | collective-permute-start | bytes 393224 | tf_op jit(solution)/shard_map/ppermute | solution.py:177
  41.3 16.4 %collective-permute-start.22 = (f32[256,128]{1,0:T(8,128)}, f32[256,128]{1,0:T(8,128)S(1)}, u32[]{:S(2)}, u32[]{:S(2)}) collective-permute-start(f32[256,128]{1,0:T(8,128)} %get-tuple-element.203), channel_id=1, source_target_pairs={{0,20},{4,24},{8,28},{12,0},{16,4},{20,8},{24,12},{28,16},{1,21},{... | collective-permute-start | bytes 393224 | tf_op jit(solution)/shard_map/ppermute | solution.py:177
  50.1 17.0 %collective-permute-start.23 = (f32[256,128]{1,0:T(8,128)S(1)}, f32[256,128]{1,0:T(8,128)S(1)}, u32[]{:S(2)}, u32[]{:S(2)}) collective-permute-start(f32[256,128]{1,0:T(8,128)S(1)} %copy-done.82), channel_id=1, source_target_pairs={{0,16},{4,20},{8,24},{12,28},{16,0},{20,4},{24,8},{28,12},{1,17},{... | collective-permute-start | bytes 393224 | tf_op jit(solution)/shard_map/ppermute | solution.py:177
  52.6 17.8 %collective-permute-start.24 = (f32[256,128]{1,0:T(8,128)S(1)}, f32[256,128]{1,0:T(8,128)S(1)}, u32[]{:S(2)}, u32[]{:S(2)}) collective-permute-start(f32[256,128]{1,0:T(8,128)S(1)} %copy-done.80), channel_id=1, source_target_pairs={{0,12},{4,16},{8,20},{12,24},{16,28},{20,0},{24,4},{28,8},{1,13},{... | collective-permute-start | bytes 393224 | tf_op jit(solution)/shard_map/ppermute | solution.py:177
  56.3 14.2 %collective-permute-start.25 = (f32[256,128]{1,0:T(8,128)S(1)}, f32[256,128]{1,0:T(8,128)S(1)}, u32[]{:S(2)}, u32[]{:S(2)}) collective-permute-start(f32[256,128]{1,0:T(8,128)S(1)} %copy-done.77), channel_id=1, source_target_pairs={{0,8},{4,12},{8,16},{12,20},{16,24},{20,28},{24,0},{28,4},{1,9},{5... | collective-permute-start | bytes 393224 | tf_op jit(solution)/shard_map/ppermute | solution.py:177
  57.5 15.4 %collective-permute-start.26 = (f32[256,128]{1,0:T(8,128)S(1)}, f32[256,128]{1,0:T(8,128)S(1)}, u32[]{:S(2)}, u32[]{:S(2)}) collective-permute-start(f32[256,128]{1,0:T(8,128)S(1)} %copy-done.73), channel_id=1, source_target_pairs={{0,4},{4,8},{8,12},{12,16},{16,20},{20,24},{24,28},{28,0},{1,5},{5... | collective-permute-start | bytes 393224 | tf_op jit(solution)/shard_map/ppermute | solution.py:177
  57.7 16.6 %collective-permute-start.13 = (f32[256,128]{1,0:T(8,128)}, f32[256,128]{1,0:T(8,128)S(1)}, u32[]{:S(2)}, u32[]{:S(2)}) collective-permute-start(f32[256,128]{1,0:T(8,128)} %get-tuple-element.194), channel_id=1, source_target_pairs={{0,28},{4,0},{8,4},{12,8},{16,12},{20,16},{24,20},{28,24},{1,29},{... | collective-permute-start | bytes 393224 | tf_op jit(solution)/shard_map/ppermute | solution.py:177
  70.5 30.4 %collective-permute-start.3 = (f32[8,64,256]{2,1,0:T(8,128)}, f32[8,64,256]{2,1,0:T(8,128)S(1)}, u32[]{:S(2)}, u32[]{:S(2)}) collective-permute-start(f32[8,64,256]{2,1,0:T(8,128)} %get-tuple-element.175), channel_id=1, source_target_pairs={{0,3},{1,0},{2,1},{3,2},{4,7},{5,4},{6,5},{7,6},{8,11},{9,8},{10,9... | collective-permute-start | bytes 1572872 | tf_op jit(solution)/shard_map/ppermute | solution.py:177
  72.9 29.4 %collective-permute-start.4 = (f32[8,64,256]{2,1,0:T(8,128)}, f32[8,64,256]{2,1,0:T(8,128)S(1)}, u32[]{:S(2)}, u32[]{:S(2)}) collective-permute-start(f32[8,64,256]{2,1,0:T(8,128)} %get-tuple-element.176), channel_id=1, source_target_pairs={{0,2},{1,3},{2,0},{3,1},{4,6},{5,7},{6,4},{7,5},{8,10},{9,11},{10,... | collective-permute-start | bytes 1572872 | tf_op jit(solution)/shard_map/ppermute | solution.py:177
  74.4 30.5 %collective-permute-start.5 = (f32[8,64,256]{2,1,0:T(8,128)}, f32[8,64,256]{2,1,0:T(8,128)S(1)}, u32[]{:S(2)}, u32[]{:S(2)}) collective-permute-start(f32[8,64,256]{2,1,0:T(8,128)} %get-tuple-element.177), channel_id=1, source_target_pairs={{0,1},{1,2},{2,3},{3,0},{4,5},{5,6},{6,7},{7,4},{8,9},{9,10},{10,1... | collective-permute-start | bytes 1572872 | tf_op jit(solution)/shard_map/ppermute | solution.py:177
  98.3 17.6 %collective-permute-start.29 = (f32[256,128]{1,0:T(8,128)}, f32[256,128]{1,0:T(8,128)S(1)}, u32[]{:S(2)}, u32[]{:S(2)}) collective-permute-start(f32[256,128]{1,0:T(8,128)} %get-tuple-element.228), channel_id=1, source_target_pairs={{0,20},{4,24},{8,28},{12,0},{16,4},{20,8},{24,12},{28,16},{1,21},{... | collective-permute-start | bytes 393224 | tf_op jit(solution)/shard_map/ppermute | solution.py:177
  100.6 18.1 %collective-permute-start.30 = (f32[256,128]{1,0:T(8,128)}, f32[256,128]{1,0:T(8,128)S(1)}, u32[]{:S(2)}, u32[]{:S(2)}) collective-permute-start(f32[256,128]{1,0:T(8,128)} %get-tuple-element.229), channel_id=1, source_target_pairs={{0,16},{4,20},{8,24},{12,28},{16,0},{20,4},{24,8},{28,12},{1,17},{... | collective-permute-start | bytes 393224 | tf_op jit(solution)/shard_map/ppermute | solution.py:177
  100.9 18.8 %collective-permute-start.31 = (f32[256,128]{1,0:T(8,128)}, f32[256,128]{1,0:T(8,128)S(1)}, u32[]{:S(2)}, u32[]{:S(2)}) collective-permute-start(f32[256,128]{1,0:T(8,128)} %get-tuple-element.230), channel_id=1, source_target_pairs={{0,12},{4,16},{8,20},{12,24},{16,28},{20,0},{24,4},{28,8},{1,13},{... | collective-permute-start | bytes 393224 | tf_op jit(solution)/shard_map/ppermute | solution.py:177
  102.3 17.4 %collective-permute-start.32 = (f32[256,128]{1,0:T(8,128)}, f32[256,128]{1,0:T(8,128)S(1)}, u32[]{:S(2)}, u32[]{:S(2)}) collective-permute-start(f32[256,128]{1,0:T(8,128)} %get-tuple-element.231), channel_id=1, source_target_pairs={{0,8},{4,12},{8,16},{12,20},{16,24},{20,28},{24,0},{28,4},{1,9},{5... | collective-permute-start | bytes 393224 | tf_op jit(solution)/shard_map/ppermute | solution.py:177
  104.9 14.8 %collective-permute-start.33 = (f32[256,128]{1,0:T(8,128)}, f32[256,128]{1,0:T(8,128)S(1)}, u32[]{:S(2)}, u32[]{:S(2)}) collective-permute-start(f32[256,128]{1,0:T(8,128)} %get-tuple-element.232), channel_id=1, source_target_pairs={{0,4},{4,8},{8,12},{12,16},{16,20},{20,24},{24,28},{28,0},{1,5},{5... | collective-permute-start | bytes 393224 | tf_op jit(solution)/shard_map/ppermute | solution.py:177
  120.4 15.6 %collective-permute-start.36 = (f32[256,128]{1,0:T(8,128)}, f32[256,128]{1,0:T(8,128)S(1)}, u32[]{:S(2)}, u32[]{:S(2)}) collective-permute-start(f32[256,128]{1,0:T(8,128)} %bitcast.106), channel_id=1, source_target_pairs={{0,20},{4,24},{8,28},{12,0},{16,4},{20,8},{24,12},{28,16},{1,21},{... | collective-permute-start | bytes 393224 | tf_op jit(solution)/shard_map/ppermute | solution.py:177
  120.4 20.2 %collective-permute-start.37 = (f32[256,128]{1,0:T(8,128)}, f32[256,128]{1,0:T(8,128)S(1)}, u32[]{:S(2)}, u32[]{:S(2)}) collective-permute-start(f32[256,128]{1,0:T(8,128)} %bitcast.103), channel_id=1, source_target_pairs={{0,16},{4,20},{8,24},{12,28},{16,0},{20,4},{24,8},{28,12},{1,17},{... | collective-permute-start | bytes 393224 | tf_op jit(solution)/shard_map/ppermute | solution.py:177
  122.2 21.6 %collective-permute-start.38 = (f32[256,128]{1,0:T(8,128)}, f32[256,128]{1,0:T(8,128)S(1)}, u32[]{:S(2)}, u32[]{:S(2)}) collective-permute-start(f32[256,128]{1,0:T(8,128)} %bitcast.100), channel_id=1, source_target_pairs={{0,12},{4,16},{8,20},{12,24},{16,28},{20,0},{24,4},{28,8},{1,13},{... | collective-permute-start | bytes 393224 | tf_op jit(solution)/shard_map/ppermute | solution.py:177
  123.4 20.4 %collective-permute-start.39 = (f32[256,128]{1,0:T(8,128)}, f32[256,128]{1,0:T(8,128)S(1)}, u32[]{:S(2)}, u32[]{:S(2)}) collective-permute-start(f32[256,128]{1,0:T(8,128)} %bitcast.98), channel_id=1, source_target_pairs={{0,8},{4,12},{8,16},{12,20},{16,24},{20,28},{24,0},{28,4},{1,9},{5... | collective-permute-start | bytes 393224 | tf_op jit(solution)/shard_map/ppermute | solution.py:177
  125.8 28.2 %collective-permute-start.40 = (f32[256,128]{1,0:T(8,128)}, f32[256,128]{1,0:T(8,128)S(1)}, u32[]{:S(2)}, u32[]{:S(2)}) collective-permute-start(f32[256,128]{1,0:T(8,128)} %bitcast.96), channel_id=1, source_target_pairs={{0,4},{4,8},{8,12},{12,16},{16,20},{20,24},{24,28},{28,0},{1,5},{5... | collective-permute-start | bytes 393224 | tf_op jit(solution)/shard_map/ppermute | solution.py:177
  136.1 23.1 %collective-permute-start.48 = (f32[264,128]{1,0:T(8,128)}, f32[264,128]{1,0:T(8,128)S(1)}, u32[]{:S(2)}, u32[]{:S(2)}) collective-permute-start(f32[264,128]{1,0:T(8,128)} %bitcast.87), channel_id=1, source_target_pairs={{0,28},{4,0},{8,4},{12,8},{16,12},{20,16},{24,20},{28,24},{1,29},{... | collective-permute-start | bytes 405512 | tf_op jit(solution)/shard_map/ppermute | solution.py:177
  140.6 18.6 %collective-permute-start.49 = (f32[264,128]{1,0:T(8,128)}, f32[264,128]{1,0:T(8,128)S(1)}, u32[]{:S(2)}, u32[]{:S(2)}) collective-permute-start(f32[264,128]{1,0:T(8,128)} %bitcast.86), channel_id=1, source_target_pairs={{0,24},{4,28},{8,0},{12,4},{16,8},{20,12},{24,16},{28,20},{1,25},{... | collective-permute-start | bytes 405512 | tf_op jit(solution)/shard_map/ppermute | solution.py:177
  143.8 19.4 %collective-permute-start.50 = (f32[264,128]{1,0:T(8,128)}, f32[264,128]{1,0:T(8,128)S(1)}, u32[]{:S(2)}, u32[]{:S(2)}) collective-permute-start(f32[264,128]{1,0:T(8,128)} %bitcast.85), channel_id=1, source_target_pairs={{0,20},{4,24},{8,28},{12,0},{16,4},{20,8},{24,12},{28,16},{1,21},{... | collective-permute-start | bytes 405512 | tf_op jit(solution)/shard_map/ppermute | solution.py:177
  143.8 22.2 %collective-permute-start.51 = (f32[264,128]{1,0:T(8,128)}, f32[264,128]{1,0:T(8,128)S(1)}, u32[]{:S(2)}, u32[]{:S(2)}) collective-permute-start(f32[264,128]{1,0:T(8,128)} %bitcast.84), channel_id=1, source_target_pairs={{0,16},{4,20},{8,24},{12,28},{16,0},{20,4},{24,8},{28,12},{1,17},{... | collective-permute-start | bytes 405512 | tf_op jit(solution)/shard_map/ppermute | solution.py:177
  154.0 14.0 %collective-permute-start.52 = (f32[264,128]{1,0:T(8,128)}, f32[264,128]{1,0:T(8,128)S(1)}, u32[]{:S(2)}, u32[]{:S(2)}) collective-permute-start(f32[264,128]{1,0:T(8,128)} %bitcast.83), channel_id=1, source_target_pairs={{0,12},{4,16},{8,20},{12,24},{16,28},{20,0},{24,4},{28,8},{1,13},{... | collective-permute-start | bytes 405512 | tf_op jit(solution)/shard_map/ppermute | solution.py:177
  159.3 11.9 %collective-permute-start.54 = (f32[264,128]{1,0:T(8,128)S(1)}, f32[264,128]{1,0:T(8,128)S(1)}, u32[]{:S(2)}, u32[]{:S(2)}) collective-permute-start(f32[264,128]{1,0:T(8,128)S(1)} %bitcast.81), channel_id=1, source_target_pairs={{0,4},{4,8},{8,12},{12,16},{16,20},{20,24},{24,28},{28,0},{1,5},{5... | collective-permute-start | bytes 405512 | tf_op jit(solution)/shard_map/ppermute | solution.py:177
  168.0 19.7 %collective-permute-start.55 = (f32[8,64,128]{2,1,0:T(8,128)}, f32[8,64,128]{2,1,0:T(8,128)S(1)}, u32[]{:S(2)}, u32[]{:S(2)}) collective-permute-start(f32[8,64,128]{2,1,0:T(8,128)} %get-tuple-element.278), channel_id=1, source_target_pairs={{0,3},{1,0},{2,1},{3,2},{4,7},{5,4},{6,5},{7,6},{8,11},{9,8},{10,9... | collective-permute-start | bytes 786440 | tf_op jit(solution)/shard_map/ppermute | solution.py:177
  171.2 17.9 %collective-permute-start.56 = (f32[8,64,128]{2,1,0:T(8,128)S(1)}, f32[8,64,128]{2,1,0:T(8,128)S(1)}, u32[]{:S(2)}, u32[]{:S(2)}) collective-permute-start(f32[8,64,128]{2,1,0:T(8,128)S(1)} %copy-done.60), channel_id=1, source_target_pairs={{0,2},{1,3},{2,0},{3,1},{4,6},{5,7},{6,4},{7,5},{8,10},{9,11},{10,... | collective-permute-start | bytes 786440 | tf_op jit(solution)/shard_map/ppermute | solution.py:177
  171.5 19.7 %collective-permute-start.57 = (f32[8,64,128]{2,1,0:T(8,128)}, f32[8,64,128]{2,1,0:T(8,128)S(1)}, u32[]{:S(2)}, u32[]{:S(2)}) collective-permute-start(f32[8,64,128]{2,1,0:T(8,128)} %get-tuple-element.280), channel_id=1, source_target_pairs={{0,1},{1,2},{2,3},{3,0},{4,5},{5,6},{6,7},{7,4},{8,9},{9,10},{10,1... | collective-permute-start | bytes 786440 | tf_op jit(solution)/shard_map/ppermute | solution.py:177
  184.4 16.5 %collective-permute-start.68 = (f32[8,64,128]{2,1,0:T(8,128)}, f32[8,64,128]{2,1,0:T(8,128)S(1)}, u32[]{:S(2)}, u32[]{:S(2)}) collective-permute-start(f32[8,64,128]{2,1,0:T(8,128)} %get-tuple-element.307), channel_id=1, source_target_pairs={{0,3},{1,0},{2,1},{3,2},{4,7},{5,4},{6,5},{7,6},{8,11},{9,8},{10,9... | collective-permute-start | bytes 786440 | tf_op jit(solution)/shard_map/ppermute | solution.py:177
  186.7 14.2 %collective-permute-start.69 = (f32[8,64,128]{2,1,0:T(8,128)}, f32[8,64,128]{2,1,0:T(8,128)S(1)}, u32[]{:S(2)}, u32[]{:S(2)}) collective-permute-start(f32[8,64,128]{2,1,0:T(8,128)} %get-tuple-element.308), channel_id=1, source_target_pairs={{0,2},{1,3},{2,0},{3,1},{4,6},{5,7},{6,4},{7,5},{8,10},{9,11},{10,... | collective-permute-start | bytes 786440 | tf_op jit(solution)/shard_map/ppermute | solution.py:177
  187.8 14.8 %collective-permute-start.70 = (f32[8,64,128]{2,1,0:T(8,128)}, f32[8,64,128]{2,1,0:T(8,128)S(1)}, u32[]{:S(2)}, u32[]{:S(2)}) collective-permute-start(f32[8,64,128]{2,1,0:T(8,128)} %get-tuple-element.309), channel_id=1, source_target_pairs={{0,1},{1,2},{2,3},{3,0},{4,5},{5,6},{6,7},{7,4},{8,9},{9,10},{10,1... | collective-permute-start | bytes 786440 | tf_op jit(solution)/shard_map/ppermute | solution.py:177
  200.9 28.2 %collective-permute-start.65 = (f32[8,64,128]{2,1,0:T(8,128)}, f32[8,64,128]{2,1,0:T(8,128)S(1)}, u32[]{:S(2)}, u32[]{:S(2)}) collective-permute-start(f32[8,64,128]{2,1,0:T(8,128)} %get-tuple-element.302), channel_id=1, source_target_pairs={{0,3},{1,0},{2,1},{3,2},{4,7},{5,4},{6,5},{7,6},{8,11},{9,8},{10,9... | collective-permute-start | bytes 786440 | tf_op jit(solution)/shard_map/ppermute | solution.py:177
  202.6 20.5 %collective-permute-start.61 = (f32[256,128]{1,0:T(8,128)}, f32[256,128]{1,0:T(8,128)S(1)}, u32[]{:S(2)}, u32[]{:S(2)}) collective-permute-start(f32[256,128]{1,0:T(8,128)} %get-tuple-element.298), channel_id=1, source_target_pairs={{0,16},{4,20},{8,24},{12,28},{16,0},{20,4},{24,8},{28,12},{1,17},{... | collective-permute-start | bytes 393224 | tf_op jit(solution)/shard_map/ppermute | solution.py:177
  205.1 20.8 %collective-permute-start.62 = (f32[256,128]{1,0:T(8,128)}, f32[256,128]{1,0:T(8,128)S(1)}, u32[]{:S(2)}, u32[]{:S(2)}) collective-permute-start(f32[256,128]{1,0:T(8,128)} %get-tuple-element.299), channel_id=1, source_target_pairs={{0,12},{4,16},{8,20},{12,24},{16,28},{20,0},{24,4},{28,8},{1,13},{... | collective-permute-start | bytes 393224 | tf_op jit(solution)/shard_map/ppermute | solution.py:177
  207.9 19.9 %collective-permute-start.63 = (f32[256,128]{1,0:T(8,128)}, f32[256,128]{1,0:T(8,128)S(1)}, u32[]{:S(2)}, u32[]{:S(2)}) collective-permute-start(f32[256,128]{1,0:T(8,128)} %get-tuple-element.300), channel_id=1, source_target_pairs={{0,8},{4,12},{8,16},{12,20},{16,24},{20,28},{24,0},{28,4},{1,9},{5... | collective-permute-start | bytes 393224 | tf_op jit(solution)/shard_map/ppermute | solution.py:177
  210.7 17.1 %collective-permute-start.64 = (f32[256,128]{1,0:T(8,128)}, f32[256,128]{1,0:T(8,128)S(1)}, u32[]{:S(2)}, u32[]{:S(2)}) collective-permute-start(f32[256,128]{1,0:T(8,128)} %get-tuple-element.301), channel_id=1, source_target_pairs={{0,4},{4,8},{8,12},{12,16},{16,20},{20,24},{24,28},{28,0},{1,5},{5... | collective-permute-start | bytes 393224 | tf_op jit(solution)/shard_map/ppermute | solution.py:177
  223.1 29.4 %collective-permute-start.71 = (f32[9,64,128]{2,1,0:T(8,128)}, f32[9,64,128]{2,1,0:T(8,128)S(1)}, u32[]{:S(2)}, u32[]{:S(2)}) collective-permute-start(f32[9,64,128]{2,1,0:T(8,128)} %get-tuple-element.315), channel_id=1, source_target_pairs={{0,3},{1,0},{2,1},{3,2},{4,7},{5,4},{6,5},{7,6},{8,11},{9,8},{10,9... | collective-permute-start | bytes 884744 | tf_op jit(solution)/shard_map/ppermute | solution.py:177
  225.9 26.6 %collective-permute-start.72 = (f32[9,64,128]{2,1,0:T(8,128)}, f32[9,64,128]{2,1,0:T(8,128)S(1)}, u32[]{:S(2)}, u32[]{:S(2)}) collective-permute-start(f32[9,64,128]{2,1,0:T(8,128)} %get-tuple-element.316), channel_id=1, source_target_pairs={{0,2},{1,3},{2,0},{3,1},{4,6},{5,7},{6,4},{7,5},{8,10},{9,11},{10,... | collective-permute-start | bytes 884744 | tf_op jit(solution)/shard_map/ppermute | solution.py:177
  227.7 24.7 %collective-permute-start.73 = (f32[9,64,128]{2,1,0:T(8,128)}, f32[9,64,128]{2,1,0:T(8,128)S(1)}, u32[]{:S(2)}, u32[]{:S(2)}) collective-permute-start(f32[9,64,128]{2,1,0:T(8,128)} %get-tuple-element.317), channel_id=1, source_target_pairs={{0,1},{1,2},{2,3},{3,0},{4,5},{5,6},{6,7},{7,4},{8,9},{9,10},{10,1... | collective-permute-start | bytes 884744 | tf_op jit(solution)/shard_map/ppermute | solution.py:177
  228.5 24.0 %collective-permute-start.66 = (f32[8,64,128]{2,1,0:T(8,128)}, f32[8,64,128]{2,1,0:T(8,128)S(1)}, u32[]{:S(2)}, u32[]{:S(2)}) collective-permute-start(f32[8,64,128]{2,1,0:T(8,128)} %get-tuple-element.303), channel_id=1, source_target_pairs={{0,2},{1,3},{2,0},{3,1},{4,6},{5,7},{6,4},{7,5},{8,10},{9,11},{10,... | collective-permute-start | bytes 786440 | tf_op jit(solution)/shard_map/ppermute | solution.py:177
  229.1 23.4 %collective-permute-start.67 = (f32[8,64,128]{2,1,0:T(8,128)}, f32[8,64,128]{2,1,0:T(8,128)S(1)}, u32[]{:S(2)}, u32[]{:S(2)}) collective-permute-start(f32[8,64,128]{2,1,0:T(8,128)} %get-tuple-element.304), channel_id=1, source_target_pairs={{0,1},{1,2},{2,3},{3,0},{4,5},{5,6},{6,7},{7,4},{8,9},{9,10},{10,1... | collective-permute-start | bytes 786440 | tf_op jit(solution)/shard_map/ppermute | solution.py:177
  (114 other events, 1985.9 us)

commit v2 on v1

--- a/solution.py
+++ b/solution.py
@@ -152,14 +152,36 @@
         return ry % (ROWS * gx) == 0 and ry // gx == ROWS and rx % gy == 0 and (rx // gy) % 2 == 0 and z % (2 * LANES) == 0 and rx % ROWS == 0
 
 
-def pack_x(plan, density, chunk, lanes):
+class Blocks:
+    def __init__(self, plan, stacked):
+        self.plan, self.stacked = plan, stacked
+        self.count = 1 if stacked else plan.gx
+
+    def shapes(self, *piece):
+        return [(self.plan.gx, *piece)] if self.stacked else [piece] * self.plan.gx
+
+    def views(self, refs):
+        return [refs[0].at[d] for d in range(self.plan.gx)] if self.stacked else list(refs)
+
+    def rows(self, t):
+        yc = self.plan.yc
+        return pl.ds(t * yc if self.stacked else slot("gx", t, self.plan.gx, yc), yc)
+
+    def shaped(self, arrays, *piece):
+        lead = (self.plan.gx,) if self.stacked else ()
+        return [a.reshape(*lead, *piece) for a in arrays]
+
+
+def pack_x(plan, density, chunk, lanes, stacked):
+    blocks = Blocks(plan, stacked)
+
     def kernel(n_ref, *outs):
-        for t, out in enumerate(outs):
-            rows = pl.ds(slot("gx", t, plan.gx, plan.yc), plan.yc)
-            out[...] = n_ref[:, rows, :].reshape(plan.rx * plan.yc, lanes)
+        for t, out in enumerate(blocks.views(outs)):
+            out[...] = n_ref[:, blocks.rows(t), :].reshape(plan.rx * plan.yc, lanes)
 
     spec = pl.BlockSpec((plan.rx, plan.ry, lanes), lambda s: (0, 0, chunk))
-    return call(kernel, [density], [(plan.rx * plan.yc, lanes)] * plan.gx, {0: spec}, flops=1 << 20)
+    outs = blocks.shapes(plan.rx * plan.yc, lanes)
+    return call(kernel, [density], outs, {0: spec}, flops=1 << 20)
 
 
 def pack_y(plan, density):
@@ -178,15 +200,31 @@
     return arrived
 
 
+def exchange(pieces, axis):
+    return [lax.all_to_all(pieces[0], axis, 0, 0, tiled=True)]
+
+
 def after(arrays, token):
     return lax.optimization_barrier((list(arrays), token))[0]
 
 
-def deriv_x(plan, matrix, pieces, lanes, with_energy):
-    gx, rx, yc = plan.gx, plan.rx, plan.yc
+def ordered_sum(pieces, axis, size, scratch):
+    for t, piece in enumerate(pieces):
+        scratch[pl.ds(slot(axis, t, size, ROWS), ROWS), :] = piece
+    total = scratch[:ROWS, :]
+    for t in range(1, size):
+        total = total + scratch[t * ROWS : (t + 1) * ROWS, :]
+    return total
+
+
+def deriv_x(plan, matrix, pieces, lanes, stacked, energy=None):
+    rx, yc = plan.rx, plan.yc
+    extra = 0 if energy is None else 1
+    blocks = Blocks(plan, stacked)
 
     def kernel(high_ref, low_ref, *refs):
-        ins, outs = refs[:gx], refs[gx : 2 * gx]
+        ins = blocks.views(refs[extra : extra + blocks.count])
+        outs = blocks.views(refs[extra + blocks.count :])
         high, low = high_ref[...], low_ref[...]
         for y in range(0, yc, 2):
             columns = [
@@ -199,30 +237,21 @@
                     out[pl.ds(y + k, rx, stride=yc), :] = result[
                         t * rx : (t + 1) * rx, k * lanes : (k + 1) * lanes
                     ]
-        if with_energy:
-            energy_ref, ordered = refs[2 * gx :]
-            for t, p in enumerate(ins):
-                ordered[pl.ds(slot("gx", t, gx, ROWS), ROWS), :] = p[rx * yc :, :]
-            total = ordered[:ROWS, :]
-            for t in range(1, gx):
-                total = total + ordered[t * ROWS : (t + 1) * ROWS, :]
-            energy_ref[...] = total
-
-    outs = [(rx * yc, lanes)] * gx
-    scratch = []
-    if with_energy:
-        outs = outs + [(ROWS, lanes)]
-        scratch = [pltpu.VMEM((gx * ROWS, lanes), jnp.float32)]
-    return call(kernel, [*matrix, *pieces], outs, scratch=scratch)
-
-
-def deriv_y(plan, matrix, pieces, lanes, energy=None):
+        if extra:
+            for out in outs:
+                out[rx * yc :, :] = refs[0][...]
+
+    outs = blocks.shapes((rx + extra) * yc, lanes)
+    ins = [*matrix] + ([energy] if extra else []) + list(pieces)
+    return call(kernel, ins, outs)
+
+
+def deriv_y(plan, matrix, pieces, lanes, with_energy=False):
     gy, sx, ry = plan.gy, plan.sx, plan.ry
     together = max(1, 2 * LANES // lanes)
-    extra = 0 if energy is None else 1
 
     def kernel(high_ref, low_ref, *refs):
-        ins, outs = refs[extra : extra + gy], refs[extra + gy :]
+        ins, outs = refs[:gy], refs[gy : 2 * gy]
         high, low = high_ref[...], low_ref[...]
         for x in range(0, sx, together):
             columns = [
@@ -233,13 +262,15 @@
             for k in range(together):
                 for t, out in enumerate(outs):
                     out[x + k] = result[t * ry : (t + 1) * ry, k * lanes : (k + 1) * lanes]
-        if extra:
-            for out in outs:
-                out[sx] = jnp.zeros((ry, lanes), jnp.float32)
-                out[sx, :ROWS, :] = refs[0][...]
-
-    ins = [*matrix] + ([energy] if extra else []) + list(pieces)
-    return call(kernel, ins, [(sx + extra, ry, lanes)] * gy)
+        if with_energy:
+            energy_ref, ordered = refs[2 * gy :]
+            energy_ref[...] = ordered_sum([p[sx, :ROWS, :] for p in ins], "gy", gy, ordered)
+
+    outs, scratch = [(sx, ry, lanes)] * gy, []
+    if with_energy:
+        outs = outs + [(ROWS, lanes)]
+        scratch = [pltpu.VMEM((gy * ROWS, lanes), jnp.float32)]
+    return call(kernel, [*matrix, *pieces], outs, scratch=scratch)
 
 
 def rows_call(kernel, rows, ins, widths, out_width, resident):
@@ -264,33 +295,37 @@
     return rows_call(kernel, rows, [flat], [plan.z], plan.z, matrix).reshape(field.shape)
 
 
-def less_deriv_z(plan, matrix, d_dens, flux):
-    def kernel(high_ref, low_ref, *refs):
-        count = len(flux)
-        dens = jnp.concatenate([r[...] for r in refs[:count]], axis=1)
-        field = jnp.concatenate([r[...] for r in refs[count : 2 * count]], axis=1)
-        refs[-1][...] = dens + times_matrix(field, high_ref[...], low_ref[...])
-
+def add_flux_z(plan, matrix, flux, chunk, lanes, terms):
     rows = plan.rx * plan.ry
-    flat = [a.reshape(rows, a.shape[2]) for a in (*d_dens, *flux)]
+    flat = [a.reshape(rows, -1) for a in (flux, *terms)]
+
+    def kernel(high_ref, low_ref, f_ref, *refs):
+        own = slice(chunk * lanes, (chunk + 1) * lanes)
+        total = times_matrix(f_ref[...], high_ref[own, :], low_ref[own, :])
+        if len(refs) > 1:
+            total = total + refs[0][...] + jnp.concatenate([r[...] for r in refs[1:-1]], axis=1)
+        refs[-1][...] = total
+
     widths = [a.shape[1] for a in flat]
     out = rows_call(kernel, rows, flat, widths, plan.z, matrix)
     return out.reshape(plan.rx, plan.ry, plan.z)
 
 
-def pointwise(plan, density, grad_z, grad_y, grad_x, chunk, lanes, before):
+def pointwise(plan, density, grad_z, grad_y, grad_x, chunk, lanes, stacked, before):
     gx, gy, rx, ry, yc, sx = plan.gx, plan.gy, plan.rx, plan.ry, plan.yc, plan.sx
     extra = 0 if before is None else 1
+    blocks = Blocks(plan, stacked)
 
     def kernel(*refs):
         n_ref, gz_ref = refs[0], refs[1]
         gy_refs = refs[2 : 2 + gy]
-        gx_refs = refs[2 + gy : 2 + gy + gx]
-        refs = refs[2 + gy + gx :]
+        gx_refs = blocks.views(refs[2 + gy : 2 + gy + blocks.count])
+        refs = refs[2 + gy + blocks.count :]
         if extra:
             before_ref, refs = refs[0], refs[1:]
-        fx_refs, fy_refs = refs[:gx], refs[gx : gx + gy]
-        fz_ref, dd_ref, energy_ref = refs[gx + gy :]
+        fx_refs, refs = blocks.views(refs[: blocks.count]), refs[blocks.count :]
+        fy_refs = refs[:gy]
+        fz_ref, dd_ref, energy_ref = refs[gy:]
         total = jnp.zeros((yc, lanes), jnp.float32)
         for part in range(gy):
             base = slot("gy", part, gy, sx)
@@ -298,7 +333,7 @@
             def step(inner, total, part=part, base=base):
                 x = base + inner
                 for t in range(gx):
-                    rows = pl.ds(slot("gx", t, gx, yc), yc)
+                    rows = blocks.rows(t)
                     n = n_ref[x, rows, :]
                     d_x = gx_refs[t][x]
                     d_y = gy_refs[part][inner, rows, :]
@@ -315,63 +350,78 @@
             total = lax.fori_loop(0, sx, step, total)
         if extra:
             total = total + before_ref[...]
-            for out in fx_refs:
-                out[rx] = total
+            for out in fy_refs:
+                out[sx] = jnp.zeros((ry, lanes), jnp.float32)
+                out[sx, :ROWS, :] = total
         energy_ref[...] = total
 
     block = pl.BlockSpec((rx, ry, lanes), lambda s: (0, 0, chunk))
     y_block = pl.BlockSpec((sx, ry, lanes), lambda s: (0, 0, chunk))
     specs = {0: block, 1: block} | {2 + t: y_block for t in range(gy)}
-    ins = [density, grad_z, *grad_y, *[p.reshape(rx, yc, lanes) for p in grad_x]]
+    ins = [density, grad_z, *grad_y, *blocks.shaped(grad_x, rx, yc, lanes)]
     if extra:
         ins.append(before)
-    outs = [(rx + extra, yc, lanes)] * gx + [(sx, ry, lanes)] * gy
+    outs = blocks.shapes(rx, yc, lanes) + [(sx + extra, ry, lanes)] * gy
     outs += [(rx, ry, lanes)] * 2 + [(yc, lanes)]
     out = call(kernel, ins, outs, specs, flops=1 << 32)
-    flux_x = [p.reshape((rx + extra) * yc, lanes) for p in out[:gx]]
-    return flux_x, out[gx : gx + gy], out[gx + gy], out[gx + gy + 1], out[gx + gy + 2]
-
-
-def finish(plan, base, div_x, div_y, lanes, cells):
-    gx, gy, rx, ry, yc, sx = plan.gx, plan.gy, plan.rx, plan.ry, plan.yc, plan.sx
-    chunks = len(div_x)
+    flux_x = blocks.shaped(out[: blocks.count], rx * yc, lanes)
+    return flux_x, out[blocks.count : blocks.count + gy], *out[blocks.count + gy :]
+
+
+def less_y(plan, base, div_y, lanes):
+    gy, rx, ry, sx = plan.gy, plan.rx, plan.ry, plan.sx
 
     def kernel(base_ref, *refs):
-        x_refs = [refs[c * gx : (c + 1) * gx] for c in range(chunks)]
-        refs = refs[chunks * gx :]
-        y_refs = [refs[c * gy : (c + 1) * gy] for c in range(chunks)]
-        out_ref, energy_ref, ordered = refs[chunks * gy :]
+        out_ref = refs[-1]
         for part in range(gy):
-            start = slot("gy", part, gy, sx)
-
-            def step(inner, carry, part=part, start=start):
-                x = start + inner
-                for c in range(chunks):
-                    where = slice(c * lanes, (c + 1) * lanes)
-                    for t in range(gx):
-                        rows = pl.ds(slot("gx", t, gx, yc), yc)
-                        out_ref[x, rows, where] = base_ref[x, rows, where] - (
-                            x_refs[c][t][x] + y_refs[c][part][inner, rows, :]
-                        )
-                return carry
-
-            lax.fori_loop(0, sx, step, 0)
-        for t, p in enumerate(y_refs[-1]):
-            ordered[pl.ds(slot("gy", t, gy, ROWS), ROWS), :] = p[sx, :ROWS, :]
-        total = ordered[:ROWS, :]
-        for t in range(1, gy):
-            total = total + ordered[t * ROWS : (t + 1) * ROWS, :]
-        energy_ref[...] = total
-
-    ins = [base]
-    for c in range(chunks):
-        ins += [p.reshape(rx, yc, lanes) for p in div_x[c]]
-    for c in range(chunks):
-        ins += list(div_y[c])
-    outs = [(rx, ry, plan.z), (ROWS, lanes)]
-    scratch = [pltpu.VMEM((gy * ROWS, lanes), jnp.float32)]
-    out, energy = call(kernel, ins, outs, scratch=scratch, flops=1 << 24)
-    return out, jnp.sum(energy) / float(cells)
+            rows = pl.ds(slot("gy", part, gy, sx), sx)
+            for c in range(len(div_y)):
+                where = slice(c * lanes, (c + 1) * lanes)
+                out_ref[rows, :, where] = base_ref[rows, :, where] - refs[c * gy + part][...]
+
+    ins = [base] + [p for pieces in div_y for p in pieces]
+    return call(kernel, ins, [(rx, ry, plan.z)], flops=1 << 24)[0]
+
+
+def finish(plan, base, div_x, chunk, lanes, stacked, before, scale):
+    gx, rx, ry, yc = plan.gx, plan.rx, plan.ry, plan.yc
+    last = scale is not None
+    blocks = Blocks(plan, stacked)
+
+    def kernel(base_ref, *refs):
+        x_refs, refs = blocks.views(refs[: blocks.count]), refs[blocks.count :]
+        out_ref = refs[1] if last else refs[0]
+        for t in range(gx):
+            rows = blocks.rows(t)
+            out_ref[:, rows, :] = base_ref[:, rows, :] - x_refs[t][:rx]
+        if last:
+            energy_ref, ordered = refs[2:]
+            total = ordered_sum([p[rx] for p in x_refs], "gx", gx, ordered)
+            energy_ref[0, 0] = jnp.sum(total) * scale
+
+    block = pl.BlockSpec((rx, ry, lanes), lambda s: (0, 0, chunk))
+    ins = [base, *blocks.shaped(div_x, rx + (1 if last else 0), yc, lanes)]
+    specs = [block] + [whole(a.shape) for a in ins[1:]]
+    out_shape = [jax.ShapeDtypeStruct((rx, ry, plan.z), jnp.float32)]
+    out_specs, scratch, aliases = [block], [], {}
+    if last:
+        aliases = {len(ins): 0}
+        ins.append(before)
+        specs.append(pl.BlockSpec(memory_space=pl.ANY))
+        out_shape.append(jax.ShapeDtypeStruct((1, 1), jnp.float32))
+        out_specs.append(pl.BlockSpec(memory_space=pltpu.SMEM))
+        scratch = [pltpu.VMEM((gx * ROWS, lanes), jnp.float32)]
+    return pl.pallas_call(
+        kernel,
+        grid=(1,),
+        in_specs=specs,
+        out_specs=out_specs,
+        out_shape=out_shape,
+        scratch_shapes=scratch,
+        input_output_aliases=aliases,
+        cost_estimate=pl.CostEstimate(flops=1 << 24, bytes_accessed=1 << 22, transcendentals=0),
+        name="finish",
+    )(*ins)
 
 
 def body(density):
@@ -383,50 +433,49 @@
     gx, gy = plan.gx, plan.gy
     count_x, count_y, count_z = plan.rx * gx, plan.ry * gy, plan.z
     matrix_x, matrix_y, matrix_z = split_matrix(count_x), split_matrix(count_y), split_matrix(count_z)
-    chunks = 2
-    lanes = plan.z // chunks
-
-    out = pack_x(plan, density, 0, lanes)
-    dens_x = [rotate(out, "gx", gx)]
+    lanes = plan.z // 2
+
+    out = pack_x(plan, density, 0, lanes, True)
+    dens_0 = exchange(out, "gx")
     out = pack_y(plan, *after([density], out[0]))
     dens_y = rotate(out, "gy", gy)
-    for c in range(1, chunks):
-        out = pack_x(plan, *after([density], out[0]), c, lanes)
-        dens_x.append(rotate(out, "gx", gx))
-    grad_z = deriv_z(plan, matrix_z, *after([density], out[0]))
-    out = deriv_y(plan, matrix_y, after(dens_y, grad_z), plan.z)
+    packed = pack_x(plan, *after([density], out[0]), 1, lanes, False)
+    grad_z = deriv_z(plan, matrix_z, *after([density], packed[0]))
+    dens_1 = rotate(after(packed, grad_z), "gx", gx)
+    out_x = deriv_x(plan, matrix_x, after(dens_0, grad_z), lanes, True)
+    grad_0 = exchange(out_x, "gx")
+    out = deriv_y(plan, matrix_y, after(dens_y, out_x[0]), plan.z)
     grad_y = rotate(out, "gy", gy)
-    grad_x = []
-    for c in range(chunks):
-        pieces = after(dens_x[c], out[0])
-        out = deriv_x(plan, matrix_x, pieces, lanes, False)
-        grad_x.append(rotate(out, "gx", gx))
-
-    token, energy = out[0], None
-    flux_x, flux_y, flux_z, d_dens = [], [], [], []
-    for c in range(chunks):
-        before = energy if c == chunks - 1 else None
-        pieces = after(grad_x[c], token)
-        f_x, f_y, f_z, dd, energy = pointwise(
-            plan, density, grad_z, grad_y, pieces, c, lanes, before
-        )
-        token = energy
-        flux_x.append(rotate(f_x, "gx", gx))
-        flux_y.append(rotate(f_y, "gy", gy))
-        flux_z.append(f_z)
-        d_dens.append(dd)
-    base = less_deriv_z(plan, matrix_z, d_dens, flux_z)
-    token = base
-    div_x, div_y = [], []
-    for c in range(chunks):
-        last = c == chunks - 1
-        out = deriv_x(plan, matrix_x, after(flux_x[c], token), lanes, last)
-        div_x.append(rotate(out[:gx], "gx", gx))
-        summed = out[gx] if last else None
-        out = deriv_y(plan, matrix_y, after(flux_y[c], out[0]), lanes, summed)
-        div_y.append(rotate(out, "gy", gy))
-        token = out[0]
-    return finish(plan, base, div_x, div_y, lanes, count_x * count_y * count_z)
+    out_x = deriv_x(plan, matrix_x, after(dens_1, out[0]), lanes, False)
+    grad_1 = rotate(out_x, "gx", gx)
+    grad_0 = after(grad_0, out_x[0])
+    f_x, f_y, f_z, part_0, energy = pointwise(
+        plan, density, grad_z, grad_y, grad_0, 0, lanes, True, None
+    )
+    flux_0 = exchange(f_x, "gx")
+    flux_y = [rotate(f_y, "gy", gy)]
+    base = add_flux_z(plan, matrix_z, *after([f_z], energy), 0, lanes, [])
+    grad_1 = after(grad_1, base)
+    f_x, f_y, f_z, part_1, energy = pointwise(
+        plan, density, grad_z, grad_y, grad_1, 1, lanes, False, energy
+    )
+    flux_1 = rotate(f_x, "gx", gx)
+    flux_y.append(rotate(f_y, "gy", gy))
+    terms = [base, part_0, part_1]
+    base = add_flux_z(plan, matrix_z, *after([f_z], energy), 1, lanes, terms)
+    out_x = deriv_x(plan, matrix_x, after(flux_0, base), lanes, True)
+    div_0 = exchange(out_x, "gx")
+    out = deriv_y(plan, matrix_y, after(flux_y[0], out_x[0]), lanes)
+    div_y = [rotate(out, "gy", gy)]
+    *out, energy = deriv_y(plan, matrix_y, after(flux_y[1], out[0]), lanes, True)
+    div_y.append(rotate(out, "gy", gy))
+    out_x = deriv_x(plan, matrix_x, after(flux_1, out[0]), lanes, False, energy)
+    div_1 = rotate(out_x, "gx", gx)
+    base = less_y(plan, *after([base], out_x[0]), div_y, lanes)
+    scale = 1.0 / float(count_x * count_y * count_z)
+    (half,) = finish(plan, base, div_0, 0, lanes, True, None, None)
+    done, energy = finish(plan, base, div_1, 1, lanes, False, half, scale)
+    return done, energy[0, 0]
 
 
 def xc_energy(electrons, grad_sq):

time: 263 us -> 301 us (1.14)
  waiting for transfers between devices: 84.7 us -> 120 us
  Pallas kernels: 65.3 us -> 73.1 us
  starting transfers between devices: 103 us -> 97.2 us
  local copies, waits for them, and re-layouts: 4.18 us -> 9.32 us
    ppermute x74 -> x46, starting transfers between devices: 103 us -> 79.9 us  [rotate(): arrived[size - t] = lax.ppermute(pieces[t], axis, pairs)]
    ppermute x74 -> x46, waiting for transfers between devices: 84.7 us -> 103 us  [rotate(): arrived[size - t] = lax.ppermute(pieces[t], axis, pairs)]
    all_to_all x0 -> x4, starting transfers between devices: none -> 17.3 us  [exchange(): return [lax.all_to_all(pieces[0], axis, 0, 0, tiled=True)]]
    all_to_all x0 -> x4, waiting for transfers between devices: none -> 16.6 us  [exchange(): return [lax.all_to_all(pieces[0], axis, 0, 0, tiled=True)]]
    pallas_call x0 -> x2, Pallas kernels: none -> 5.51 us  [finish(): pl.pallas_call(kernel, grid=(1,), in_specs=specs, out_specs=out_specs, ou...]
    unnamed x176 -> x122, local copies, waits for them, and re-layouts: 4.18 us -> 9.32 us
    pallas_call x2 -> x3, Pallas kernels: 9.81 us -> 14 us  [rows_call(): pl.pallas_call(kernel, grid=(4,), in_specs=[pl.BlockSpec(m.shape, lambda...]
  transfers between devices with their start and end apart: 74 -> 50, of which waited for: 23 -> 19; matrix products, arithmetic and copies ran while one was open for 0% -> 0% of each run, Pallas kernels for 21% -> 17%
where the time goes in v2:
time: 301 us; the launch traced here: 300 us
  waiting for transfers between devices  120 us (40%)
  starting transfers between devices  97.2 us (32%)
  Pallas kernels  73.1 us (24%)
  local copies, waits for them, and re-layouts  9.32 us (3%)
    ppermute x46, waiting for transfers between devices, rotate(): arrived[size - t] = lax.ppermute(pieces[t], axis, pairs)  103 us
    ppermute x46, starting transfers between devices, rotate(): arrived[size - t] = lax.ppermute(pieces[t], axis, pairs)  79.9 us
    pallas_call x13, Pallas kernels, call(): pl.pallas_call(kernel, grid=(1,), in_specs=specs, out_specs=[whole(o) for...  53.6 us
    all_to_all x4, starting transfers between devices, exchange(): return [lax.all_to_all(pieces[0], axis, 0, 0, tiled=True)]  17.3 us
    all_to_all x4, waiting for transfers between devices, exchange(): return [lax.all_to_all(pieces[0], axis, 0, 0, tiled=True)]  16.6 us
    pallas_call x3, Pallas kernels, rows_call(): pl.pallas_call(kernel, grid=(4,), in_specs=[pl.BlockSpec(m.shape, lambda...  14 us
    unnamed x122, local copies, waits for them, and re-layouts  9.32 us
  transfers between devices with their start and end apart: 50, of which 19 were waited for; matrix products, arithmetic and copies ran while one was open for 0% of the time, Pallas kernels for 17%

profile of v2, /device:TPU:0, one launch (start us, length us, event | category | flops | bytes accessed | tf_op | source)
XLA Modules:
  0.0 300.4 jit_solution(16471553759821016021)
XLA Ops:
  2.9 6.4 %all-to-all-start = ((f32[8,256,128]{2,1,0:T(8,128)}), f32[8,256,128]{2,1,0:T(8,128)S(1)}, u32[]{:S(2)}, u32[]{:S(2)}) async-start(f32[8,256,128]{2,1,0:T(8,128)} %shard_map.86), calls=%async_computation | async-start | bytes 2097152 | tf_op jit(solution)/shard_map/all_to_all | solution.py:204
  9.3 3.1 %shard_map.87 = (f32[8,64,256]{2,1,0:T(8,128)}, f32[8,64,256]{2,1,0:T(8,128)}, f32[8,64,256]{2,1,0:T(8,128)}, f32[8,64,256]{2,1,0:T(8,128)}) custom-call(f32[32,64,256]{2,1,0:T(8,128)} %refs_0_.3), custom_call_target="tpu_custom_call" | custom-call | flops 1048576 | bytes 4194304 | tf_op jit(solution)/shard_map/pallas_call | solution.py:127
  14.7 4.5 %shard_map.89 = f32[2048,256]{1,0:T(8,128)} custom-call(bf16[256,256]{1,0:T(8,128)(2,1)} %constant.4.clone.high_ref, bf16[256,256]{1,0:T(8,128)(2,1)} %constant.5.clone.low_ref, f32[2048,256]{1,0:T(8,128)} %bitcast.35), custom_call_target="tpu_custom_call" | custom-call | flops 268435456 | bytes 4194304 | tf_op jit(solution)/shard_map/pallas_call | solution.py:278
  19.2 16.6 %all-to-all-done.refs_0_ = f32[8,256,128]{2,1,0:T(8,128)S(1)} async-done(((f32[8,256,128]{2,1,0:T(8,128)}), f32[8,256,128]{2,1,0:T(8,128)S(1)}, u32[]{:S(2)}, u32[]{:S(2)}) %all-to-all-start) | async-done | bytes 1048608 | tf_op jit(solution)/shard_map/all_to_all | solution.py:204
  36.8 3.1 %shard_map.90 = f32[8,256,128]{2,1,0:T(8,128)} custom-call(bf16[256,256]{1,0:T(8,128)(2,1)} %constant.4.clone.high_ref, bf16[256,256]{1,0:T(8,128)(2,1)} %constant.5.clone.low_ref, f32[8,256,128]{2,1,0:T(8,128)} %copy-done.2), custom_call_target="tpu_custom_call" | custom-call | flops 268435456 | bytes 2621440 | tf_op jit(solution)/shard_map/pallas_call | solution.py:127
  39.9 3.7 %all-to-all-start.1 = ((f32[8,256,128]{2,1,0:T(8,128)}), f32[8,256,128]{2,1,0:T(8,128)S(1)}, u32[]{:S(2)}, u32[]{:S(2)}) async-start(f32[8,256,128]{2,1,0:T(8,128)} %shard_map.90), calls=%async_computation.1 | async-start | bytes 2097152 | tf_op jit(solution)/shard_map/all_to_all | solution.py:204
  43.6 2.5 collective-permute-start
  47.2 2.6 collective-permute-start.6
  49.8 9.0 %collective-permute-done.refs_1_ = f32[8,64,256]{2,1,0:T(8,128)S(1)} collective-permute-done((f32[8,64,256]{2,1,0:T(8,128)}, f32[8,64,256]{2,1,0:T(8,128)S(1)}, u32[]{:S(2)}, u32[]{:S(2)}) %collective-permute-start) | collective-permute-done | bytes 524320 | tf_op jit(solution)/shard_map/ppermute | solution.py:199
  58.8 12.7 %collective-permute-done.1.refs_2_ = f32[8,64,256]{2,1,0:T(8,128)S(1)} collective-permute-done((f32[8,64,256]{2,1,0:T(8,128)}, f32[8,64,256]{2,1,0:T(8,128)S(1)}, u32[]{:S(2)}, u32[]{:S(2)}) %collective-permute-start.1) | collective-permute-done | bytes 524320 | tf_op jit(solution)/shard_map/ppermute | solution.py:199
  73.1 3.9 %shard_map.91 = (f32[8,64,256]{2,1,0:T(8,128)}, f32[8,64,256]{2,1,0:T(8,128)}, f32[8,64,256]{2,1,0:T(8,128)}, f32[8,64,256]{2,1,0:T(8,128)}) custom-call(bf16[256,256]{1,0:T(8,128)(2,1)} %constant.4.clone.high_ref, bf16[256,256]{1,0:T(8,128)(2,1)} %constant.5.clone.low_ref, f32[8,64,256]{2,1,0:T(8,128)} %get-tuple-element.128.refs_0_, ...), custom_call_target="tpu_custom_call" | custom-call | flops 268435456 | bytes 4718592 | tf_op jit(solution)/shard_map/pallas_call | solution.py:127
  79.5 3.5 %collective-permute-start.7 = (f32[256,128]{1,0:T(8,128)}, f32[256,128]{1,0:T(8,128)S(1)}, u32[]{:S(2)}, u32[]{:S(2)}) collective-permute-start(f32[256,128]{1,0:T(8,128)} %get-tuple-element.145), channel_id=1, source_target_pairs={{0,24},{4,28},{8,0},{12,4},{16,8},{20,12},{24,16},{28,20},{1,25},{... | collective-permute-start | bytes 393224 | tf_op jit(solution)/shard_map/ppermute | solution.py:199
  83.0 4.2 %collective-permute-done.7.refs_2_ = f32[256,128]{1,0:T(8,128)S(1)} collective-permute-done((f32[256,128]{1,0:T(8,128)}, f32[256,128]{1,0:T(8,128)S(1)}, u32[]{:S(2)}, u32[]{:S(2)}) %collective-permute-start.7) | collective-permute-done | bytes 131104 | tf_op jit(solution)/shard_map/ppermute | solution.py:199
  90.8 6.8 %collective-permute-done.9.refs_4_ = f32[256,128]{1,0:T(8,128)S(1)} collective-permute-done((f32[256,128]{1,0:T(8,128)}, f32[256,128]{1,0:T(8,128)S(1)}, u32[]{:S(2)}, u32[]{:S(2)}) %collective-permute-start.9) | collective-permute-done | bytes 131104 | tf_op jit(solution)/shard_map/ppermute | solution.py:199
  97.7 3.4 %collective-permute-done.10.refs_5_ = f32[256,128]{1,0:T(8,128)S(1)} collective-permute-done((f32[256,128]{1,0:T(8,128)}, f32[256,128]{1,0:T(8,128)S(1)}, u32[]{:S(2)}, u32[]{:S(2)}) %collective-permute-start.10) | collective-permute-done | bytes 131104 | tf_op jit(solution)/shard_map/ppermute | solution.py:199
  101.1 3.3 %collective-permute-done.11.refs_6_ = f32[256,128]{1,0:T(8,128)S(1)} collective-permute-done((f32[256,128]{1,0:T(8,128)S(1)}, f32[256,128]{1,0:T(8,128)S(1)}, u32[]{:S(2)}, u32[]{:S(2)}) %collective-permute-start.11) | collective-permute-done | bytes 131104 | tf_op jit(solution)/shard_map/ppermute | solution.py:199
  104.4 2.9 collective-permute-done.12.refs_7_
  107.9 3.0 shard_map.92
  112.3 10.1 %shard_map.93 = (f32[8,32,8,128]{3,2,1,0:T(8,128)}, f32[8,64,128]{2,1,0:T(8,128)}, f32[8,64,128]{2,1,0:T(8,128)}, f32[8,64,128]{2,1,0:T(8,128)}, f32[8,64,128]{2...) custom-call(f32[32,64,256]{2,1,0:T(8,128)} %refs_0_.3, f32[32,64,256]{2,1,0:T(8,128)} %bitcast.38, ...), custom_call_target="tpu_custom_call" | custom-call | flops 4294967296 | bytes 11538432 | tf_op jit(solution)/shard_map/pallas_call | solution.py:127
  122.4 3.7 %all-to-all-start.2 = ((f32[8,256,128]{2,1,0:T(8,128)}), f32[8,256,128]{2,1,0:T(8,128)S(1)}, u32[]{:S(2)}, u32[]{:S(2)}) async-start(f32[8,256,128]{2,1,0:T(8,128)} %bitcast.41), calls=%async_computation.2 | async-start | bytes 2097152 | tf_op jit(solution)/shard_map/all_to_all | solution.py:204
  126.1 3.5 %collective-permute-start.13 = (f32[256,128]{1,0:T(8,128)S(1)}, f32[256,128]{1,0:T(8,128)S(1)}, u32[]{:S(2)}, u32[]{:S(2)}) collective-permute-start(f32[256,128]{1,0:T(8,128)S(1)} %copy-done.55), channel_id=1, source_target_pairs={{0,28},{4,0},{8,4},{12,8},{16,12},{20,16},{24,20},{28,24},{1,29},{... | collective-permute-start | bytes 393224 | tf_op jit(solution)/shard_map/ppermute | solution.py:199
  130.2 2.5 collective-permute-start.16
  132.7 14.5 %collective-permute-done.13 = f32[256,128]{1,0:T(8,128)S(1)} collective-permute-done((f32[256,128]{1,0:T(8,128)S(1)}, f32[256,128]{1,0:T(8,128)S(1)}, u32[]{:S(2)}, u32[]{:S(2)}) %collective-permute-start.13) | collective-permute-done | bytes 131104 | tf_op jit(solution)/shard_map/ppermute | solution.py:199
  147.1 2.8 collective-permute-done.14
  149.9 17.8 %collective-permute-start.19 = (f32[256,128]{1,0:T(8,128)S(1)}, f32[256,128]{1,0:T(8,128)S(1)}, u32[]{:S(2)}, u32[]{:S(2)}) collective-permute-start(f32[256,128]{1,0:T(8,128)S(1)} %copy-done.46), channel_id=1, source_target_pairs={{0,4},{4,8},{8,12},{12,16},{16,20},{20,24},{24,28},{28,0},{1,5},{5... | collective-permute-start | bytes 393224 | tf_op jit(solution)/shard_map/ppermute | solution.py:199
  167.7 7.4 %collective-permute-done.16 = f32[256,128]{1,0:T(8,128)S(1)} collective-permute-done((f32[256,128]{1,0:T(8,128)S(1)}, f32[256,128]{1,0:T(8,128)S(1)}, u32[]{:S(2)}, u32[]{:S(2)}) %collective-permute-start.16) | collective-permute-done | bytes 131104 | tf_op jit(solution)/shard_map/ppermute | solution.py:199
  175.9 10.1 %shard_map.94 = (f32[32,8,128]{2,1,0:T(8,128)}, f32[32,8,128]{2,1,0:T(8,128)}, f32[32,8,128]{2,1,0:T(8,128)}, f32[32,8,128]{2,1,0:T(8,128)}, f32[32,8,128]{2,1,0...) custom-call(f32[32,64,256]{2,1,0:T(8,128)} %refs_0_.3, ...), custom_call_target="tpu_custom_call" | custom-call | flops 4294967296 | bytes 11673600 | tf_op jit(solution)/shard_map/pallas_call | solution.py:127
  186.0 4.3 %shard_map.95.refs_0_ = f32[2048,256]{1,0:T(8,128)} custom-call(bf16[256,256]{1,0:T(8,128)(2,1)} %constant.4.clone.high_ref, bf16[256,256]{1,0:T(8,128)(2,1)} %constant.5.clone.low_ref, f32[2048,128]{1,0:T(8,128)} %bitcast.42), custom_call_target="tpu_custom_call" | custom-call | flops 268435456 | bytes 4194304 | tf_op jit(solution)/shard_map/pallas_call | solution.py:278
  190.3 5.2 %shard_map.96 = f32[2048,256]{1,0:T(8,128)} custom-call(bf16[256,256]{1,0:T(8,128)(2,1)} %constant.4.clone.high_ref, bf16[256,256]{1,0:T(8,128)(2,1)} %constant.5.clone.low_ref, f32[2048,128]{1,0:T(8,128)} %bitcast.44, f32[2048,256]{1,0:T(8,128)} %shard_map.95.refs_0_, f32[2048,128]{1,0:T(8,128)} %bitcast.43, f32[2048,128]{1,0:T(8,128)} %bitcast.45), custom_call_target="tpu_custom_call" | custom-call | flops 268435456 | bytes 4194304 | tf_op jit(solution)/shard_map/pallas_call | solution.py:278
  196.5 3.1 %shard_map.97 = f32[8,256,128]{2,1,0:T(8,128)} custom-call(bf16[256,256]{1,0:T(8,128)(2,1)} %constant.4.clone.high_ref, bf16[256,256]{1,0:T(8,128)(2,1)} %constant.5.clone.low_ref, f32[8,256,128]{2,1,0:T(8,128)} %copy-done.1), custom_call_target="tpu_custom_call" | custom-call | flops 268435456 | bytes 2621440 | tf_op jit(solution)/shard_map/pallas_call | solution.py:127
  199.7 3.6 %all-to-all-start.3 = ((f32[8,256,128]{2,1,0:T(8,128)}), f32[8,256,128]{2,1,0:T(8,128)S(1)}, u32[]{:S(2)}, u32[]{:S(2)}) async-start(f32[8,256,128]{2,1,0:T(8,128)} %shard_map.97), calls=%async_computation.3 | async-start | bytes 2097152 | tf_op jit(solution)/shard_map/all_to_all | solution.py:204
  203.3 3.5 %collective-permute-start.26 = (f32[256,128]{1,0:T(8,128)S(1)}, f32[256,128]{1,0:T(8,128)S(1)}, u32[]{:S(2)}, u32[]{:S(2)}) collective-permute-start(f32[256,128]{1,0:T(8,128)S(1)} %bitcast.65), channel_id=1, source_target_pairs={{0,28},{4,0},{8,4},{12,8},{16,12},{20,16},{24,20},{28,24},{1,29},{... | collective-permute-start | bytes 393224 | tf_op jit(solution)/shard_map/ppermute | solution.py:199
  211.2 11.3 %collective-permute-done.26.refs_2_ = f32[256,128]{1,0:T(8,128)S(1)} collective-permute-done((f32[256,128]{1,0:T(8,128)S(1)}, f32[256,128]{1,0:T(8,128)S(1)}, u32[]{:S(2)}, u32[]{:S(2)}) %collective-permute-start.26) | collective-permute-done | bytes 131104 | tf_op jit(solution)/shard_map/ppermute | solution.py:199
  224.1 3.5 %collective-permute-start.27 = (f32[256,128]{1,0:T(8,128)}, f32[256,128]{1,0:T(8,128)S(1)}, u32[]{:S(2)}, u32[]{:S(2)}) collective-permute-start(f32[256,128]{1,0:T(8,128)} %bitcast.60), channel_id=1, source_target_pairs={{0,24},{4,28},{8,0},{12,4},{16,8},{20,12},{24,16},{28,20},{1,25},{... | collective-permute-start | bytes 393224 | tf_op jit(solution)/shard_map/ppermute | solution.py:199
  227.7 6.0 %collective-permute-start.28 = (f32[256,128]{1,0:T(8,128)}, f32[256,128]{1,0:T(8,128)S(1)}, u32[]{:S(2)}, u32[]{:S(2)}) collective-permute-start(f32[256,128]{1,0:T(8,128)} %bitcast.58), channel_id=1, source_target_pairs={{0,20},{4,24},{8,28},{12,0},{16,4},{20,8},{24,12},{28,16},{1,21},{... | collective-permute-start | bytes 393224 | tf_op jit(solution)/shard_map/ppermute | solution.py:199
  233.7 4.7 %collective-permute-start.29 = (f32[256,128]{1,0:T(8,128)}, f32[256,128]{1,0:T(8,128)S(1)}, u32[]{:S(2)}, u32[]{:S(2)}) collective-permute-start(f32[256,128]{1,0:T(8,128)} %bitcast.57), channel_id=1, source_target_pairs={{0,16},{4,20},{8,24},{12,28},{16,0},{20,4},{24,8},{28,12},{1,17},{... | collective-permute-start | bytes 393224 | tf_op jit(solution)/shard_map/ppermute | solution.py:199
  240.5 2.9 shard_map.98
  243.4 2.9 shard_map.99
  248.2 4.6 %collective-permute-done.29.refs_5_ = f32[256,128]{1,0:T(8,128)S(1)} collective-permute-done((f32[256,128]{1,0:T(8,128)}, f32[256,128]{1,0:T(8,128)S(1)}, u32[]{:S(2)}, u32[]{:S(2)}) %collective-permute-start.29) | collective-permute-done | bytes 131104 | tf_op jit(solution)/shard_map/ppermute | solution.py:199
  255.8 3.0 shard_map.100
  260.1 2.9 collective-permute-start.38
  263.1 2.7 collective-permute-start.33
  266.3 2.4 collective-permute-start.35
  268.7 7.2 %collective-permute-done.37.refs_6_ = f32[8,64,128]{2,1,0:T(8,128)S(1)} collective-permute-done((f32[8,64,128]{2,1,0:T(8,128)}, f32[8,64,128]{2,1,0:T(8,128)S(1)}, u32[]{:S(2)}, u32[]{:S(2)}) %collective-permute-start.37) | collective-permute-done | bytes 262176 | tf_op jit(solution)/shard_map/ppermute | solution.py:199
  277.8 6.8 %collective-permute-done.34.refs_2_ = f32[8,64,128]{2,1,0:T(8,128)S(1)} collective-permute-done((f32[8,64,128]{2,1,0:T(8,128)}, f32[8,64,128]{2,1,0:T(8,128)S(1)}, u32[]{:S(2)}, u32[]{:S(2)}) %collective-permute-start.34) | collective-permute-done | bytes 262176 | tf_op jit(solution)/shard_map/ppermute | solution.py:199
  287.1 3.7 %shard_map.101.base_ref = f32[32,64,256]{2,1,0:T(8,128)} custom-call(f32[32,64,256]{2,1,0:T(8,128)} %bitcast.36, f32[8,64,128]{2,1,0:T(8,128)} %get-tuple-element.196.refs_0_, f32[8,64,128]{2,1,0:T(8,128)} %copy-done.16, f32[8,64,128]{2,1,0:T(8,128)} %copy-done.17, f32[8,64,128]{2,1,0:T(8,128)} %copy-done.18, f32[8,64,128]{2,1,0:T(8,128)} %get-tuple-element.210.refs_4_, ...), custom_call_target="tpu_custom_call" | custom-call | flops 16777216 | bytes 6291456 | tf_op jit(solution)/shard_map/pallas_call | solution.py:127
  291.8 2.7 finish.2.refs_8_
  297.6 2.8 finish.3
  (192 shorter events, 42.0 us)
Async XLA Ops:
  2.9 32.9 %all-to-all-start = ((f32[8,256,128]{2,1,0:T(8,128)}), f32[8,256,128]{2,1,0:T(8,128)S(1)}, u32[]{:S(2)}, u32[]{:S(2)}) async-start(f32[8,256,128]{2,1,0:T(8,128)} %shard_map.86), calls=%async_computation | async-start | bytes 2097152 | tf_op jit(solution)/shard_map/all_to_all | solution.py:204
  39.9 71.0 %all-to-all-start.1 = ((f32[8,256,128]{2,1,0:T(8,128)}), f32[8,256,128]{2,1,0:T(8,128)S(1)}, u32[]{:S(2)}, u32[]{:S(2)}) async-start(f32[8,256,128]{2,1,0:T(8,128)} %shard_map.90), calls=%async_computation.1 | async-start | bytes 2097152 | tf_op jit(solution)/shard_map/all_to_all | solution.py:204
  43.6 15.2 %collective-permute-start = (f32[8,64,256]{2,1,0:T(8,128)}, f32[8,64,256]{2,1,0:T(8,128)S(1)}, u32[]{:S(2)}, u32[]{:S(2)}) collective-permute-start(f32[8,64,256]{2,1,0:T(8,128)} %get-tuple-element.124), channel_id=1, source_target_pairs={{0,3},{1,0},{2,1},{3,2},{4,7},{5,4},{6,5},{7,6},{8,11},{9,8},{10,9... | collective-permute-start | bytes 1572872 | tf_op jit(solution)/shard_map/ppermute | solution.py:199
  46.1 25.3 %collective-permute-start.1 = (f32[8,64,256]{2,1,0:T(8,128)}, f32[8,64,256]{2,1,0:T(8,128)S(1)}, u32[]{:S(2)}, u32[]{:S(2)}) collective-permute-start(f32[8,64,256]{2,1,0:T(8,128)} %get-tuple-element.125), channel_id=1, source_target_pairs={{0,2},{1,3},{2,0},{3,1},{4,6},{5,7},{6,4},{7,5},{8,10},{9,11},{10,... | collective-permute-start | bytes 1572872 | tf_op jit(solution)/shard_map/ppermute | solution.py:199
  46.6 24.8 %collective-permute-start.2 = (f32[8,64,256]{2,1,0:T(8,128)S(1)}, f32[8,64,256]{2,1,0:T(8,128)S(1)}, u32[]{:S(2)}, u32[]{:S(2)}) collective-permute-start(f32[8,64,256]{2,1,0:T(8,128)S(1)} %copy-done.40), channel_id=1, source_target_pairs={{0,1},{1,2},{2,3},{3,0},{4,5},{5,6},{6,7},{7,4},{8,9},{9,10},{10,1... | collective-permute-start | bytes 1572872 | tf_op jit(solution)/shard_map/ppermute | solution.py:199
  47.2 35.8 %collective-permute-start.6 = (f32[256,128]{1,0:T(8,128)}, f32[256,128]{1,0:T(8,128)S(1)}, u32[]{:S(2)}, u32[]{:S(2)}) collective-permute-start(f32[256,128]{1,0:T(8,128)} %get-tuple-element.144), channel_id=1, source_target_pairs={{0,28},{4,0},{8,4},{12,8},{16,12},{20,16},{24,20},{28,24},{1,29},{... | collective-permute-start | bytes 393224 | tf_op jit(solution)/shard_map/ppermute | solution.py:199
  77.0 34.0 %collective-permute-start.3 = (f32[8,64,256]{2,1,0:T(8,128)}, f32[8,64,256]{2,1,0:T(8,128)S(1)}, u32[]{:S(2)}, u32[]{:S(2)}) collective-permute-start(f32[8,64,256]{2,1,0:T(8,128)} %get-tuple-element.133), channel_id=1, source_target_pairs={{0,3},{1,0},{2,1},{3,2},{4,7},{5,4},{6,5},{7,6},{8,11},{9,8},{10,9... | collective-permute-start | bytes 1572872 | tf_op jit(solution)/shard_map/ppermute | solution.py:199
  77.5 33.5 %collective-permute-start.4 = (f32[8,64,256]{2,1,0:T(8,128)}, f32[8,64,256]{2,1,0:T(8,128)S(1)}, u32[]{:S(2)}, u32[]{:S(2)}) collective-permute-start(f32[8,64,256]{2,1,0:T(8,128)} %get-tuple-element.134), channel_id=1, source_target_pairs={{0,2},{1,3},{2,0},{3,1},{4,6},{5,7},{6,4},{7,5},{8,10},{9,11},{10,... | collective-permute-start | bytes 1572872 | tf_op jit(solution)/shard_map/ppermute | solution.py:199
  78.0 33.0 %collective-permute-start.5 = (f32[8,64,256]{2,1,0:T(8,128)}, f32[8,64,256]{2,1,0:T(8,128)}, u32[]{:S(2)}, u32[]{:S(2)}) collective-permute-start(f32[8,64,256]{2,1,0:T(8,128)} %get-tuple-element.135), channel_id=1, source_target_pairs={{0,1},{1,2},{2,3},{3,0},{4,5},{5,6},{6,7},{7,4},{8,9},{9,10},{10,1... | collective-permute-start | bytes 1572872 | tf_op jit(solution)/shard_map/ppermute | solution.py:199
  79.5 7.7 %collective-permute-start.7 = (f32[256,128]{1,0:T(8,128)}, f32[256,128]{1,0:T(8,128)S(1)}, u32[]{:S(2)}, u32[]{:S(2)}) collective-permute-start(f32[256,128]{1,0:T(8,128)} %get-tuple-element.145), channel_id=1, source_target_pairs={{0,24},{4,28},{8,0},{12,4},{16,8},{20,12},{24,16},{28,20},{1,25},{... | collective-permute-start | bytes 393224 | tf_op jit(solution)/shard_map/ppermute | solution.py:199
  83.0 7.0 %collective-permute-start.8 = (f32[256,128]{1,0:T(8,128)}, f32[256,128]{1,0:T(8,128)S(1)}, u32[]{:S(2)}, u32[]{:S(2)}) collective-permute-start(f32[256,128]{1,0:T(8,128)} %get-tuple-element.146), channel_id=1, source_target_pairs={{0,20},{4,24},{8,28},{12,0},{16,4},{20,8},{24,12},{28,16},{1,21},{... | collective-permute-start | bytes 393224 | tf_op jit(solution)/shard_map/ppermute | solution.py:199
  87.2 10.4 %collective-permute-start.9 = (f32[256,128]{1,0:T(8,128)}, f32[256,128]{1,0:T(8,128)S(1)}, u32[]{:S(2)}, u32[]{:S(2)}) collective-permute-start(f32[256,128]{1,0:T(8,128)} %get-tuple-element.147), channel_id=1, source_target_pairs={{0,16},{4,20},{8,24},{12,28},{16,0},{20,4},{24,8},{28,12},{1,17},{... | collective-permute-start | bytes 393224 | tf_op jit(solution)/shard_map/ppermute | solution.py:199
  90.0 11.1 %collective-permute-start.10 = (f32[256,128]{1,0:T(8,128)}, f32[256,128]{1,0:T(8,128)S(1)}, u32[]{:S(2)}, u32[]{:S(2)}) collective-permute-start(f32[256,128]{1,0:T(8,128)} %get-tuple-element.148), channel_id=1, source_target_pairs={{0,12},{4,16},{8,20},{12,24},{16,28},{20,0},{24,4},{28,8},{1,13},{... | collective-permute-start | bytes 393224 | tf_op jit(solution)/shard_map/ppermute | solution.py:199
  97.6 6.8 %collective-permute-start.11 = (f32[256,128]{1,0:T(8,128)S(1)}, f32[256,128]{1,0:T(8,128)S(1)}, u32[]{:S(2)}, u32[]{:S(2)}) collective-permute-start(f32[256,128]{1,0:T(8,128)S(1)} %copy-done.45), channel_id=1, source_target_pairs={{0,8},{4,12},{8,16},{12,20},{16,24},{20,28},{24,0},{28,4},{1,9},{5... | collective-permute-start | bytes 393224 | tf_op jit(solution)/shard_map/ppermute | solution.py:199
  122.4 73.1 %all-to-all-start.2 = ((f32[8,256,128]{2,1,0:T(8,128)}), f32[8,256,128]{2,1,0:T(8,128)S(1)}, u32[]{:S(2)}, u32[]{:S(2)}) async-start(f32[8,256,128]{2,1,0:T(8,128)} %bitcast.41), calls=%async_computation.2 | async-start | bytes 2097152 | tf_op jit(solution)/shard_map/all_to_all | solution.py:204
  126.1 21.0 %collective-permute-start.13 = (f32[256,128]{1,0:T(8,128)S(1)}, f32[256,128]{1,0:T(8,128)S(1)}, u32[]{:S(2)}, u32[]{:S(2)}) collective-permute-start(f32[256,128]{1,0:T(8,128)S(1)} %copy-done.55), channel_id=1, source_target_pairs={{0,28},{4,0},{8,4},{12,8},{16,12},{20,16},{24,20},{28,24},{1,29},{... | collective-permute-start | bytes 393224 | tf_op jit(solution)/shard_map/ppermute | solution.py:199
  129.6 20.3 %collective-permute-start.14 = (f32[256,128]{1,0:T(8,128)S(1)}, f32[256,128]{1,0:T(8,128)S(1)}, u32[]{:S(2)}, u32[]{:S(2)}) collective-permute-start(f32[256,128]{1,0:T(8,128)S(1)} %copy-done.52), channel_id=1, source_target_pairs={{0,24},{4,28},{8,0},{12,4},{16,8},{20,12},{24,16},{28,20},{1,25},{... | collective-permute-start | bytes 393224 | tf_op jit(solution)/shard_map/ppermute | solution.py:199
  130.2 37.5 %collective-permute-start.15 = (f32[256,128]{1,0:T(8,128)S(1)}, f32[256,128]{1,0:T(8,128)S(1)}, u32[]{:S(2)}, u32[]{:S(2)}) collective-permute-start(f32[256,128]{1,0:T(8,128)S(1)} %copy-done.50), channel_id=1, source_target_pairs={{0,20},{4,24},{8,28},{12,0},{16,4},{20,8},{24,12},{28,16},{1,21},{... | collective-permute-start | bytes 393224 | tf_op jit(solution)/shard_map/ppermute | solution.py:199
  130.2 44.9 %collective-permute-start.16 = (f32[256,128]{1,0:T(8,128)S(1)}, f32[256,128]{1,0:T(8,128)S(1)}, u32[]{:S(2)}, u32[]{:S(2)}) collective-permute-start(f32[256,128]{1,0:T(8,128)S(1)} %copy-done.49), channel_id=1, source_target_pairs={{0,16},{4,20},{8,24},{12,28},{16,0},{20,4},{24,8},{28,12},{1,17},{... | collective-permute-start | bytes 393224 | tf_op jit(solution)/shard_map/ppermute | solution.py:199
  132.7 42.4 %collective-permute-start.17 = (f32[256,128]{1,0:T(8,128)S(1)}, f32[256,128]{1,0:T(8,128)S(1)}, u32[]{:S(2)}, u32[]{:S(2)}) collective-permute-start(f32[256,128]{1,0:T(8,128)S(1)} %copy-done.48), channel_id=1, source_target_pairs={{0,12},{4,16},{8,20},{12,24},{16,28},{20,0},{24,4},{28,8},{1,13},{... | collective-permute-start | bytes 393224 | tf_op jit(solution)/shard_map/ppermute | solution.py:199
  147.1 28.0 %collective-permute-start.18 = (f32[256,128]{1,0:T(8,128)S(1)}, f32[256,128]{1,0:T(8,128)S(1)}, u32[]{:S(2)}, u32[]{:S(2)}) collective-permute-start(f32[256,128]{1,0:T(8,128)S(1)} %copy-done.47), channel_id=1, source_target_pairs={{0,8},{4,12},{8,16},{12,20},{16,24},{20,28},{24,0},{28,4},{1,9},{5... | collective-permute-start | bytes 393224 | tf_op jit(solution)/shard_map/ppermute | solution.py:199
  149.9 25.2 %collective-permute-start.19 = (f32[256,128]{1,0:T(8,128)S(1)}, f32[256,128]{1,0:T(8,128)S(1)}, u32[]{:S(2)}, u32[]{:S(2)}) collective-permute-start(f32[256,128]{1,0:T(8,128)S(1)} %copy-done.46), channel_id=1, source_target_pairs={{0,4},{4,8},{8,12},{12,16},{16,20},{20,24},{24,28},{28,0},{1,5},{5... | collective-permute-start | bytes 393224 | tf_op jit(solution)/shard_map/ppermute | solution.py:199
  199.7 91.2 %all-to-all-start.3 = ((f32[8,256,128]{2,1,0:T(8,128)}), f32[8,256,128]{2,1,0:T(8,128)S(1)}, u32[]{:S(2)}, u32[]{:S(2)}) async-start(f32[8,256,128]{2,1,0:T(8,128)} %shard_map.97), calls=%async_computation.3 | async-start | bytes 2097152 | tf_op jit(solution)/shard_map/all_to_all | solution.py:204
  203.2 20.9 %collective-permute-start.23 = (f32[8,64,128]{2,1,0:T(8,128)S(1)}, f32[8,64,128]{2,1,0:T(8,128)S(1)}, u32[]{:S(2)}, u32[]{:S(2)}) collective-permute-start(f32[8,64,128]{2,1,0:T(8,128)S(1)} %copy-done.43), channel_id=1, source_target_pairs={{0,3},{1,0},{2,1},{3,2},{4,7},{5,4},{6,5},{7,6},{8,11},{9,8},{10,9... | collective-permute-start | bytes 786440 | tf_op jit(solution)/shard_map/ppermute | solution.py:199
  203.3 19.3 %collective-permute-start.26 = (f32[256,128]{1,0:T(8,128)S(1)}, f32[256,128]{1,0:T(8,128)S(1)}, u32[]{:S(2)}, u32[]{:S(2)}) collective-permute-start(f32[256,128]{1,0:T(8,128)S(1)} %bitcast.65), channel_id=1, source_target_pairs={{0,28},{4,0},{8,4},{12,8},{16,12},{20,16},{24,20},{28,24},{1,29},{... | collective-permute-start | bytes 393224 | tf_op jit(solution)/shard_map/ppermute | solution.py:199
  206.8 17.3 %collective-permute-start.24 = (f32[8,64,128]{2,1,0:T(8,128)}, f32[8,64,128]{2,1,0:T(8,128)S(1)}, u32[]{:S(2)}, u32[]{:S(2)}) collective-permute-start(f32[8,64,128]{2,1,0:T(8,128)} %get-tuple-element.188), channel_id=1, source_target_pairs={{0,2},{1,3},{2,0},{3,1},{4,6},{5,7},{6,4},{7,5},{8,10},{9,11},{10,... | collective-permute-start | bytes 786440 | tf_op jit(solution)/shard_map/ppermute | solution.py:199
  208.3 19.4 %collective-permute-start.25 = (f32[8,64,128]{2,1,0:T(8,128)S(1)}, f32[8,64,128]{2,1,0:T(8,128)S(1)}, u32[]{:S(2)}, u32[]{:S(2)}) collective-permute-start(f32[8,64,128]{2,1,0:T(8,128)S(1)} %copy-done.42), channel_id=1, source_target_pairs={{0,1},{1,2},{2,3},{3,0},{4,5},{5,6},{6,7},{7,4},{8,9},{9,10},{10,1... | collective-permute-start | bytes 786440 | tf_op jit(solution)/shard_map/ppermute | solution.py:199
  210.0 28.4 %collective-permute-start.20 = (f32[9,64,128]{2,1,0:T(8,128)S(1)}, f32[9,64,128]{2,1,0:T(8,128)S(1)}, u32[]{:S(2)}, u32[]{:S(2)}) collective-permute-start(f32[9,64,128]{2,1,0:T(8,128)S(1)} %copy-done.41), channel_id=1, source_target_pairs={{0,3},{1,0},{2,1},{3,2},{4,7},{5,4},{6,5},{7,6},{8,11},{9,8},{10,9... | collective-permute-start | bytes 884744 | tf_op jit(solution)/shard_map/ppermute | solution.py:199
  222.6 15.8 %collective-permute-start.21 = (f32[9,64,128]{2,1,0:T(8,128)}, f32[9,64,128]{2,1,0:T(8,128)S(1)}, u32[]{:S(2)}, u32[]{:S(2)}) collective-permute-start(f32[9,64,128]{2,1,0:T(8,128)} %get-tuple-element.184), channel_id=1, source_target_pairs={{0,2},{1,3},{2,0},{3,1},{4,6},{5,7},{6,4},{7,5},{8,10},{9,11},{10,... | collective-permute-start | bytes 884744 | tf_op jit(solution)/shard_map/ppermute | solution.py:199
  224.1 14.4 %collective-permute-start.22 = (f32[9,64,128]{2,1,0:T(8,128)}, f32[9,64,128]{2,1,0:T(8,128)S(1)}, u32[]{:S(2)}, u32[]{:S(2)}) collective-permute-start(f32[9,64,128]{2,1,0:T(8,128)} %get-tuple-element.185), channel_id=1, source_target_pairs={{0,1},{1,2},{2,3},{3,0},{4,5},{5,6},{6,7},{7,4},{8,9},{9,10},{10,1... | collective-permute-start | bytes 884744 | tf_op jit(solution)/shard_map/ppermute | solution.py:199
  224.1 9.5 %collective-permute-start.27 = (f32[256,128]{1,0:T(8,128)}, f32[256,128]{1,0:T(8,128)S(1)}, u32[]{:S(2)}, u32[]{:S(2)}) collective-permute-start(f32[256,128]{1,0:T(8,128)} %bitcast.60), channel_id=1, source_target_pairs={{0,24},{4,28},{8,0},{12,4},{16,8},{20,12},{24,16},{28,20},{1,25},{... | collective-permute-start | bytes 393224 | tf_op jit(solution)/shard_map/ppermute | solution.py:199
  227.7 18.7 %collective-permute-start.28 = (f32[256,128]{1,0:T(8,128)}, f32[256,128]{1,0:T(8,128)S(1)}, u32[]{:S(2)}, u32[]{:S(2)}) collective-permute-start(f32[256,128]{1,0:T(8,128)} %bitcast.58), channel_id=1, source_target_pairs={{0,20},{4,24},{8,28},{12,0},{16,4},{20,8},{24,12},{28,16},{1,21},{... | collective-permute-start | bytes 393224 | tf_op jit(solution)/shard_map/ppermute | solution.py:199
  233.7 19.1 %collective-permute-start.29 = (f32[256,128]{1,0:T(8,128)}, f32[256,128]{1,0:T(8,128)S(1)}, u32[]{:S(2)}, u32[]{:S(2)}) collective-permute-start(f32[256,128]{1,0:T(8,128)} %bitcast.57), channel_id=1, source_target_pairs={{0,16},{4,20},{8,24},{12,28},{16,0},{20,4},{24,8},{28,12},{1,17},{... | collective-permute-start | bytes 393224 | tf_op jit(solution)/shard_map/ppermute | solution.py:199
  238.4 16.7 %collective-permute-start.30 = (f32[256,128]{1,0:T(8,128)}, f32[256,128]{1,0:T(8,128)S(1)}, u32[]{:S(2)}, u32[]{:S(2)}) collective-permute-start(f32[256,128]{1,0:T(8,128)} %bitcast.56), channel_id=1, source_target_pairs={{0,12},{4,16},{8,20},{12,24},{16,28},{20,0},{24,4},{28,8},{1,13},{... | collective-permute-start | bytes 393224 | tf_op jit(solution)/shard_map/ppermute | solution.py:199
  238.4 16.7 %collective-permute-start.31 = (f32[256,128]{1,0:T(8,128)}, f32[256,128]{1,0:T(8,128)S(1)}, u32[]{:S(2)}, u32[]{:S(2)}) collective-permute-start(f32[256,128]{1,0:T(8,128)} %bitcast.55), channel_id=1, source_target_pairs={{0,8},{4,12},{8,16},{12,20},{16,24},{20,28},{24,0},{28,4},{1,9},{5... | collective-permute-start | bytes 393224 | tf_op jit(solution)/shard_map/ppermute | solution.py:199
  238.5 16.6 %collective-permute-start.32 = (f32[256,128]{1,0:T(8,128)}, f32[256,128]{1,0:T(8,128)}, u32[]{:S(2)}, u32[]{:S(2)}) collective-permute-start(f32[256,128]{1,0:T(8,128)} %bitcast.54), channel_id=1, source_target_pairs={{0,4},{4,8},{8,12},{12,16},{16,20},{20,24},{24,28},{28,0},{1,5},{5... | collective-permute-start | bytes 393224 | tf_op jit(solution)/shard_map/ppermute | solution.py:199
  246.3 19.9 %collective-permute-start.36 = (f32[8,64,128]{2,1,0:T(8,128)}, f32[8,64,128]{2,1,0:T(8,128)S(1)}, u32[]{:S(2)}, u32[]{:S(2)}) collective-permute-start(f32[8,64,128]{2,1,0:T(8,128)} %get-tuple-element.224), channel_id=1, source_target_pairs={{0,3},{1,0},{2,1},{3,2},{4,7},{5,4},{6,5},{7,6},{8,11},{9,8},{10,9... | collective-permute-start | bytes 786440 | tf_op jit(solution)/shard_map/ppermute | solution.py:199
  258.8 7.0 %collective-permute-start.40 = (f32[264,128]{1,0:T(8,128)}, f32[264,128]{1,0:T(8,128)S(1)}, u32[]{:S(2)}, u32[]{:S(2)}) collective-permute-start(f32[264,128]{1,0:T(8,128)} %get-tuple-element.228), channel_id=1, source_target_pairs={{0,24},{4,28},{8,0},{12,4},{16,8},{20,12},{24,16},{28,20},{1,25},{... | collective-permute-start | bytes 405512 | tf_op jit(solution)/shard_map/ppermute | solution.py:199
  259.6 16.2 %collective-permute-start.37 = (f32[8,64,128]{2,1,0:T(8,128)}, f32[8,64,128]{2,1,0:T(8,128)S(1)}, u32[]{:S(2)}, u32[]{:S(2)}) collective-permute-start(f32[8,64,128]{2,1,0:T(8,128)} %get-tuple-element.225), channel_id=1, source_target_pairs={{0,2},{1,3},{2,0},{3,1},{4,6},{5,7},{6,4},{7,5},{8,10},{9,11},{10,... | collective-permute-start | bytes 786440 | tf_op jit(solution)/shard_map/ppermute | solution.py:199
  260.1 15.7 %collective-permute-start.38 = (f32[8,64,128]{2,1,0:T(8,128)}, f32[8,64,128]{2,1,0:T(8,128)S(1)}, u32[]{:S(2)}, u32[]{:S(2)}) collective-permute-start(f32[8,64,128]{2,1,0:T(8,128)} %get-tuple-element.226), channel_id=1, source_target_pairs={{0,1},{1,2},{2,3},{3,0},{4,5},{5,6},{6,7},{7,4},{8,9},{9,10},{10,1... | collective-permute-start | bytes 786440 | tf_op jit(solution)/shard_map/ppermute | solution.py:199
  263.1 13.3 %collective-permute-start.33 = (f32[8,64,128]{2,1,0:T(8,128)}, f32[8,64,128]{2,1,0:T(8,128)S(1)}, u32[]{:S(2)}, u32[]{:S(2)}) collective-permute-start(f32[8,64,128]{2,1,0:T(8,128)} %get-tuple-element.221), channel_id=1, source_target_pairs={{0,3},{1,0},{2,1},{3,2},{4,7},{5,4},{6,5},{7,6},{8,11},{9,8},{10,9... | collective-permute-start | bytes 786440 | tf_op jit(solution)/shard_map/ppermute | solution.py:199
  265.8 18.8 %collective-permute-start.34 = (f32[8,64,128]{2,1,0:T(8,128)}, f32[8,64,128]{2,1,0:T(8,128)S(1)}, u32[]{:S(2)}, u32[]{:S(2)}) collective-permute-start(f32[8,64,128]{2,1,0:T(8,128)} %get-tuple-element.222), channel_id=1, source_target_pairs={{0,2},{1,3},{2,0},{3,1},{4,6},{5,7},{6,4},{7,5},{8,10},{9,11},{10,... | collective-permute-start | bytes 786440 | tf_op jit(solution)/shard_map/ppermute | solution.py:199
  266.3 20.0 %collective-permute-start.35 = (f32[8,64,128]{2,1,0:T(8,128)}, f32[8,64,128]{2,1,0:T(8,128)S(1)}, u32[]{:S(2)}, u32[]{:S(2)}) collective-permute-start(f32[8,64,128]{2,1,0:T(8,128)} %get-tuple-element.223), channel_id=1, source_target_pairs={{0,1},{1,2},{2,3},{3,0},{4,5},{5,6},{6,7},{7,4},{8,9},{9,10},{10,1... | collective-permute-start | bytes 786440 | tf_op jit(solution)/shard_map/ppermute | solution.py:199
  275.9 18.6 %collective-permute-start.41 = (f32[264,128]{1,0:T(8,128)}, f32[264,128]{1,0:T(8,128)S(1)}, u32[]{:S(2)}, u32[]{:S(2)}) collective-permute-start(f32[264,128]{1,0:T(8,128)} %get-tuple-element.229), channel_id=1, source_target_pairs={{0,20},{4,24},{8,28},{12,0},{16,4},{20,8},{24,12},{28,16},{1,21},{... | collective-permute-start | bytes 405512 | tf_op jit(solution)/shard_map/ppermute | solution.py:199
  275.9 19.3 %collective-permute-start.42 = (f32[264,128]{1,0:T(8,128)}, f32[264,128]{1,0:T(8,128)S(1)}, u32[]{:S(2)}, u32[]{:S(2)}) collective-permute-start(f32[264,128]{1,0:T(8,128)} %get-tuple-element.230), channel_id=1, source_target_pairs={{0,16},{4,20},{8,24},{12,28},{16,0},{20,4},{24,8},{28,12},{1,17},{... | collective-permute-start | bytes 405512 | tf_op jit(solution)/shard_map/ppermute | solution.py:199
  276.4 20.5 %collective-permute-start.43 = (f32[264,128]{1,0:T(8,128)}, f32[264,128]{1,0:T(8,128)S(1)}, u32[]{:S(2)}, u32[]{:S(2)}) collective-permute-start(f32[264,128]{1,0:T(8,128)} %get-tuple-element.231), channel_id=1, source_target_pairs={{0,12},{4,16},{8,20},{12,24},{16,28},{20,0},{24,4},{28,8},{1,13},{... | collective-permute-start | bytes 405512 | tf_op jit(solution)/shard_map/ppermute | solution.py:199
  284.6 12.3 %collective-permute-start.44 = (f32[264,128]{1,0:T(8,128)}, f32[264,128]{1,0:T(8,128)S(1)}, u32[]{:S(2)}, u32[]{:S(2)}) collective-permute-start(f32[264,128]{1,0:T(8,128)} %get-tuple-element.232), channel_id=1, source_target_pairs={{0,8},{4,12},{8,16},{12,20},{16,24},{20,28},{24,0},{28,4},{1,9},{5... | collective-permute-start | bytes 405512 | tf_op jit(solution)/shard_map/ppermute | solution.py:199
  286.4 10.5 %collective-permute-start.45 = (f32[264,128]{1,0:T(8,128)}, f32[264,128]{1,0:T(8,128)}, u32[]{:S(2)}, u32[]{:S(2)}) collective-permute-start(f32[264,128]{1,0:T(8,128)} %get-tuple-element.233), channel_id=1, source_target_pairs={{0,4},{4,8},{8,12},{12,16},{16,20},{20,24},{24,28},{28,0},{1,5},{5... | collective-permute-start | bytes 405512 | tf_op jit(solution)/shard_map/ppermute | solution.py:199
  (63 other events, 683.4 us)

commit v3 on v2

--- a/solution.py
+++ b/solution.py
@@ -21,6 +21,7 @@
 pw_third = 1.6382
 pw_fourth = 0.49294
 
+GRANT = 16 << 20
 LANES = 128
 ROWS = 8
 
@@ -116,19 +117,15 @@
     return pl.multiple_of(lax.rem(lax.axis_index(axis) + step, size) * width, width)
 
 
-def whole(shape):
-    return pl.BlockSpec(shape, lambda s: (0,) * len(shape))
-
-
-def call(kernel, ins, outs, in_specs=None, scratch=(), flops=1 << 28):
-    specs = [whole(a.shape) for a in ins]
-    for position, spec in (in_specs or {}).items():
-        specs[position] = spec
+VMEM = pl.BlockSpec(memory_space=pltpu.VMEM)
+HBM = pl.BlockSpec(memory_space=pltpu.HBM)
+
+
+def call(kernel, ins, outs, scratch=(), flops=1 << 28):
     return pl.pallas_call(
         kernel,
-        grid=(1,),
-        in_specs=specs,
-        out_specs=[whole(o) for o in outs],
+        in_specs=[VMEM] * len(ins),
+        out_specs=[VMEM] * len(outs),
         out_shape=[jax.ShapeDtypeStruct(o, jnp.float32) for o in outs],
         scratch_shapes=list(scratch),
         cost_estimate=pl.CostEstimate(
@@ -136,7 +133,31 @@
             bytes_accessed=sum(4 * math.prod(o) for o in outs) + sum(4 * a.size for a in ins),
             transcendentals=0,
         ),
+        compiler_params=pltpu.CompilerParams(vmem_limit_bytes=GRANT),
     )(*ins)
+
+
+def pack(field, outs, parts, grant=GRANT):
+    def kernel(field_ref, *refs):
+        out_refs, semaphore = refs[:-1], refs[-1]
+        copies = [
+            pltpu.make_async_copy(field_ref.at[part], out, semaphore.at[k])
+            for k, (part, out) in enumerate(zip(parts(), out_refs))
+        ]
+        for copy in copies:
+            copy.start()
+        for copy in copies:
+            copy.wait()
+
+    return pl.pallas_call(
+        kernel,
+        in_specs=[pl.BlockSpec(memory_space=pl.ANY)],
+        out_specs=[VMEM] * len(outs),
+        out_shape=[jax.ShapeDtypeStruct(o, jnp.float32) for o in outs],
+        scratch_shapes=[pltpu.SemaphoreType.DMA((len(outs),))],
+        cost_estimate=pl.CostEstimate(flops=1 << 20, bytes_accessed=1 << 22, transcendentals=0),
+        compiler_params=pltpu.CompilerParams(vmem_limit_bytes=grant),
+    )(field)
 
 
 class Plan:
@@ -152,44 +173,26 @@
         return ry % (ROWS * gx) == 0 and ry // gx == ROWS and rx % gy == 0 and (rx // gy) % 2 == 0 and z % (2 * LANES) == 0 and rx % ROWS == 0
 
 
-class Blocks:
-    def __init__(self, plan, stacked):
-        self.plan, self.stacked = plan, stacked
-        self.count = 1 if stacked else plan.gx
-
-    def shapes(self, *piece):
-        return [(self.plan.gx, *piece)] if self.stacked else [piece] * self.plan.gx
-
-    def views(self, refs):
-        return [refs[0].at[d] for d in range(self.plan.gx)] if self.stacked else list(refs)
-
-    def rows(self, t):
-        yc = self.plan.yc
-        return pl.ds(t * yc if self.stacked else slot("gx", t, self.plan.gx, yc), yc)
-
-    def shaped(self, arrays, *piece):
-        lead = (self.plan.gx,) if self.stacked else ()
-        return [a.reshape(*lead, *piece) for a in arrays]
-
-
-def pack_x(plan, density, chunk, lanes, stacked):
-    blocks = Blocks(plan, stacked)
-
-    def kernel(n_ref, *outs):
-        for t, out in enumerate(blocks.views(outs)):
-            out[...] = n_ref[:, blocks.rows(t), :].reshape(plan.rx * plan.yc, lanes)
-
-    spec = pl.BlockSpec((plan.rx, plan.ry, lanes), lambda s: (0, 0, chunk))
-    outs = blocks.shapes(plan.rx * plan.yc, lanes)
-    return call(kernel, [density], outs, {0: spec}, flops=1 << 20)
+def chunk_rows(plan, t):
+    return pl.ds(slot("gx", t, plan.gx, plan.yc), plan.yc)
+
+
+def pack_x(plan, density, chunk, lanes):
+    def parts():
+        own = pl.ds(chunk * lanes, lanes)
+        return [(slice(None), chunk_rows(plan, t), own) for t in range(plan.gx)]
+
+    outs = [(plan.rx, plan.yc, lanes)] * plan.gx
+    grant = None if chunk == 0 else GRANT
+    out = pack(density, outs, parts, grant)
+    return [p.reshape(plan.rx * plan.yc, lanes) for p in out]
 
 
 def pack_y(plan, density):
-    def kernel(n_ref, *outs):
-        for t, out in enumerate(outs):
-            out[...] = n_ref[pl.ds(slot("gy", t, plan.gy, plan.sx), plan.sx)]
-
-    return call(kernel, [density], [(plan.sx, plan.ry, plan.z)] * plan.gy, flops=1 << 20)
+    def parts():
+        return [(pl.ds(slot("gy", t, plan.gy, plan.sx), plan.sx),) for t in range(plan.gy)]
+
+    return pack(density, [(plan.sx, plan.ry, plan.z)] * plan.gy, parts)
 
 
 def rotate(pieces, axis, size):
@@ -198,10 +201,6 @@
         pairs = [(i, (i + t) % size) for i in range(size)]
         arrived[size - t] = lax.ppermute(pieces[t], axis, pairs)
     return arrived
-
-
-def exchange(pieces, axis):
-    return [lax.all_to_all(pieces[0], axis, 0, 0, tiled=True)]
 
 
 def after(arrays, token):
@@ -217,14 +216,12 @@
     return total
 
 
-def deriv_x(plan, matrix, pieces, lanes, stacked, energy=None):
-    rx, yc = plan.rx, plan.yc
+def deriv_x(plan, matrix, pieces, lanes, energy=None):
+    gx, rx, yc = plan.gx, plan.rx, plan.yc
     extra = 0 if energy is None else 1
-    blocks = Blocks(plan, stacked)
 
     def kernel(high_ref, low_ref, *refs):
-        ins = blocks.views(refs[extra : extra + blocks.count])
-        outs = blocks.views(refs[extra + blocks.count :])
+        ins, outs = refs[extra : extra + gx], refs[extra + gx :]
         high, low = high_ref[...], low_ref[...]
         for y in range(0, yc, 2):
             columns = [
@@ -241,7 +238,7 @@
             for out in outs:
                 out[rx * yc :, :] = refs[0][...]
 
-    outs = blocks.shapes((rx + extra) * yc, lanes)
+    outs = [((rx + extra) * yc, lanes)] * gx
     ins = [*matrix] + ([energy] if extra else []) + list(pieces)
     return call(kernel, ins, outs)
 
@@ -270,74 +267,67 @@
     if with_energy:
         outs = outs + [(ROWS, lanes)]
         scratch = [pltpu.VMEM((gy * ROWS, lanes), jnp.float32)]
-    return call(kernel, [*matrix, *pieces], outs, scratch=scratch)
-
-
-def rows_call(kernel, rows, ins, widths, out_width, resident):
+    return call(kernel, [*matrix, *pieces], outs, scratch)
+
+
+def deriv_z(plan, matrix, field):
+    rows = plan.rx * plan.ry
     block = rows // 4
-    return pl.pallas_call(
-        kernel,
-        grid=(4,),
-        in_specs=[pl.BlockSpec(m.shape, lambda s: (0, 0)) for m in resident]
-        + [pl.BlockSpec((block, w), lambda s: (s, 0)) for w in widths],
-        out_specs=pl.BlockSpec((block, out_width), lambda s: (s, 0)),
-        out_shape=jax.ShapeDtypeStruct((rows, out_width), jnp.float32),
-        cost_estimate=pl.CostEstimate(flops=1 << 28, bytes_accessed=1 << 22, transcendentals=0),
-    )(*resident, *ins)
-
-
-def deriv_z(plan, matrix, field):
+
     def kernel(high_ref, low_ref, f_ref, out_ref):
-        out_ref[...] = -times_matrix(f_ref[...], high_ref[...], low_ref[...])
-
-    rows = plan.rx * plan.ry
-    flat = field.reshape(rows, plan.z)
-    return rows_call(kernel, rows, [flat], [plan.z], plan.z, matrix).reshape(field.shape)
+        for r in range(0, rows, block):
+            part = slice(r, r + block)
+            out_ref[part, :] = -times_matrix(f_ref[part, :], high_ref[...], low_ref[...])
+
+    out = call(kernel, [*matrix, field.reshape(rows, plan.z)], [(rows, plan.z)])
+    return out[0].reshape(field.shape)
 
 
 def add_flux_z(plan, matrix, flux, chunk, lanes, terms):
     rows = plan.rx * plan.ry
+    block = rows // 4
     flat = [a.reshape(rows, -1) for a in (flux, *terms)]
 
     def kernel(high_ref, low_ref, f_ref, *refs):
         own = slice(chunk * lanes, (chunk + 1) * lanes)
-        total = times_matrix(f_ref[...], high_ref[own, :], low_ref[own, :])
-        if len(refs) > 1:
-            total = total + refs[0][...] + jnp.concatenate([r[...] for r in refs[1:-1]], axis=1)
-        refs[-1][...] = total
-
-    widths = [a.shape[1] for a in flat]
-    out = rows_call(kernel, rows, flat, widths, plan.z, matrix)
-    return out.reshape(plan.rx, plan.ry, plan.z)
-
-
-def pointwise(plan, density, grad_z, grad_y, grad_x, chunk, lanes, stacked, before):
+        for r in range(0, rows, block):
+            part = slice(r, r + block)
+            total = times_matrix(f_ref[part, :], high_ref[own, :], low_ref[own, :])
+            if len(refs) > 1:
+                rest = jnp.concatenate([t[part, :] for t in refs[1:-1]], axis=1)
+                total = total + refs[0][part, :] + rest
+            refs[-1][part, :] = total
+
+    out = call(kernel, [*matrix, *flat], [(rows, plan.z)])
+    return out[0].reshape(plan.rx, plan.ry, plan.z)
+
+
+def pointwise(plan, density, grad_z, grad_y, grad_x, chunk, lanes, before):
     gx, gy, rx, ry, yc, sx = plan.gx, plan.gy, plan.rx, plan.ry, plan.yc, plan.sx
     extra = 0 if before is None else 1
-    blocks = Blocks(plan, stacked)
 
     def kernel(*refs):
         n_ref, gz_ref = refs[0], refs[1]
         gy_refs = refs[2 : 2 + gy]
-        gx_refs = blocks.views(refs[2 + gy : 2 + gy + blocks.count])
-        refs = refs[2 + gy + blocks.count :]
+        gx_refs = refs[2 + gy : 2 + gy + gx]
+        refs = refs[2 + gy + gx :]
         if extra:
             before_ref, refs = refs[0], refs[1:]
-        fx_refs, refs = blocks.views(refs[: blocks.count]), refs[blocks.count :]
-        fy_refs = refs[:gy]
-        fz_ref, dd_ref, energy_ref = refs[gy:]
+        fx_refs, fy_refs = refs[:gx], refs[gx : gx + gy]
+        fz_ref, dd_ref, energy_ref = refs[gx + gy :]
         total = jnp.zeros((yc, lanes), jnp.float32)
+        own = slice(chunk * lanes, (chunk + 1) * lanes)
         for part in range(gy):
             base = slot("gy", part, gy, sx)
 
             def step(inner, total, part=part, base=base):
                 x = base + inner
                 for t in range(gx):
-                    rows = blocks.rows(t)
-                    n = n_ref[x, rows, :]
+                    rows = chunk_rows(plan, t)
+                    n = n_ref[x, rows, own]
                     d_x = gx_refs[t][x]
-                    d_y = gy_refs[part][inner, rows, :]
-                    d_z = gz_ref[x, rows, :]
+                    d_y = gy_refs[part][inner, rows, own]
+                    d_z = gz_ref[x, rows, own]
                     f, d_dens, d_grad = xc_partials(n, d_x * d_x + d_y * d_y + d_z * d_z)
                     twice = 2.0 * d_grad
                     fx_refs[t][x] = twice * d_x
@@ -355,17 +345,14 @@
                 out[sx, :ROWS, :] = total
         energy_ref[...] = total
 
-    block = pl.BlockSpec((rx, ry, lanes), lambda s: (0, 0, chunk))
-    y_block = pl.BlockSpec((sx, ry, lanes), lambda s: (0, 0, chunk))
-    specs = {0: block, 1: block} | {2 + t: y_block for t in range(gy)}
-    ins = [density, grad_z, *grad_y, *blocks.shaped(grad_x, rx, yc, lanes)]
+    ins = [density, grad_z, *grad_y, *[p.reshape(rx, yc, lanes) for p in grad_x]]
     if extra:
         ins.append(before)
-    outs = blocks.shapes(rx, yc, lanes) + [(sx + extra, ry, lanes)] * gy
+    outs = [(rx, yc, lanes)] * gx + [(sx + extra, ry, lanes)] * gy
     outs += [(rx, ry, lanes)] * 2 + [(yc, lanes)]
-    out = call(kernel, ins, outs, specs, flops=1 << 32)
-    flux_x = blocks.shaped(out[: blocks.count], rx * yc, lanes)
-    return flux_x, out[blocks.count : blocks.count + gy], *out[blocks.count + gy :]
+    out = call(kernel, ins, outs, flops=1 << 32)
+    flux_x = [p.reshape(rx * yc, lanes) for p in out[:gx]]
+    return flux_x, out[gx : gx + gy], *out[gx + gy :]
 
 
 def less_y(plan, base, div_y, lanes):
@@ -383,25 +370,25 @@
     return call(kernel, ins, [(rx, ry, plan.z)], flops=1 << 24)[0]
 
 
-def finish(plan, base, div_x, chunk, lanes, stacked, before, scale):
+def finish(plan, base, div_x, chunk, lanes, before, scale):
     gx, rx, ry, yc = plan.gx, plan.rx, plan.ry, plan.yc
     last = scale is not None
-    blocks = Blocks(plan, stacked)
 
     def kernel(base_ref, *refs):
-        x_refs, refs = blocks.views(refs[: blocks.count]), refs[blocks.count :]
+        x_refs, refs = refs[:gx], refs[gx:]
         out_ref = refs[1] if last else refs[0]
+        own = slice(chunk * lanes, (chunk + 1) * lanes)
         for t in range(gx):
-            rows = blocks.rows(t)
-            out_ref[:, rows, :] = base_ref[:, rows, :] - x_refs[t][:rx]
+            rows = chunk_rows(plan, t)
+            out_ref[:, rows, :] = base_ref[:, rows, own] - x_refs[t][:rx]
         if last:
             energy_ref, ordered = refs[2:]
             total = ordered_sum([p[rx] for p in x_refs], "gx", gx, ordered)
             energy_ref[0, 0] = jnp.sum(total) * scale
 
     block = pl.BlockSpec((rx, ry, lanes), lambda s: (0, 0, chunk))
-    ins = [base, *blocks.shaped(div_x, rx + (1 if last else 0), yc, lanes)]
-    specs = [block] + [whole(a.shape) for a in ins[1:]]
+    ins = [base, *[p.reshape(-1, yc, lanes) for p in div_x]]
+    specs = [VMEM] * len(ins)
     out_shape = [jax.ShapeDtypeStruct((rx, ry, plan.z), jnp.float32)]
     out_specs, scratch, aliases = [block], [], {}
     if last:
@@ -420,6 +407,7 @@
         scratch_shapes=scratch,
         input_output_aliases=aliases,
         cost_estimate=pl.CostEstimate(flops=1 << 24, bytes_accessed=1 << 22, transcendentals=0),
+        compiler_params=pltpu.CompilerParams(vmem_limit_bytes=GRANT),
         name="finish",
     )(*ins)
 
@@ -435,46 +423,44 @@
     matrix_x, matrix_y, matrix_z = split_matrix(count_x), split_matrix(count_y), split_matrix(count_z)
     lanes = plan.z // 2
 
-    out = pack_x(plan, density, 0, lanes, True)
-    dens_0 = exchange(out, "gx")
+    out = pack_x(plan, density, 0, lanes)
+    dens_0 = rotate(out, "gx", gx)
     out = pack_y(plan, *after([density], out[0]))
     dens_y = rotate(out, "gy", gy)
-    packed = pack_x(plan, *after([density], out[0]), 1, lanes, False)
+    packed = pack_x(plan, *after([density], out[0]), 1, lanes)
     grad_z = deriv_z(plan, matrix_z, *after([density], packed[0]))
     dens_1 = rotate(after(packed, grad_z), "gx", gx)
-    out_x = deriv_x(plan, matrix_x, after(dens_0, grad_z), lanes, True)
-    grad_0 = exchange(out_x, "gx")
+    out_x = deriv_x(plan, matrix_x, after(dens_0, grad_z), lanes)
+    grad_0 = rotate(out_x, "gx", gx)
     out = deriv_y(plan, matrix_y, after(dens_y, out_x[0]), plan.z)
     grad_y = rotate(out, "gy", gy)
-    out_x = deriv_x(plan, matrix_x, after(dens_1, out[0]), lanes, False)
+    out_x = deriv_x(plan, matrix_x, after(dens_1, out[0]), lanes)
     grad_1 = rotate(out_x, "gx", gx)
     grad_0 = after(grad_0, out_x[0])
-    f_x, f_y, f_z, part_0, energy = pointwise(
-        plan, density, grad_z, grad_y, grad_0, 0, lanes, True, None
-    )
-    flux_0 = exchange(f_x, "gx")
+    f_x, f_y, f_z, part_0, energy = pointwise(plan, density, grad_z, grad_y, grad_0, 0, lanes, None)
+    flux_0 = rotate(f_x, "gx", gx)
     flux_y = [rotate(f_y, "gy", gy)]
     base = add_flux_z(plan, matrix_z, *after([f_z], energy), 0, lanes, [])
     grad_1 = after(grad_1, base)
     f_x, f_y, f_z, part_1, energy = pointwise(
-        plan, density, grad_z, grad_y, grad_1, 1, lanes, False, energy
+        plan, density, grad_z, grad_y, grad_1, 1, lanes, energy
     )
     flux_1 = rotate(f_x, "gx", gx)
     flux_y.append(rotate(f_y, "gy", gy))
     terms = [base, part_0, part_1]
     base = add_flux_z(plan, matrix_z, *after([f_z], energy), 1, lanes, terms)
-    out_x = deriv_x(plan, matrix_x, after(flux_0, base), lanes, True)
-    div_0 = exchange(out_x, "gx")
+    out_x = deriv_x(plan, matrix_x, after(flux_0, base), lanes)
+    div_0 = rotate(out_x, "gx", gx)
     out = deriv_y(plan, matrix_y, after(flux_y[0], out_x[0]), lanes)
     div_y = [rotate(out, "gy", gy)]
     *out, energy = deriv_y(plan, matrix_y, after(flux_y[1], out[0]), lanes, True)
     div_y.append(rotate(out, "gy", gy))
-    out_x = deriv_x(plan, matrix_x, after(flux_1, out[0]), lanes, False, energy)
+    out_x = deriv_x(plan, matrix_x, after(flux_1, out[0]), lanes, energy)
     div_1 = rotate(out_x, "gx", gx)
     base = less_y(plan, *after([base], out_x[0]), div_y, lanes)
     scale = 1.0 / float(count_x * count_y * count_z)
-    (half,) = finish(plan, base, div_0, 0, lanes, True, None, None)
-    done, energy = finish(plan, base, div_1, 1, lanes, False, half, scale)
+    (half,) = finish(plan, base, div_0, 0, lanes, None, None)
+    done, energy = finish(plan, base, div_1, 1, lanes, half, scale)
     return done, energy[0, 0]
 
 

time: 301 us -> 245 us (0.81)
  Pallas kernels: 73.1 us -> 26.2 us
  local copies, waits for them, and re-layouts: 9.32 us -> 0.03 us
  starting transfers between devices: 97.2 us -> 102 us
  waiting for transfers between devices: 120 us -> 116 us
    pallas_call x16, Pallas kernels: 67.6 us -> 23.8 us  [the longest x13 20.9 us: call(): pl.pallas_call(kernel, in_specs=[VMEM] * len(ins), out_specs=[VMEM] * len...]
    ppermute x46 -> x74, starting transfers between devices: 79.9 us -> 102 us  [rotate(): arrived[size - t] = lax.ppermute(pieces[t], axis, pairs)]
    all_to_all x4 -> x0, starting transfers between devices: 17.3 us -> none  [exchange(): return [lax.all_to_all(pieces[0], axis, 0, 0, tiled=True)]]
    all_to_all x4 -> x0, waiting for transfers between devices: 16.6 us -> none  [exchange(): return [lax.all_to_all(pieces[0], axis, 0, 0, tiled=True)]]
    ppermute x46 -> x74, waiting for transfers between devices: 103 us -> 116 us  [rotate(): arrived[size - t] = lax.ppermute(pieces[t], axis, pairs)]
    unnamed x122 -> x14, local copies, waits for them, and re-layouts: 9.32 us -> 0.03 us
    pallas_call x2, Pallas kernels: 5.51 us -> 2.4 us  [finish(): pl.pallas_call(kernel, grid=(1,), in_specs=specs, out_specs=out_specs, ou...]
  transfers between devices with their start and end apart: 50 -> 74, of which waited for: 19 -> 31; matrix products, arithmetic and copies ran while one was open for 0% -> 0% of each run, Pallas kernels for 17% -> 9%
where the time goes in v3:
time: 245 us
  waiting for transfers between devices  116 us (47%)
  starting transfers between devices  102 us (42%)
  Pallas kernels  26.2 us (11%)
    ppermute x74, waiting for transfers between devices, rotate(): arrived[size - t] = lax.ppermute(pieces[t], axis, pairs)  116 us
    ppermute x74, starting transfers between devices, rotate(): arrived[size - t] = lax.ppermute(pieces[t], axis, pairs)  102 us
    pallas_call x13, Pallas kernels, call(): pl.pallas_call(kernel, in_specs=[VMEM] * len(ins), out_specs=[VMEM] * len...  20.9 us
  transfers between devices with their start and end apart: 74, of which 31 were waited for; matrix products, arithmetic and copies ran while one was open for 0% of the time, Pallas kernels for 9%

profile of v3, /device:TPU:0, one launch (start us, length us, event | category | flops | bytes accessed | tf_op | source)
XLA Modules:
  0.0 245.3 jit_solution(2173932190866742375)
XLA Ops:
  0.6 2.5 %shard_map.86 = (f32[32,8,128]{2,1,0:T(8,128)}, f32[32,8,128]{2,1,0:T(8,128)}, f32[32,8,128]{2,1,0:T(8,128)}, f32[32,8,128]{2,1,0:T(8,128)}, f32[32,8,128]{2,1,0...) custom-call(f32[32,64,256]{2,1,0:T(8,128)} %refs_0_.3), custom_call_target="tpu_custom_call" | custom-call | flops 1048576 | bytes 4194304 | tf_op jit(solution)/shard_map/pallas_call | solution.py:152
  3.1 4.6 %collective-permute-start.3 = (f32[256,128]{1,0:T(8,128)}, f32[256,128]{1,0:T(8,128)S(1)}, u32[]{:S(2)}, u32[]{:S(2)}) collective-permute-start(f32[256,128]{1,0:T(8,128)} %bitcast.143), channel_id=1, source_target_pairs={{0,28},{4,0},{8,4},{12,8},{16,12},{20,16},{24,20},{28,24},{1,29},{... | collective-permute-start | bytes 393224 | tf_op jit(solution)/shard_map/ppermute | solution.py:202
  8.3 2.7 %collective-permute-start.6 = (f32[256,128]{1,0:T(8,128)}, f32[256,128]{1,0:T(8,128)S(1)}, u32[]{:S(2)}, u32[]{:S(2)}) collective-permute-start(f32[256,128]{1,0:T(8,128)} %bitcast.140), channel_id=1, source_target_pairs={{0,16},{4,20},{8,24},{12,28},{16,0},{20,4},{24,8},{28,12},{1,17},{... | collective-permute-start | bytes 393224 | tf_op jit(solution)/shard_map/ppermute | solution.py:202
  11.2 2.5 %collective-permute-start = (f32[8,64,256]{2,1,0:T(8,128)S(1)}, f32[8,64,256]{2,1,0:T(8,128)S(1)}, u32[]{:S(2)}, u32[]{:S(2)}) collective-permute-start(f32[8,64,256]{2,1,0:T(8,128)S(1)} %get-tuple-element.177), channel_id=1, source_target_pairs={{0,3},{1,0},{2,1},{3,2},{4,7},{5,4},{6,5},{7,6},{8,11},{9,8},{10,9... | collective-permute-start | bytes 1572872 | tf_op jit(solution)/shard_map/ppermute | solution.py:202
  14.7 1.5 collective-permute-start.2
  18.5 5.3 %collective-permute-done.6.refs_4_ = f32[256,128]{1,0:T(8,128)S(1)} collective-permute-done((f32[256,128]{1,0:T(8,128)}, f32[256,128]{1,0:T(8,128)S(1)}, u32[]{:S(2)}, u32[]{:S(2)}) %collective-permute-start.6) | collective-permute-done | bytes 131104 | tf_op jit(solution)/shard_map/ppermute | solution.py:202
  23.9 3.5 %collective-permute-start.8 = (f32[256,128]{1,0:T(8,128)S(1)}, f32[256,128]{1,0:T(8,128)S(1)}, u32[]{:S(2)}, u32[]{:S(2)}) collective-permute-start(f32[256,128]{1,0:T(8,128)S(1)} %bitcast.138), channel_id=1, source_target_pairs={{0,8},{4,12},{8,16},{12,20},{16,24},{20,28},{24,0},{28,4},{1,9},{5... | collective-permute-start | bytes 393224 | tf_op jit(solution)/shard_map/ppermute | solution.py:202
  28.8 4.3 %collective-permute-done.8.refs_6_ = f32[256,128]{1,0:T(8,128)S(1)} collective-permute-done((f32[256,128]{1,0:T(8,128)S(1)}, f32[256,128]{1,0:T(8,128)S(1)}, u32[]{:S(2)}, u32[]{:S(2)}) %collective-permute-start.8) | collective-permute-done | bytes 131104 | tf_op jit(solution)/shard_map/ppermute | solution.py:202
  33.1 2.3 collective-permute-done.9.refs_7_
  36.5 3.4 %collective-permute-start.15 = (f32[256,128]{1,0:T(8,128)S(1)}, f32[256,128]{1,0:T(8,128)S(1)}, u32[]{:S(2)}, u32[]{:S(2)}) collective-permute-start(f32[256,128]{1,0:T(8,128)S(1)} %bitcast.134), channel_id=1, source_target_pairs={{0,20},{4,24},{8,28},{12,0},{16,4},{20,8},{24,12},{28,16},{1,21},{... | collective-permute-start | bytes 393224 | tf_op jit(solution)/shard_map/ppermute | solution.py:202
  41.2 1.4 collective-permute-start.16
  45.8 3.8 %collective-permute-start.18 = (f32[256,128]{1,0:T(8,128)S(1)}, f32[256,128]{1,0:T(8,128)S(1)}, u32[]{:S(2)}, u32[]{:S(2)}) collective-permute-start(f32[256,128]{1,0:T(8,128)S(1)} %bitcast.116), channel_id=1, source_target_pairs={{0,8},{4,12},{8,16},{12,20},{16,24},{20,28},{24,0},{28,4},{1,9},{5... | collective-permute-start | bytes 393224 | tf_op jit(solution)/shard_map/ppermute | solution.py:202
  49.6 3.5 %collective-permute-start.27 = (f32[256,128]{1,0:T(8,128)S(1)}, f32[256,128]{1,0:T(8,128)S(1)}, u32[]{:S(2)}, u32[]{:S(2)}) collective-permute-start(f32[256,128]{1,0:T(8,128)S(1)} %get-tuple-element.243), channel_id=1, source_target_pairs={{0,28},{4,0},{8,4},{12,8},{16,12},{20,16},{24,20},{28,24},{1,29},{... | collective-permute-start | bytes 393224 | tf_op jit(solution)/shard_map/ppermute | solution.py:202
  53.1 2.8 %collective-permute-start.28 = (f32[256,128]{1,0:T(8,128)S(1)}, f32[256,128]{1,0:T(8,128)S(1)}, u32[]{:S(2)}, u32[]{:S(2)}) collective-permute-start(f32[256,128]{1,0:T(8,128)S(1)} %get-tuple-element.244), channel_id=1, source_target_pairs={{0,24},{4,28},{8,0},{12,4},{16,8},{20,12},{24,16},{28,20},{1,25},{... | collective-permute-start | bytes 393224 | tf_op jit(solution)/shard_map/ppermute | solution.py:202
  55.9 3.2 %collective-permute-done.17.refs_5_ = f32[256,128]{1,0:T(8,128)S(1)} collective-permute-done((f32[256,128]{1,0:T(8,128)S(1)}, f32[256,128]{1,0:T(8,128)S(1)}, u32[]{:S(2)}, u32[]{:S(2)}) %collective-permute-start.17) | collective-permute-done | bytes 131104 | tf_op jit(solution)/shard_map/ppermute | solution.py:202
  60.8 2.3 collective-permute-start.11
  65.0 6.8 %collective-permute-start.30 = (f32[256,128]{1,0:T(8,128)S(1)}, f32[256,128]{1,0:T(8,128)S(1)}, u32[]{:S(2)}, u32[]{:S(2)}) collective-permute-start(f32[256,128]{1,0:T(8,128)S(1)} %get-tuple-element.246), channel_id=1, source_target_pairs={{0,16},{4,20},{8,24},{12,28},{16,0},{20,4},{24,8},{28,12},{1,17},{... | collective-permute-start | bytes 393224 | tf_op jit(solution)/shard_map/ppermute | solution.py:202
  71.8 10.3 %collective-permute-done.30 = f32[256,128]{1,0:T(8,128)S(1)} collective-permute-done((f32[256,128]{1,0:T(8,128)S(1)}, f32[256,128]{1,0:T(8,128)S(1)}, u32[]{:S(2)}, u32[]{:S(2)}) %collective-permute-start.30) | collective-permute-done | bytes 131104 | tf_op jit(solution)/shard_map/ppermute | solution.py:202
  83.0 6.9 %collective-permute-done.32 = f32[256,128]{1,0:T(8,128)S(1)} collective-permute-done((f32[256,128]{1,0:T(8,128)S(1)}, f32[256,128]{1,0:T(8,128)S(1)}, u32[]{:S(2)}, u32[]{:S(2)}) %collective-permute-start.32) | collective-permute-done | bytes 131104 | tf_op jit(solution)/shard_map/ppermute | solution.py:202
  90.3 3.3 %collective-permute-done.20 = f32[256,128]{1,0:T(8,128)S(1)} collective-permute-done((f32[256,128]{1,0:T(8,128)S(1)}, f32[256,128]{1,0:T(8,128)S(1)}, u32[]{:S(2)}, u32[]{:S(2)}) %collective-permute-start.20) | collective-permute-done | bytes 131104 | tf_op jit(solution)/shard_map/ppermute | solution.py:202
  93.6 2.8 %collective-permute-done.21 = f32[256,128]{1,0:T(8,128)S(1)} collective-permute-done((f32[256,128]{1,0:T(8,128)S(1)}, f32[256,128]{1,0:T(8,128)S(1)}, u32[]{:S(2)}, u32[]{:S(2)}) %collective-permute-start.21) | collective-permute-done | bytes 131104 | tf_op jit(solution)/shard_map/ppermute | solution.py:202
  96.4 1.5 collective-permute-start.24
  97.9 3.4 %collective-permute-start.25 = (f32[256,128]{1,0:T(8,128)S(1)}, f32[256,128]{1,0:T(8,128)S(1)}, u32[]{:S(2)}, u32[]{:S(2)}) collective-permute-start(f32[256,128]{1,0:T(8,128)S(1)} %get-tuple-element.233), channel_id=1, source_target_pairs={{0,8},{4,12},{8,16},{12,20},{16,24},{20,28},{24,0},{28,4},{1,9},{5... | collective-permute-start | bytes 393224 | tf_op jit(solution)/shard_map/ppermute | solution.py:202
  101.3 5.9 %shard_map.93 = (f32[32,8,128]{2,1,0:T(8,128)S(1)}, f32[32,8,128]{2,1,0:T(8,128)S(1)}, f32[32,8,128]{2,1,0:T(8,128)S(1)}, f32[32,8,128]{2,1,0:T(8,128)S(1)}, f32...) custom-call(f32[32,64,256]{2,1,0:T(8,128)S(1)} %copy-done, ...), custom_call_target="tpu_custom_call" | custom-call | flops 4294967296 | bytes 11538432 | tf_op jit(solution)/shard_map/pallas_call | solution.py:125
  107.3 3.6 %collective-permute-start.40 = (f32[256,128]{1,0:T(8,128)S(1)}, f32[256,128]{1,0:T(8,128)S(1)}, u32[]{:S(2)}, u32[]{:S(2)}) collective-permute-start(f32[256,128]{1,0:T(8,128)S(1)} %bitcast.133), channel_id=1, source_target_pairs={{0,28},{4,0},{8,4},{12,8},{16,12},{20,16},{24,20},{28,24},{1,29},{... | collective-permute-start | bytes 393224 | tf_op jit(solution)/shard_map/ppermute | solution.py:202
  110.8 2.3 collective-permute-done.23
  113.7 10.1 %collective-permute-start.43 = (f32[256,128]{1,0:T(8,128)S(1)}, f32[256,128]{1,0:T(8,128)S(1)}, u32[]{:S(2)}, u32[]{:S(2)}) collective-permute-start(f32[256,128]{1,0:T(8,128)S(1)} %bitcast.118), channel_id=1, source_target_pairs={{0,16},{4,20},{8,24},{12,28},{16,0},{20,4},{24,8},{28,12},{1,17},{... | collective-permute-start | bytes 393224 | tf_op jit(solution)/shard_map/ppermute | solution.py:202
  123.7 1.5 collective-permute-start.44
  125.3 6.5 %shard_map.94 = (f32[32,8,128]{2,1,0:T(8,128)S(1)}, f32[32,8,128]{2,1,0:T(8,128)S(1)}, f32[32,8,128]{2,1,0:T(8,128)S(1)}, f32[32,8,128]{2,1,0:T(8,128)S(1)}, f32...) custom-call(f32[32,64,256]{2,1,0:T(8,128)S(1)} %copy-done, ...), custom_call_target="tpu_custom_call" | custom-call | flops 4294967296 | bytes 11673600 | tf_op jit(solution)/shard_map/pallas_call | solution.py:125
  131.9 3.4 %collective-permute-start.47 = (f32[256,128]{1,0:T(8,128)S(1)}, f32[256,128]{1,0:T(8,128)S(1)}, u32[]{:S(2)}, u32[]{:S(2)}) collective-permute-start(f32[256,128]{1,0:T(8,128)S(1)} %bitcast.132), channel_id=1, source_target_pairs={{0,28},{4,0},{8,4},{12,8},{16,12},{20,16},{24,20},{28,24},{1,29},{... | collective-permute-start | bytes 393224 | tf_op jit(solution)/shard_map/ppermute | solution.py:202
  135.3 6.8 %collective-permute-done.43.refs_4_ = f32[256,128]{1,0:T(8,128)S(1)} collective-permute-done((f32[256,128]{1,0:T(8,128)S(1)}, f32[256,128]{1,0:T(8,128)S(1)}, u32[]{:S(2)}, u32[]{:S(2)}) %collective-permute-start.43) | collective-permute-done | bytes 131104 | tf_op jit(solution)/shard_map/ppermute | solution.py:202
  144.4 1.7 collective-permute-start.51
  147.5 1.9 collective-permute-done.49.refs_4_
  150.4 11.2 %collective-permute-done.50.refs_5_ = f32[256,128]{1,0:T(8,128)S(1)} collective-permute-done((f32[256,128]{1,0:T(8,128)S(1)}, f32[256,128]{1,0:T(8,128)S(1)}, u32[]{:S(2)}, u32[]{:S(2)}) %collective-permute-start.50) | collective-permute-done | bytes 131104 | tf_op jit(solution)/shard_map/ppermute | solution.py:202
  161.6 1.7 collective-permute-start.39
  165.0 1.4 collective-permute-start.35
  169.3 2.5 %collective-permute-done.39.refs_3_ = f32[8,64,128]{2,1,0:T(8,128)S(1)} collective-permute-done((f32[8,64,128]{2,1,0:T(8,128)S(1)}, f32[8,64,128]{2,1,0:T(8,128)S(1)}, u32[]{:S(2)}, u32[]{:S(2)}) %collective-permute-start.39) | collective-permute-done | bytes 262176 | tf_op jit(solution)/shard_map/ppermute | solution.py:202
  172.8 2.6 %collective-permute-done.53.refs_8_ = f32[256,128]{1,0:T(8,128)S(1)} collective-permute-done((f32[256,128]{1,0:T(8,128)S(1)}, f32[256,128]{1,0:T(8,128)S(1)}, u32[]{:S(2)}, u32[]{:S(2)}) %collective-permute-start.53) | collective-permute-done | bytes 131104 | tf_op jit(solution)/shard_map/ppermute | solution.py:202
  175.4 1.8 collective-permute-start.68
  177.9 4.5 %collective-permute-start.70 = (f32[256,128]{1,0:T(8,128)S(1)}, f32[256,128]{1,0:T(8,128)S(1)}, u32[]{:S(2)}, u32[]{:S(2)}) collective-permute-start(f32[256,128]{1,0:T(8,128)S(1)} %get-tuple-element.334), channel_id=1, source_target_pairs={{0,16},{4,20},{8,24},{12,28},{16,0},{20,4},{24,8},{28,12},{1,17},{... | collective-permute-start | bytes 393224 | tf_op jit(solution)/shard_map/ppermute | solution.py:202
  186.5 2.6 %collective-permute-start.61 = (f32[264,128]{1,0:T(8,128)S(1)}, f32[264,128]{1,0:T(8,128)S(1)}, u32[]{:S(2)}, u32[]{:S(2)}) collective-permute-start(f32[264,128]{1,0:T(8,128)S(1)} %get-tuple-element.325), channel_id=1, source_target_pairs={{0,24},{4,28},{8,0},{12,4},{16,8},{20,12},{24,16},{28,20},{1,25},{... | collective-permute-start | bytes 405512 | tf_op jit(solution)/shard_map/ppermute | solution.py:202
  189.1 8.8 %collective-permute-done.70 = f32[256,128]{1,0:T(8,128)S(1)} collective-permute-done((f32[256,128]{1,0:T(8,128)S(1)}, f32[256,128]{1,0:T(8,128)S(1)}, u32[]{:S(2)}, u32[]{:S(2)}) %collective-permute-start.70) | collective-permute-done | bytes 131104 | tf_op jit(solution)/shard_map/ppermute | solution.py:202
  197.9 7.6 %collective-permute-done.72 = f32[256,128]{1,0:T(8,128)S(1)} collective-permute-done((f32[256,128]{1,0:T(8,128)S(1)}, f32[256,128]{1,0:T(8,128)S(1)}, u32[]{:S(2)}, u32[]{:S(2)}) %collective-permute-start.72) | collective-permute-done | bytes 131104 | tf_op jit(solution)/shard_map/ppermute | solution.py:202
  206.5 2.9 %collective-permute-start.57 = (f32[8,64,128]{2,1,0:T(8,128)S(1)}, f32[8,64,128]{2,1,0:T(8,128)S(1)}, u32[]{:S(2)}, u32[]{:S(2)}) collective-permute-start(f32[8,64,128]{2,1,0:T(8,128)S(1)} %get-tuple-element.321), channel_id=1, source_target_pairs={{0,3},{1,0},{2,1},{3,2},{4,7},{5,4},{6,5},{7,6},{8,11},{9,8},{10,9... | collective-permute-start | bytes 786440 | tf_op jit(solution)/shard_map/ppermute | solution.py:202
  210.5 10.7 %collective-permute-done.55.refs_2_ = f32[8,64,128]{2,1,0:T(8,128)S(1)} collective-permute-done((f32[8,64,128]{2,1,0:T(8,128)S(1)}, f32[8,64,128]{2,1,0:T(8,128)S(1)}, u32[]{:S(2)}, u32[]{:S(2)}) %collective-permute-start.55) | collective-permute-done | bytes 262176 | tf_op jit(solution)/shard_map/ppermute | solution.py:202
  221.2 4.4 %collective-permute-start.63 = (f32[264,128]{1,0:T(8,128)S(1)}, f32[264,128]{1,0:T(8,128)S(1)}, u32[]{:S(2)}, u32[]{:S(2)}) collective-permute-start(f32[264,128]{1,0:T(8,128)S(1)} %get-tuple-element.327), channel_id=1, source_target_pairs={{0,16},{4,20},{8,24},{12,28},{16,0},{20,4},{24,8},{28,12},{1,17},{... | collective-permute-start | bytes 405512 | tf_op jit(solution)/shard_map/ppermute | solution.py:202
  225.6 1.5 collective-permute-start.64
  230.3 13.4 %collective-permute-done.63 = f32[264,128]{1,0:T(8,128)S(1)} collective-permute-done((f32[264,128]{1,0:T(8,128)S(1)}, f32[264,128]{1,0:T(8,128)S(1)}, u32[]{:S(2)}, u32[]{:S(2)}) %collective-permute-start.63) | collective-permute-done | bytes 135200 | tf_op jit(solution)/shard_map/ppermute | solution.py:202
  (132 shorter events, 38.2 us)
Async XLA Ops:
  8.3 15.5 %collective-permute-start.6 = (f32[256,128]{1,0:T(8,128)}, f32[256,128]{1,0:T(8,128)S(1)}, u32[]{:S(2)}, u32[]{:S(2)}) collective-permute-start(f32[256,128]{1,0:T(8,128)} %bitcast.140), channel_id=1, source_target_pairs={{0,16},{4,20},{8,24},{12,28},{16,0},{20,4},{24,8},{28,12},{1,17},{... | collective-permute-start | bytes 393224 | tf_op jit(solution)/shard_map/ppermute | solution.py:202
  11.2 34.5 %collective-permute-start = (f32[8,64,256]{2,1,0:T(8,128)S(1)}, f32[8,64,256]{2,1,0:T(8,128)S(1)}, u32[]{:S(2)}, u32[]{:S(2)}) collective-permute-start(f32[8,64,256]{2,1,0:T(8,128)S(1)} %get-tuple-element.177), channel_id=1, source_target_pairs={{0,3},{1,0},{2,1},{3,2},{4,7},{5,4},{6,5},{7,6},{8,11},{9,8},{10,9... | collective-permute-start | bytes 1572872 | tf_op jit(solution)/shard_map/ppermute | solution.py:202
  13.7 35.9 %collective-permute-start.1 = (f32[8,64,256]{2,1,0:T(8,128)S(1)}, f32[8,64,256]{2,1,0:T(8,128)S(1)}, u32[]{:S(2)}, u32[]{:S(2)}) collective-permute-start(f32[8,64,256]{2,1,0:T(8,128)S(1)} %get-tuple-element.178), channel_id=1, source_target_pairs={{0,2},{1,3},{2,0},{3,1},{4,6},{5,7},{6,4},{7,5},{8,10},{9,11},{10,... | collective-permute-start | bytes 1572872 | tf_op jit(solution)/shard_map/ppermute | solution.py:202
  14.7 34.9 %collective-permute-start.2 = (f32[8,64,256]{2,1,0:T(8,128)S(1)}, f32[8,64,256]{2,1,0:T(8,128)S(1)}, u32[]{:S(2)}, u32[]{:S(2)}) collective-permute-start(f32[8,64,256]{2,1,0:T(8,128)S(1)} %get-tuple-element.179), channel_id=1, source_target_pairs={{0,1},{1,2},{2,3},{3,0},{4,5},{5,6},{6,7},{7,4},{8,9},{9,10},{10,1... | collective-permute-start | bytes 1572872 | tf_op jit(solution)/shard_map/ppermute | solution.py:202
  41.2 11.9 %collective-permute-start.16 = (f32[256,128]{1,0:T(8,128)S(1)}, f32[256,128]{1,0:T(8,128)S(1)}, u32[]{:S(2)}, u32[]{:S(2)}) collective-permute-start(f32[256,128]{1,0:T(8,128)S(1)} %bitcast.127), channel_id=1, source_target_pairs={{0,16},{4,20},{8,24},{12,28},{16,0},{20,4},{24,8},{28,12},{1,17},{... | collective-permute-start | bytes 393224 | tf_op jit(solution)/shard_map/ppermute | solution.py:202
  43.8 15.3 %collective-permute-start.17 = (f32[256,128]{1,0:T(8,128)S(1)}, f32[256,128]{1,0:T(8,128)S(1)}, u32[]{:S(2)}, u32[]{:S(2)}) collective-permute-start(f32[256,128]{1,0:T(8,128)S(1)} %bitcast.124), channel_id=1, source_target_pairs={{0,12},{4,16},{8,20},{12,24},{16,28},{20,0},{24,4},{28,8},{1,13},{... | collective-permute-start | bytes 393224 | tf_op jit(solution)/shard_map/ppermute | solution.py:202
  45.8 14.4 %collective-permute-start.18 = (f32[256,128]{1,0:T(8,128)S(1)}, f32[256,128]{1,0:T(8,128)S(1)}, u32[]{:S(2)}, u32[]{:S(2)}) collective-permute-start(f32[256,128]{1,0:T(8,128)S(1)} %bitcast.116), channel_id=1, source_target_pairs={{0,8},{4,12},{8,16},{12,20},{16,24},{20,28},{24,0},{28,4},{1,9},{5... | collective-permute-start | bytes 393224 | tf_op jit(solution)/shard_map/ppermute | solution.py:202
  49.6 13.5 %collective-permute-start.27 = (f32[256,128]{1,0:T(8,128)S(1)}, f32[256,128]{1,0:T(8,128)S(1)}, u32[]{:S(2)}, u32[]{:S(2)}) collective-permute-start(f32[256,128]{1,0:T(8,128)S(1)} %get-tuple-element.243), channel_id=1, source_target_pairs={{0,28},{4,0},{8,4},{12,8},{16,12},{20,16},{24,20},{28,24},{1,29},{... | collective-permute-start | bytes 393224 | tf_op jit(solution)/shard_map/ppermute | solution.py:202
  53.1 11.9 %collective-permute-start.28 = (f32[256,128]{1,0:T(8,128)S(1)}, f32[256,128]{1,0:T(8,128)S(1)}, u32[]{:S(2)}, u32[]{:S(2)}) collective-permute-start(f32[256,128]{1,0:T(8,128)S(1)} %get-tuple-element.244), channel_id=1, source_target_pairs={{0,24},{4,28},{8,0},{12,4},{16,8},{20,12},{24,16},{28,20},{1,25},{... | collective-permute-start | bytes 393224 | tf_op jit(solution)/shard_map/ppermute | solution.py:202
  59.1 12.7 %collective-permute-start.29 = (f32[256,128]{1,0:T(8,128)S(1)}, f32[256,128]{1,0:T(8,128)S(1)}, u32[]{:S(2)}, u32[]{:S(2)}) collective-permute-start(f32[256,128]{1,0:T(8,128)S(1)} %get-tuple-element.245), channel_id=1, source_target_pairs={{0,20},{4,24},{8,28},{12,0},{16,4},{20,8},{24,12},{28,16},{1,21},{... | collective-permute-start | bytes 393224 | tf_op jit(solution)/shard_map/ppermute | solution.py:202
  60.2 36.3 %collective-permute-start.10 = (f32[8,64,256]{2,1,0:T(8,128)S(1)}, f32[8,64,256]{2,1,0:T(8,128)S(1)}, u32[]{:S(2)}, u32[]{:S(2)}) collective-permute-start(f32[8,64,256]{2,1,0:T(8,128)S(1)} %get-tuple-element.201), channel_id=1, source_target_pairs={{0,3},{1,0},{2,1},{3,2},{4,7},{5,4},{6,5},{7,6},{8,11},{9,8},{10,9... | collective-permute-start | bytes 1572872 | tf_op jit(solution)/shard_map/ppermute | solution.py:202
  60.8 37.1 %collective-permute-start.11 = (f32[8,64,256]{2,1,0:T(8,128)S(1)}, f32[8,64,256]{2,1,0:T(8,128)S(1)}, u32[]{:S(2)}, u32[]{:S(2)}) collective-permute-start(f32[8,64,256]{2,1,0:T(8,128)S(1)} %get-tuple-element.202), channel_id=1, source_target_pairs={{0,2},{1,3},{2,0},{3,1},{4,6},{5,7},{6,4},{7,5},{8,10},{9,11},{10,... | collective-permute-start | bytes 1572872 | tf_op jit(solution)/shard_map/ppermute | solution.py:202
  63.2 38.2 %collective-permute-start.12 = (f32[8,64,256]{2,1,0:T(8,128)S(1)}, f32[8,64,256]{2,1,0:T(8,128)S(1)}, u32[]{:S(2)}, u32[]{:S(2)}) collective-permute-start(f32[8,64,256]{2,1,0:T(8,128)S(1)} %get-tuple-element.203), channel_id=1, source_target_pairs={{0,1},{1,2},{2,3},{3,0},{4,5},{5,6},{6,7},{7,4},{8,9},{9,10},{10,1... | collective-permute-start | bytes 1572872 | tf_op jit(solution)/shard_map/ppermute | solution.py:202
  65.0 17.1 %collective-permute-start.30 = (f32[256,128]{1,0:T(8,128)S(1)}, f32[256,128]{1,0:T(8,128)S(1)}, u32[]{:S(2)}, u32[]{:S(2)}) collective-permute-start(f32[256,128]{1,0:T(8,128)S(1)} %get-tuple-element.246), channel_id=1, source_target_pairs={{0,16},{4,20},{8,24},{12,28},{16,0},{20,4},{24,8},{28,12},{1,17},{... | collective-permute-start | bytes 393224 | tf_op jit(solution)/shard_map/ppermute | solution.py:202
  93.6 13.7 %collective-permute-start.22 = (f32[256,128]{1,0:T(8,128)S(1)}, f32[256,128]{1,0:T(8,128)S(1)}, u32[]{:S(2)}, u32[]{:S(2)}) collective-permute-start(f32[256,128]{1,0:T(8,128)S(1)} %get-tuple-element.230), channel_id=1, source_target_pairs={{0,20},{4,24},{8,28},{12,0},{16,4},{20,8},{24,12},{28,16},{1,21},{... | collective-permute-start | bytes 393224 | tf_op jit(solution)/shard_map/ppermute | solution.py:202
  96.4 16.7 %collective-permute-start.23 = (f32[256,128]{1,0:T(8,128)S(1)}, f32[256,128]{1,0:T(8,128)S(1)}, u32[]{:S(2)}, u32[]{:S(2)}) collective-permute-start(f32[256,128]{1,0:T(8,128)S(1)} %get-tuple-element.231), channel_id=1, source_target_pairs={{0,16},{4,20},{8,24},{12,28},{16,0},{20,4},{24,8},{28,12},{1,17},{... | collective-permute-start | bytes 393224 | tf_op jit(solution)/shard_map/ppermute | solution.py:202
  96.4 16.7 %collective-permute-start.24 = (f32[256,128]{1,0:T(8,128)S(1)}, f32[256,128]{1,0:T(8,128)S(1)}, u32[]{:S(2)}, u32[]{:S(2)}) collective-permute-start(f32[256,128]{1,0:T(8,128)S(1)} %get-tuple-element.232), channel_id=1, source_target_pairs={{0,12},{4,16},{8,20},{12,24},{16,28},{20,0},{24,4},{28,8},{1,13},{... | collective-permute-start | bytes 393224 | tf_op jit(solution)/shard_map/ppermute | solution.py:202
  97.9 15.3 %collective-permute-start.25 = (f32[256,128]{1,0:T(8,128)S(1)}, f32[256,128]{1,0:T(8,128)S(1)}, u32[]{:S(2)}, u32[]{:S(2)}) collective-permute-start(f32[256,128]{1,0:T(8,128)S(1)} %get-tuple-element.233), channel_id=1, source_target_pairs={{0,8},{4,12},{8,16},{12,20},{16,24},{20,28},{24,0},{28,4},{1,9},{5... | collective-permute-start | bytes 393224 | tf_op jit(solution)/shard_map/ppermute | solution.py:202
  107.3 17.9 %collective-permute-start.40 = (f32[256,128]{1,0:T(8,128)S(1)}, f32[256,128]{1,0:T(8,128)S(1)}, u32[]{:S(2)}, u32[]{:S(2)}) collective-permute-start(f32[256,128]{1,0:T(8,128)S(1)} %bitcast.133), channel_id=1, source_target_pairs={{0,28},{4,0},{8,4},{12,8},{16,12},{20,16},{24,20},{28,24},{1,29},{... | collective-permute-start | bytes 393224 | tf_op jit(solution)/shard_map/ppermute | solution.py:202
  113.1 12.1 %collective-permute-start.41 = (f32[256,128]{1,0:T(8,128)S(1)}, f32[256,128]{1,0:T(8,128)S(1)}, u32[]{:S(2)}, u32[]{:S(2)}) collective-permute-start(f32[256,128]{1,0:T(8,128)S(1)} %bitcast.131), channel_id=1, source_target_pairs={{0,24},{4,28},{8,0},{12,4},{16,8},{20,12},{24,16},{28,20},{1,25},{... | collective-permute-start | bytes 393224 | tf_op jit(solution)/shard_map/ppermute | solution.py:202
  113.2 18.7 %collective-permute-start.42 = (f32[256,128]{1,0:T(8,128)S(1)}, f32[256,128]{1,0:T(8,128)S(1)}, u32[]{:S(2)}, u32[]{:S(2)}) collective-permute-start(f32[256,128]{1,0:T(8,128)S(1)} %bitcast.121), channel_id=1, source_target_pairs={{0,20},{4,24},{8,28},{12,0},{16,4},{20,8},{24,12},{28,16},{1,21},{... | collective-permute-start | bytes 393224 | tf_op jit(solution)/shard_map/ppermute | solution.py:202
  113.7 28.4 %collective-permute-start.43 = (f32[256,128]{1,0:T(8,128)S(1)}, f32[256,128]{1,0:T(8,128)S(1)}, u32[]{:S(2)}, u32[]{:S(2)}) collective-permute-start(f32[256,128]{1,0:T(8,128)S(1)} %bitcast.118), channel_id=1, source_target_pairs={{0,16},{4,20},{8,24},{12,28},{16,0},{20,4},{24,8},{28,12},{1,17},{... | collective-permute-start | bytes 393224 | tf_op jit(solution)/shard_map/ppermute | solution.py:202
  123.7 19.2 %collective-permute-start.44 = (f32[256,128]{1,0:T(8,128)S(1)}, f32[256,128]{1,0:T(8,128)S(1)}, u32[]{:S(2)}, u32[]{:S(2)}) collective-permute-start(f32[256,128]{1,0:T(8,128)S(1)} %bitcast.114), channel_id=1, source_target_pairs={{0,12},{4,16},{8,20},{12,24},{16,28},{20,0},{24,4},{28,8},{1,13},{... | collective-permute-start | bytes 393224 | tf_op jit(solution)/shard_map/ppermute | solution.py:202
  125.2 19.1 %collective-permute-start.45 = (f32[256,128]{1,0:T(8,128)S(1)}, f32[256,128]{1,0:T(8,128)S(1)}, u32[]{:S(2)}, u32[]{:S(2)}) collective-permute-start(f32[256,128]{1,0:T(8,128)S(1)} %bitcast.111), channel_id=1, source_target_pairs={{0,8},{4,12},{8,16},{12,20},{16,24},{20,28},{24,0},{28,4},{1,9},{5... | collective-permute-start | bytes 393224 | tf_op jit(solution)/shard_map/ppermute | solution.py:202
  125.2 19.1 %collective-permute-start.46 = (f32[256,128]{1,0:T(8,128)S(1)}, f32[256,128]{1,0:T(8,128)S(1)}, u32[]{:S(2)}, u32[]{:S(2)}) collective-permute-start(f32[256,128]{1,0:T(8,128)S(1)} %bitcast.109), channel_id=1, source_target_pairs={{0,4},{4,8},{8,12},{12,16},{16,20},{20,24},{24,28},{28,0},{1,5},{5... | collective-permute-start | bytes 393224 | tf_op jit(solution)/shard_map/ppermute | solution.py:202
  131.9 12.6 %collective-permute-start.47 = (f32[256,128]{1,0:T(8,128)S(1)}, f32[256,128]{1,0:T(8,128)S(1)}, u32[]{:S(2)}, u32[]{:S(2)}) collective-permute-start(f32[256,128]{1,0:T(8,128)S(1)} %bitcast.132), channel_id=1, source_target_pairs={{0,28},{4,0},{8,4},{12,8},{16,12},{20,16},{24,20},{28,24},{1,29},{... | collective-permute-start | bytes 393224 | tf_op jit(solution)/shard_map/ppermute | solution.py:202
  142.9 23.5 %collective-permute-start.37 = (f32[8,64,128]{2,1,0:T(8,128)S(1)}, f32[8,64,128]{2,1,0:T(8,128)S(1)}, u32[]{:S(2)}, u32[]{:S(2)}) collective-permute-start(f32[8,64,128]{2,1,0:T(8,128)S(1)} %get-tuple-element.269), channel_id=1, source_target_pairs={{0,3},{1,0},{2,1},{3,2},{4,7},{5,4},{6,5},{7,6},{8,11},{9,8},{10,9... | collective-permute-start | bytes 786440 | tf_op jit(solution)/shard_map/ppermute | solution.py:202
  144.3 17.3 %collective-permute-start.50 = (f32[256,128]{1,0:T(8,128)S(1)}, f32[256,128]{1,0:T(8,128)S(1)}, u32[]{:S(2)}, u32[]{:S(2)}) collective-permute-start(f32[256,128]{1,0:T(8,128)S(1)} %bitcast.128), channel_id=1, source_target_pairs={{0,16},{4,20},{8,24},{12,28},{16,0},{20,4},{24,8},{28,12},{1,17},{... | collective-permute-start | bytes 393224 | tf_op jit(solution)/shard_map/ppermute | solution.py:202
  144.4 19.2 %collective-permute-start.51 = (f32[256,128]{1,0:T(8,128)S(1)}, f32[256,128]{1,0:T(8,128)S(1)}, u32[]{:S(2)}, u32[]{:S(2)}) collective-permute-start(f32[256,128]{1,0:T(8,128)S(1)} %bitcast.126), channel_id=1, source_target_pairs={{0,12},{4,16},{8,20},{12,24},{16,28},{20,0},{24,4},{28,8},{1,13},{... | collective-permute-start | bytes 393224 | tf_op jit(solution)/shard_map/ppermute | solution.py:202
  147.3 17.7 %collective-permute-start.52 = (f32[256,128]{1,0:T(8,128)S(1)}, f32[256,128]{1,0:T(8,128)S(1)}, u32[]{:S(2)}, u32[]{:S(2)}) collective-permute-start(f32[256,128]{1,0:T(8,128)S(1)} %bitcast.123), channel_id=1, source_target_pairs={{0,8},{4,12},{8,16},{12,20},{16,24},{20,28},{24,0},{28,4},{1,9},{5... | collective-permute-start | bytes 393224 | tf_op jit(solution)/shard_map/ppermute | solution.py:202
  149.4 19.8 %collective-permute-start.38 = (f32[8,64,128]{2,1,0:T(8,128)S(1)}, f32[8,64,128]{2,1,0:T(8,128)S(1)}, u32[]{:S(2)}, u32[]{:S(2)}) collective-permute-start(f32[8,64,128]{2,1,0:T(8,128)S(1)} %get-tuple-element.270), channel_id=1, source_target_pairs={{0,2},{1,3},{2,0},{3,1},{4,6},{5,7},{6,4},{7,5},{8,10},{9,11},{10,... | collective-permute-start | bytes 786440 | tf_op jit(solution)/shard_map/ppermute | solution.py:202
  163.6 14.3 %collective-permute-start.34 = (f32[9,64,128]{2,1,0:T(8,128)S(1)}, f32[9,64,128]{2,1,0:T(8,128)S(1)}, u32[]{:S(2)}, u32[]{:S(2)}) collective-permute-start(f32[9,64,128]{2,1,0:T(8,128)S(1)} %get-tuple-element.265), channel_id=1, source_target_pairs={{0,3},{1,0},{2,1},{3,2},{4,7},{5,4},{6,5},{7,6},{8,11},{9,8},{10,9... | collective-permute-start | bytes 884744 | tf_op jit(solution)/shard_map/ppermute | solution.py:202
  165.0 17.4 %collective-permute-start.35 = (f32[9,64,128]{2,1,0:T(8,128)S(1)}, f32[9,64,128]{2,1,0:T(8,128)S(1)}, u32[]{:S(2)}, u32[]{:S(2)}) collective-permute-start(f32[9,64,128]{2,1,0:T(8,128)S(1)} %get-tuple-element.266), channel_id=1, source_target_pairs={{0,2},{1,3},{2,0},{3,1},{4,6},{5,7},{6,4},{7,5},{8,10},{9,11},{10,... | collective-permute-start | bytes 884744 | tf_op jit(solution)/shard_map/ppermute | solution.py:202
  166.4 17.4 %collective-permute-start.36 = (f32[9,64,128]{2,1,0:T(8,128)S(1)}, f32[9,64,128]{2,1,0:T(8,128)S(1)}, u32[]{:S(2)}, u32[]{:S(2)}) collective-permute-start(f32[9,64,128]{2,1,0:T(8,128)S(1)} %get-tuple-element.267), channel_id=1, source_target_pairs={{0,1},{1,2},{2,3},{3,0},{4,5},{5,6},{6,7},{7,4},{8,9},{9,10},{10,1... | collective-permute-start | bytes 884744 | tf_op jit(solution)/shard_map/ppermute | solution.py:202
  177.9 20.0 %collective-permute-start.70 = (f32[256,128]{1,0:T(8,128)S(1)}, f32[256,128]{1,0:T(8,128)S(1)}, u32[]{:S(2)}, u32[]{:S(2)}) collective-permute-start(f32[256,128]{1,0:T(8,128)S(1)} %get-tuple-element.334), channel_id=1, source_target_pairs={{0,16},{4,20},{8,24},{12,28},{16,0},{20,4},{24,8},{28,12},{1,17},{... | collective-permute-start | bytes 393224 | tf_op jit(solution)/shard_map/ppermute | solution.py:202
  182.4 15.5 %collective-permute-start.71 = (f32[256,128]{1,0:T(8,128)S(1)}, f32[256,128]{1,0:T(8,128)S(1)}, u32[]{:S(2)}, u32[]{:S(2)}) collective-permute-start(f32[256,128]{1,0:T(8,128)S(1)} %get-tuple-element.335), channel_id=1, source_target_pairs={{0,12},{4,16},{8,20},{12,24},{16,28},{20,0},{24,4},{28,8},{1,13},{... | collective-permute-start | bytes 393224 | tf_op jit(solution)/shard_map/ppermute | solution.py:202
  183.8 26.7 %collective-permute-start.54 = (f32[8,64,128]{2,1,0:T(8,128)S(1)}, f32[8,64,128]{2,1,0:T(8,128)S(1)}, u32[]{:S(2)}, u32[]{:S(2)}) collective-permute-start(f32[8,64,128]{2,1,0:T(8,128)S(1)} %get-tuple-element.318), channel_id=1, source_target_pairs={{0,3},{1,0},{2,1},{3,2},{4,7},{5,4},{6,5},{7,6},{8,11},{9,8},{10,9... | collective-permute-start | bytes 786440 | tf_op jit(solution)/shard_map/ppermute | solution.py:202
  185.7 20.8 %collective-permute-start.60 = (f32[264,128]{1,0:T(8,128)S(1)}, f32[264,128]{1,0:T(8,128)S(1)}, u32[]{:S(2)}, u32[]{:S(2)}) collective-permute-start(f32[264,128]{1,0:T(8,128)S(1)} %get-tuple-element.324), channel_id=1, source_target_pairs={{0,28},{4,0},{8,4},{12,8},{16,12},{20,16},{24,20},{28,24},{1,29},{... | collective-permute-start | bytes 405512 | tf_op jit(solution)/shard_map/ppermute | solution.py:202
  186.5 22.9 %collective-permute-start.61 = (f32[264,128]{1,0:T(8,128)S(1)}, f32[264,128]{1,0:T(8,128)S(1)}, u32[]{:S(2)}, u32[]{:S(2)}) collective-permute-start(f32[264,128]{1,0:T(8,128)S(1)} %get-tuple-element.325), channel_id=1, source_target_pairs={{0,24},{4,28},{8,0},{12,4},{16,8},{20,12},{24,16},{28,20},{1,25},{... | collective-permute-start | bytes 405512 | tf_op jit(solution)/shard_map/ppermute | solution.py:202
  205.5 15.7 %collective-permute-start.55 = (f32[8,64,128]{2,1,0:T(8,128)S(1)}, f32[8,64,128]{2,1,0:T(8,128)S(1)}, u32[]{:S(2)}, u32[]{:S(2)}) collective-permute-start(f32[8,64,128]{2,1,0:T(8,128)S(1)} %get-tuple-element.319), channel_id=1, source_target_pairs={{0,2},{1,3},{2,0},{3,1},{4,6},{5,7},{6,4},{7,5},{8,10},{9,11},{10,... | collective-permute-start | bytes 786440 | tf_op jit(solution)/shard_map/ppermute | solution.py:202
  206.5 14.7 %collective-permute-start.56 = (f32[8,64,128]{2,1,0:T(8,128)S(1)}, f32[8,64,128]{2,1,0:T(8,128)S(1)}, u32[]{:S(2)}, u32[]{:S(2)}) collective-permute-start(f32[8,64,128]{2,1,0:T(8,128)S(1)} %get-tuple-element.320), channel_id=1, source_target_pairs={{0,1},{1,2},{2,3},{3,0},{4,5},{5,6},{6,7},{7,4},{8,9},{9,10},{10,1... | collective-permute-start | bytes 786440 | tf_op jit(solution)/shard_map/ppermute | solution.py:202
  206.5 19.1 %collective-permute-start.57 = (f32[8,64,128]{2,1,0:T(8,128)S(1)}, f32[8,64,128]{2,1,0:T(8,128)S(1)}, u32[]{:S(2)}, u32[]{:S(2)}) collective-permute-start(f32[8,64,128]{2,1,0:T(8,128)S(1)} %get-tuple-element.321), channel_id=1, source_target_pairs={{0,3},{1,0},{2,1},{3,2},{4,7},{5,4},{6,5},{7,6},{8,11},{9,8},{10,9... | collective-permute-start | bytes 786440 | tf_op jit(solution)/shard_map/ppermute | solution.py:202
  209.4 18.1 %collective-permute-start.58 = (f32[8,64,128]{2,1,0:T(8,128)S(1)}, f32[8,64,128]{2,1,0:T(8,128)S(1)}, u32[]{:S(2)}, u32[]{:S(2)}) collective-permute-start(f32[8,64,128]{2,1,0:T(8,128)S(1)} %get-tuple-element.322), channel_id=1, source_target_pairs={{0,2},{1,3},{2,0},{3,1},{4,6},{5,7},{6,4},{7,5},{8,10},{9,11},{10,... | collective-permute-start | bytes 786440 | tf_op jit(solution)/shard_map/ppermute | solution.py:202
  210.5 18.3 %collective-permute-start.59 = (f32[8,64,128]{2,1,0:T(8,128)S(1)}, f32[8,64,128]{2,1,0:T(8,128)S(1)}, u32[]{:S(2)}, u32[]{:S(2)}) collective-permute-start(f32[8,64,128]{2,1,0:T(8,128)S(1)} %get-tuple-element.323), channel_id=1, source_target_pairs={{0,1},{1,2},{2,3},{3,0},{4,5},{5,6},{6,7},{7,4},{8,9},{9,10},{10,1... | collective-permute-start | bytes 786440 | tf_op jit(solution)/shard_map/ppermute | solution.py:202
  221.2 22.5 %collective-permute-start.63 = (f32[264,128]{1,0:T(8,128)S(1)}, f32[264,128]{1,0:T(8,128)S(1)}, u32[]{:S(2)}, u32[]{:S(2)}) collective-permute-start(f32[264,128]{1,0:T(8,128)S(1)} %get-tuple-element.327), channel_id=1, source_target_pairs={{0,16},{4,20},{8,24},{12,28},{16,0},{20,4},{24,8},{28,12},{1,17},{... | collective-permute-start | bytes 405512 | tf_op jit(solution)/shard_map/ppermute | solution.py:202
  225.6 18.4 %collective-permute-start.64 = (f32[264,128]{1,0:T(8,128)S(1)}, f32[264,128]{1,0:T(8,128)S(1)}, u32[]{:S(2)}, u32[]{:S(2)}) collective-permute-start(f32[264,128]{1,0:T(8,128)S(1)} %get-tuple-element.328), channel_id=1, source_target_pairs={{0,12},{4,16},{8,20},{12,24},{16,28},{20,0},{24,4},{28,8},{1,13},{... | collective-permute-start | bytes 405512 | tf_op jit(solution)/shard_map/ppermute | solution.py:202
  227.5 16.4 %collective-permute-start.65 = (f32[264,128]{1,0:T(8,128)S(1)}, f32[264,128]{1,0:T(8,128)S(1)}, u32[]{:S(2)}, u32[]{:S(2)}) collective-permute-start(f32[264,128]{1,0:T(8,128)S(1)} %get-tuple-element.329), channel_id=1, source_target_pairs={{0,8},{4,12},{8,16},{12,20},{16,24},{20,28},{24,0},{28,4},{1,9},{5... | collective-permute-start | bytes 405512 | tf_op jit(solution)/shard_map/ppermute | solution.py:202
  228.7 15.2 %collective-permute-start.66 = (f32[264,128]{1,0:T(8,128)S(1)}, f32[264,128]{1,0:T(8,128)S(1)}, u32[]{:S(2)}, u32[]{:S(2)}) collective-permute-start(f32[264,128]{1,0:T(8,128)S(1)} %get-tuple-element.330), channel_id=1, source_target_pairs={{0,4},{4,8},{8,12},{12,16},{16,20},{20,24},{24,28},{28,0},{1,5},{5... | collective-permute-start | bytes 405512 | tf_op jit(solution)/shard_map/ppermute | solution.py:202
  (33 other events, 303.6 us)

commit v4 on v0

--- a/solution.py
+++ b/solution.py
@@ -2,11 +2,14 @@
 
 import jax
 import jax.numpy as jnp
+import numpy as np
 from jax import lax
+from jax.experimental import pallas as pl
+from jax.experimental.pallas import tpu as pltpu
 from jax.sharding import PartitionSpec as P
 
+
 spacing = 1.0
-highest = lax.Precision.HIGHEST
 pbe_kappa = 0.804
 pbe_mu = 0.2195149727645171
 pbe_beta = 0.06672455060314922
@@ -17,6 +20,608 @@
 pw_second = 3.5876
 pw_third = 1.6382
 pw_fourth = 0.49294
+
+GRANT = 16 << 20
+LANES = 128
+CHUNKS = 4
+CHIPS = 4
+ROWS = 8
+
+
+def deriv_matrix(count):
+    index = np.arange(count)
+    signed = np.where(index < count // 2, index, index - count)
+    signed = np.where(index == count // 2, 0, signed)
+    waves = signed * (2.0 * math.pi / (count * spacing))
+    return np.fft.ifft(1j * waves[:, None] * np.fft.fft(np.eye(count), axis=0), axis=0).real
+
+
+def split_matrix(count):
+    return split_values(deriv_matrix(count))
+
+
+def split_values(matrix):
+    high = matrix.astype(jnp.bfloat16)
+    low = (matrix - high.astype(np.float64)).astype(jnp.bfloat16)
+    return jnp.asarray(high), jnp.asarray(low)
+
+
+def halves(field):
+    high = field.astype(jnp.bfloat16)
+    return high, (field - high.astype(jnp.float32)).astype(jnp.bfloat16)
+
+
+def dot(left, right):
+    return jnp.dot(left, right, preferred_element_type=jnp.float32)
+
+
+def matrix_times(high, low, field):
+    f_high, f_low = halves(field)
+    return dot(high, f_high) + (dot(high, f_low) + dot(low, f_high))
+
+
+def times_matrix(field, high, low):
+    f_high, f_low = halves(field)
+    return dot(f_high, high) + (dot(f_low, high) + dot(f_high, low))
+
+
+def xc_partials(n, g):
+    c_fermi = (3.0 * math.pi**2) ** (1.0 / 3.0)
+    c_wigner = (3.0 / (4.0 * math.pi)) ** (1.0 / 3.0)
+    c_ratio = pbe_beta / pbe_gamma
+    v = jnp.exp(jnp.log(n) * (-1.0 / 6.0))
+    v2 = v * v
+    v4 = v2 * v2
+    n13 = n * v4
+    v8 = v4 * v4
+    v14 = v8 * v4 * v2
+    ex = n13 * (-0.75 * c_fermi / math.pi)
+    s_scale = (v14 * v2) * (1.0 / (4.0 * c_fermi**2))
+    s2 = g * s_scale
+    r_x = 1.0 / (pbe_kappa + pbe_mu * s2)
+    fx = (1.0 + pbe_kappa) - pbe_kappa**2 * r_x
+    dfx = (pbe_mu * pbe_kappa**2) * (r_x * r_x)
+    rs = c_wigner * v2
+    root = math.sqrt(c_wigner) * v
+    q_series = (2.0 * pw_coef) * (
+        root * (pw_first + pw_third * rs) + rs * (pw_second + pw_fourth * rs)
+    )
+    q_slope = (2.0 * pw_coef) * (
+        root * (0.5 * pw_first + 1.5 * pw_third * rs) + rs * (pw_second + (2.0 * pw_fourth) * rs)
+    )
+    r_q = 1.0 / (q_series * (q_series + 1.0))
+    log_q = jnp.log(1.0 + (q_series + 1.0) * r_q)
+    lead = (2.0 * pw_coef) * (1.0 + pw_alpha * rs)
+    ec = -lead * log_q
+    nd = (-1.0 / 3.0) * (lead * q_slope * r_q - (2.0 * pw_coef * pw_alpha) * rs * log_q)
+    t_scale = v14 * (math.pi / (16.0 * c_fermi))
+    t2 = g * t_scale
+    grown = jnp.exp(ec * (-1.0 / pbe_gamma))
+    r_e = 1.0 / (grown - 1.0)
+    factor = c_ratio * r_e
+    q = factor * t2
+    den = 1.0 + q + q * q
+    full = den + c_ratio * t2 * (1.0 + q)
+    r_d = 1.0 / (den * full)
+    h = pbe_gamma * jnp.log(full * full * r_d)
+    h_t = pbe_beta * (1.0 + 2.0 * q) * r_d
+    h_p = (-pbe_beta) * (t2 * t2) * (q * (2.0 + q)) * r_d
+    energy = n * (ex * fx + ec + h)
+    d_grad = n * (ex * dfx * s_scale + h_t * t_scale)
+    d_dens = (
+        ex * ((4.0 / 3.0) * fx - (8.0 / 3.0) * (s2 * dfx))
+        + ec
+        + h
+        + nd * (1.0 + h_p * factor * grown * r_e * (1.0 / pbe_gamma))
+        - (7.0 / 3.0) * t2 * h_t
+    )
+    return energy, d_dens, d_grad
+
+
+def slot(axis, step, size, width):
+    return pl.multiple_of(lax.rem(lax.axis_index(axis) + step, size) * width, width)
+
+
+VMEM = pl.BlockSpec(memory_space=pltpu.VMEM)
+HBM = pl.BlockSpec(memory_space=pltpu.HBM)
+
+
+def call(kernel, ins, outs, scratch=(), flops=1 << 28):
+    return pl.pallas_call(
+        kernel,
+        in_specs=[VMEM] * len(ins),
+        out_specs=[VMEM] * len(outs),
+        out_shape=[jax.ShapeDtypeStruct(o, jnp.float32) for o in outs],
+        scratch_shapes=list(scratch),
+        cost_estimate=pl.CostEstimate(
+            flops=flops,
+            bytes_accessed=sum(4 * math.prod(o) for o in outs) + sum(4 * a.size for a in ins),
+            transcendentals=0,
+        ),
+        compiler_params=pltpu.CompilerParams(vmem_limit_bytes=GRANT),
+    )(*ins)
+
+
+def after(arrays, token):
+    return lax.optimization_barrier((list(arrays), token))[0]
+
+
+class Plan:
+    def __init__(self, shape):
+        self.gx, self.gy = lax.axis_size("gx"), lax.axis_size("gy")
+        self.own, self.ry, self.z = shape
+        self.rows = 2 * self.own
+        self.half = self.z // 2
+        self.yc = self.ry // CHUNKS
+        self.sx = self.rows // self.gy
+
+    @staticmethod
+    def fits(shape, gx, gy):
+        rx, ry, z = shape
+        return (
+            gx == 2 * CHIPS
+            and z == 2 * LANES
+            and ry % (CHUNKS * ROWS) == 0
+            and 2 * rx % (4 * gy) == 0
+            and rx % ROWS == 0
+        )
+
+
+def pairs(chips):
+    return [(2 * a + k, 2 * b + k) for a, b in chips for k in range(2)]
+
+
+INWARD = pairs([(0, 1), (3, 2)])
+ACROSS = pairs([(1, 2), (2, 1)])
+OUTWARD = pairs([(1, 0), (2, 3)])
+NEAR = pairs([(0, 1), (1, 0), (2, 3), (3, 2)])
+FAR = pairs([(0, 3), (3, 0), (1, 2), (2, 1)])
+SWAP = [(i, i ^ 1) for i in range(2 * CHIPS)]
+
+
+def move(array, to):
+    return lax.ppermute(array, "gx", to)
+
+
+def core():
+    return lax.rem(lax.axis_index("gx"), 2)
+
+
+def chip():
+    return lax.div(lax.axis_index("gx"), 2)
+
+
+def is_inner():
+    return jnp.logical_or(chip() == 1, chip() == 2)
+
+
+def at_core(k, width):
+    return pl.ds(pl.multiple_of(k * width, width), width)
+
+
+def assemble(plan, density, far):
+    def kernel(own_ref, far_ref, *refs):
+        outs, semaphore = refs[:-1], refs[-1]
+        copies = []
+        for h in range(2):
+            k = core() if h == 0 else 1 - core()
+            lanes = at_core(k, plan.half)
+            for c in range(CHUNKS):
+                part = (slice(None), pl.ds(c * plan.yc, plan.yc), lanes)
+                out = outs[h * CHUNKS + c]
+                for j, (ref, place) in enumerate(((own_ref, core()), (far_ref, 1 - core()))):
+                    target = out.at[at_core(place, plan.own)]
+                    sem = semaphore.at[(h * CHUNKS + c) * 2 + j]
+                    copies.append(pltpu.make_async_copy(ref.at[part], target, sem))
+        for copy in copies:
+            copy.start()
+        for copy in copies:
+            copy.wait()
+
+    shape = jax.ShapeDtypeStruct((plan.rows, plan.yc, plan.half), jnp.float32)
+    out = pl.pallas_call(
+        kernel,
+        in_specs=[pl.BlockSpec(memory_space=pl.ANY)] * 2,
+        out_specs=[VMEM] * (2 * CHUNKS),
+        out_shape=[shape] * (2 * CHUNKS),
+        scratch_shapes=[pltpu.SemaphoreType.DMA((4 * CHUNKS,))],
+        cost_estimate=pl.CostEstimate(flops=1 << 20, bytes_accessed=1 << 22, transcendentals=0),
+        compiler_params=pltpu.CompilerParams(vmem_limit_bytes=GRANT),
+        name="assemble",
+    )(density, far)
+    return out
+
+
+def pack_y(plan, chunks, stacked=False):
+    def kernel(*refs):
+        ins, outs = refs[:CHUNKS], refs[CHUNKS:]
+        for t, out in enumerate(outs[: plan.gy]):
+            for c, ref in enumerate(ins):
+                rows = pl.ds(slot("gy", t, plan.gy, plan.sx), plan.sx)
+                out[:, c * plan.yc : (c + 1) * plan.yc, :] = ref[rows]
+        if stacked:
+            for c, ref in enumerate(ins):
+                outs[-1][c] = ref[...]
+
+    outs = [(plan.sx, plan.ry, plan.half)] * plan.gy
+    if stacked:
+        outs = outs + [(CHUNKS, plan.rows, plan.yc, plan.half)]
+    return call(kernel, chunks, outs, flops=1 << 20)
+
+
+def join_y(plan, pieces):
+    parts = CHUNKS - 1
+
+    def kernel(*refs):
+        ins, outs = refs[: plan.gy * parts], refs[plan.gy * parts :]
+        for t, out in enumerate(outs):
+            for c in range(parts):
+                out[:, c * plan.yc : (c + 1) * plan.yc, :] = ins[t * parts + c][...]
+
+    outs = [(plan.sx, parts * plan.yc, plan.half)] * plan.gy
+    return call(kernel, pieces, outs, flops=1 << 20)
+
+
+def add(tiles):
+    def kernel(a_ref, b_ref, out_ref):
+        out_ref[...] = a_ref[...] + b_ref[...]
+
+    return call(kernel, tiles, [tiles[0].shape], flops=1 << 10)
+
+
+def stack(plan, chunks):
+    def kernel(*refs):
+        for c in range(CHUNKS):
+            refs[-1][c] = refs[c][...]
+
+    outs = [(CHUNKS, plan.rows, plan.yc, plan.half)]
+    return call(kernel, chunks, outs, flops=1 << 20)
+
+
+def rotate(pieces, axis, size):
+    arrived = [pieces[0]] + [None] * (size - 1)
+    for t in sorted(range(1, size), key=lambda t: abs(2 * t - size)):
+        to = [(i, (i + t) % size) for i in range(size)]
+        arrived[size - t] = lax.ppermute(pieces[t], axis, to)
+    return arrived
+
+
+def ordered_sum(pieces, axis, size, scratch):
+    for t, piece in enumerate(pieces):
+        scratch[pl.ds(slot(axis, t, size, ROWS), ROWS), :] = piece
+    total = scratch[:ROWS, :]
+    for t in range(1, size):
+        total = total + scratch[t * ROWS : (t + 1) * ROWS, :]
+    return total
+
+
+def deriv_x(plan, matrix, pieces, count):
+    rows, yc, lanes = plan.rows, plan.yc, plan.half
+
+    def kernel(high_ref, low_ref, *refs):
+        ins, outs = refs[:CHIPS], refs[CHIPS:]
+        size = CHIPS * rows
+        first = pl.multiple_of(lax.div(chip(), CHIPS // 2) * size, size)
+        high = high_ref[pl.ds(first, count * rows), :]
+        low = low_ref[pl.ds(first, count * rows), :]
+        for y in range(0, yc, 2):
+            columns = [
+                jnp.concatenate([p[pl.ds(y + k, rows, stride=yc), :] for p in ins], axis=0)
+                for k in range(2)
+            ]
+            result = matrix_times(high, low, jnp.concatenate(columns, axis=1))
+            for k in range(2):
+                for t, out in enumerate(outs):
+                    out[pl.ds(y + k, rows, stride=yc), :] = result[
+                        t * rows : (t + 1) * rows, k * lanes : (k + 1) * lanes
+                    ]
+
+    flat = [p.reshape(rows * yc, lanes) for p in pieces]
+    out = call(kernel, [*flat[:0], *matrix, *flat], [(rows * yc, lanes)] * count)
+    return [o.reshape(rows, yc, lanes) for o in out]
+
+
+def deriv_y(plan, matrix, pieces, with_energy=False):
+    gy, sx, ry, lanes = plan.gy, plan.sx, plan.ry, plan.half
+    parts = len(pieces[0])
+
+    def kernel(high_ref, low_ref, *refs):
+        ins, outs = refs[: gy * parts], refs[gy * parts : gy * parts + gy]
+        high, low = high_ref[...], low_ref[...]
+
+        def step(group, carry):
+            for x in (4 * group, 4 * group + 2):
+                columns = [jnp.concatenate([p[x + k] for p in ins], axis=0) for k in range(2)]
+                result = matrix_times(high, low, jnp.concatenate(columns, axis=1))
+                for k in range(2):
+                    for t, out in enumerate(outs):
+                        out[x + k] = result[t * ry : (t + 1) * ry, k * lanes : (k + 1) * lanes]
+            return carry
+
+        lax.fori_loop(0, sx // 4, step, 0)
+        if with_energy:
+            energy_ref, ordered = refs[gy * parts + gy :]
+            tiles = [ins[t * parts + parts - 1][sx, :ROWS, :] for t in range(gy)]
+            energy_ref[...] = ordered_sum(tiles, "gy", gy, ordered)
+
+    outs, scratch = [(sx, ry, lanes)] * gy, []
+    if with_energy:
+        outs = outs + [(ROWS, lanes)]
+        scratch = [pltpu.VMEM((gy * ROWS, lanes), jnp.float32)]
+    return call(kernel, [*matrix, *[c for p in pieces for c in p]], outs, scratch)
+
+
+def deriv_z(plan, matrix, chunks, others, terms=None):
+    rows, lanes, count = plan.rows * plan.yc, plan.half, len(chunks)
+    stacked = len(others) == 1
+    given = count + len(others)
+
+    def kernel(high_ref, low_ref, *refs):
+        outs = refs[-count:]
+        for c in range(count):
+            other = refs[count][c] if stacked else refs[count + c][...]
+            field = jnp.concatenate([refs[c][...], other], axis=1)
+            result = -times_matrix(field, high_ref[:, :lanes], low_ref[:, :lanes])
+            outs[c][...] = result if terms is None else refs[given + c][...] - result
+
+    ins = [a.reshape(rows, lanes) for a in chunks]
+    ins += [a.reshape(*a.shape[: a.ndim - 3], rows, lanes) for a in others]
+    ins += [a.reshape(rows, lanes) for a in terms or []]
+    out = call(kernel, [*matrix, *ins], [(rows, lanes)] * count)
+    return [o.reshape(plan.rows, plan.yc, lanes) for o in out]
+
+
+def pointwise(plan, chunk, dens, grad_z, grad_y, grad_x, mirror, before):
+    gy, rows, yc, sx, lanes = plan.gy, plan.rows, plan.yc, plan.sx, plan.half
+    last = chunk == CHUNKS - 1
+    extra = 1 if last else 0
+    ins = [dens, grad_z, *grad_y, *grad_x] + ([] if before is None else [before])
+
+    def kernel(*refs):
+        n_ref, gz_ref = refs[:2]
+        gy_refs = refs[2 : 2 + gy]
+        gx_refs = refs[2 + gy : 2 + gy + len(grad_x)]
+        outs = refs[len(ins) :]
+        fx_ref = outs[0]
+        if not mirror:
+            fy_refs, (fz_ref, dd_ref, energy_ref) = outs[1 : 1 + gy], outs[1 + gy :]
+            inner_chip = is_inner()
+        total = jnp.zeros((ROWS, lanes), jnp.float32)
+
+        def step(inner, total):
+            for part in range(gy):
+                x = slot("gy", part, gy, sx) + inner
+                for y in range(0, yc, ROWS):
+                    local = pl.ds(y, ROWS)
+                    n = n_ref[x, local, :]
+                    d_x = gx_refs[0][x, local, :]
+                    if not mirror:
+                        d_x = jnp.where(inner_chip, d_x, gx_refs[1][x, local, :])
+                    d_y = gy_refs[part][inner, pl.ds(chunk * yc + y, ROWS), :]
+                    d_z = gz_ref[x, local, :]
+                    f, d_dens, d_grad = xc_partials(n, d_x * d_x + d_y * d_y + d_z * d_z)
+                    twice = 2.0 * d_grad
+                    fx_ref[x, local, :] = twice * d_x
+                    if not mirror:
+                        fy_refs[part][inner, local, :] = twice * d_y
+                        fz_ref[x, local, :] = twice * d_z
+                        dd_ref[x, local, :] = d_dens
+                        total = total + f
+            return total
+
+        total = lax.fori_loop(0, sx, step, total)
+        if not mirror:
+            if before is not None:
+                total = total + refs[len(ins) - 1][...]
+            if last:
+                for out in fy_refs:
+                    out[sx] = jnp.zeros((yc, lanes), jnp.float32)
+                    out[sx, :ROWS, :] = total
+            energy_ref[...] = total
+
+    block = (rows, yc, lanes)
+    outs = [block]
+    if not mirror:
+        outs += [(sx + extra, yc, lanes)] * gy + [block] * 2 + [(ROWS, lanes)]
+    return call(kernel, ins, outs, flops=1 << 30)
+
+
+def finish(plan, chunk, base, div_y, div_x):
+    gy, rows, yc, sx, lanes, own = plan.gy, plan.rows, plan.yc, plan.sx, plan.half, plan.own
+
+    def kernel(base_ref, *refs):
+        y_refs, (inner_ref, outer_ref, keep_ref, give_ref, full) = refs[:gy], refs[gy:]
+        own_y = slice(chunk * yc, (chunk + 1) * yc)
+        inner_chip = is_inner()
+        for t in range(gy):
+            part = pl.ds(slot("gy", t, gy, sx), sx)
+            d_x = jnp.where(inner_chip, inner_ref[part], outer_ref[part])
+            full[part] = base_ref[part] - (d_x + y_refs[t][:, own_y, :])
+        keep_ref[...] = full[at_core(core(), own)]
+        give_ref[...] = full[at_core(1 - core(), own)]
+
+    scratch = [pltpu.VMEM((rows, yc, lanes), jnp.float32)]
+    ins = [base, *div_y, *div_x]
+    return call(kernel, ins, [(own, yc, lanes)] * 2, scratch, flops=1 << 24)
+
+
+def place(plan, kept, given, energies, scale):
+    yc, half = plan.yc, plan.half
+    count = 2 * CHUNKS
+
+    def kernel(*refs):
+        ins, tiles = refs[:count], refs[count : count + 2]
+        out_ref, energy_ref, semaphore = refs[count + 2 :]
+        copies = []
+        for j, ref in enumerate(ins):
+            c, k = j % CHUNKS, core() if j < CHUNKS else 1 - core()
+            target = out_ref.at[:, pl.ds(c * yc, yc), at_core(k, half)]
+            copies.append(pltpu.make_async_copy(ref, target, semaphore.at[j]))
+        for copy in copies:
+            copy.start()
+        energy_ref[0, 0] = jnp.sum(tiles[0][...] + tiles[1][...]) * scale
+        for copy in copies:
+            copy.wait()
+
+    return pl.pallas_call(
+        kernel,
+        in_specs=[VMEM] * (count + 2),
+        out_specs=[pl.BlockSpec(memory_space=pl.ANY), pl.BlockSpec(memory_space=pltpu.SMEM)],
+        out_shape=[
+            jax.ShapeDtypeStruct((plan.own, plan.ry, plan.z), jnp.float32),
+            jax.ShapeDtypeStruct((1, 1), jnp.float32),
+        ],
+        scratch_shapes=[pltpu.SemaphoreType.DMA((count,))],
+        cost_estimate=pl.CostEstimate(flops=1 << 20, bytes_accessed=1 << 22, transcendentals=0),
+        compiler_params=pltpu.CompilerParams(vmem_limit_bytes=GRANT),
+        name="place",
+    )(*kept, *given, *energies)
+
+
+def body(density):
+    return tiled_body(density)
+
+
+def inner_matrices(plan):
+    matrix = deriv_matrix(plan.own * plan.gx)
+    found = []
+    for order in ((1, 0, 2, 3), (2, 3, 1, 0)):
+        index = np.concatenate([np.arange(plan.rows) + plan.rows * o for o in order])
+        found.append(matrix[index][:, index])
+    return split_values(np.concatenate(found))
+
+
+def tiled_body(density):
+    plan = Plan(density.shape)
+    gx, gy = plan.gx, plan.gy
+    matrix_x = inner_matrices(plan)
+    matrix_y, matrix_z = split_matrix(plan.ry * gy), split_matrix(plan.z)
+    token = None
+    chunks = range(CHUNKS)
+
+    def run(kernel, arrays, *args, **kwargs):
+        nonlocal token
+        if token is not None:
+            arrays = after(arrays, token)
+        out = kernel(arrays, *args, **kwargs)
+        token = out[0]
+        return out
+
+    far = move(density, SWAP)
+    out = run(lambda a: assemble(plan, *a), [density, far])
+    dens, other = out[:CHUNKS], out[CHUNKS:]
+    mirror, outer, beyond = [], [], []
+    for c in chunks:
+        mirror.append(move(dens[c], ACROSS))
+        outer.append(move(dens[c], INWARD))
+    out = run(lambda a: pack_y(plan, a), dens)
+    dens_y = rotate(out, "gy", gy)
+    grad_z, early = [], CHUNKS // 2
+    for part in (chunks[:early], chunks[early:]):
+        arrays = [dens[c] for c in part] + [other[c] for c in part]
+        grad_z += run(lambda a: deriv_z(plan, matrix_z, a[: len(a) // 2], a[len(a) // 2 :]), arrays)
+    beyond = [move(outer[c], ACROSS) for c in chunks]
+    out = run(lambda a: deriv_y(plan, matrix_y, [[p] for p in a]), dens_y)
+    grad_y = rotate(out, "gy", gy)
+    grad_x, flux, relay, mirror_f, div_x = {}, {}, {}, {}, {}
+
+    def gradient_x(c):
+        pieces = [dens[c], outer[c], mirror[c], beyond[c]]
+        own, out_, mirrored = run(lambda a: deriv_x(plan, matrix_x, a, 3), pieces)
+        return (own, move(out_, OUTWARD)), mirrored
+
+    grad_x[0] = gradient_x(0)
+
+    energy = None
+
+    def point(c):
+        nonlocal energy
+        arrays = [dens[c], grad_z[c], *grad_y, *grad_x[c][0]]
+        f_x, *out = run(
+            lambda a: pointwise(
+                plan, c, a[0], a[1], a[2 : 2 + gy], a[2 + gy :], False, energy
+            ),
+            arrays,
+        )
+        energy = out[-1]
+        f_z, part = out[gy], out[gy + 1]
+        inward = move(f_x, INWARD)
+        return dict(x=f_x, outer=inward, y=out[:gy], z=f_z, d=part)
+
+    def mirrored_point(c):
+        arrays = [mirror[c], mirror_gz[c], *mirror_gy, grad_x[c][1]]
+        return run(
+            lambda a: pointwise(plan, c, a[0], a[1], a[2 : 2 + gy], a[2 + gy :], True, None), arrays
+        )[0]
+
+    def relay_on(c):
+        relay[c] = move(flux[c]["outer"], ACROSS)
+
+    def divergence_x(c):
+        pieces = [flux[c]["x"], flux[c]["outer"], mirror_f[c], relay[c]]
+        own, out_ = run(lambda a: deriv_x(plan, matrix_x, a, 2), pieces)
+        div_x[c] = own, move(out_, OUTWARD)
+
+    flux[0] = point(0)
+    *out, both = run(lambda a: pack_y(plan, a, True), mirror)
+    mirror_y = rotate(out, "gy", gy)
+    mirror_other = move(both, SWAP)
+    grad_x[1] = gradient_x(1)
+    mirror_gz = run(
+        lambda a: deriv_z(plan, matrix_z, a[:CHUNKS], a[CHUNKS:]), [*mirror, mirror_other]
+    )
+    grad_x[2] = gradient_x(2)
+    flux[1] = point(1)
+    relay_on(0)
+    out = run(lambda a: deriv_y(plan, matrix_y, [[p] for p in a]), mirror_y)
+    mirror_gy = rotate(out, "gy", gy)
+    grad_x[3] = gradient_x(3)
+    flux[2] = point(2)
+    relay_on(1)
+    flat = [flux[c]["y"][t] for t in range(gy) for c in chunks[:-1]]
+    early = rotate(run(lambda a: join_y(plan, a), flat), "gy", gy)
+    flux[3] = point(3)
+    relay_on(2)
+    mirror_f[0] = mirrored_point(0)
+    divergence_x(0)
+    mirror_f[1] = mirrored_point(1)
+    divergence_x(1)
+    relay_on(3)
+    mirror_f[2] = mirrored_point(2)
+    late = rotate(flux[CHUNKS - 1]["y"], "gy", gy)
+    flat = [p for pair in zip(early, late) for p in pair]
+    *out, energy = run(
+        lambda a: deriv_y(plan, matrix_y, [a[2 * t : 2 * t + 2] for t in range(gy)], True), flat
+    )
+    div_y = rotate(out, "gy", gy)
+    tiles = [energy, move(energy, SWAP)]
+    divergence_x(2)
+    (both,) = run(lambda a: stack(plan, a), [flux[c]["z"] for c in chunks])
+    flux_other = move(both, SWAP)
+    mirror_f[3] = mirrored_point(3)
+    (energy,) = run(add, tiles)
+    tiles = [energy, move(energy, NEAR)]
+    divergence_x(3)
+    base = run(
+        lambda a: deriv_z(plan, matrix_z, a[:CHUNKS], a[CHUNKS : CHUNKS + 1], a[CHUNKS + 1 :]),
+        [flux[c]["z"] for c in chunks] + [flux_other] + [flux[c]["d"] for c in chunks],
+    )
+    (energy,) = run(add, tiles)
+    tiles = [energy, move(energy, FAR)]
+    kept, given = [], []
+    for c in chunks:
+        keep, give = run(
+            lambda a, c=c: finish(plan, c, a[0], a[1 : 1 + gy], a[1 + gy :]),
+            [base[c], *div_y, *div_x[c]],
+        )
+        kept.append(keep)
+        given.append(move(give, SWAP))
+    scale = 1.0 / float(plan.own * gx * plan.ry * gy * plan.z)
+    done, energy = run(
+        lambda a: place(plan, a[:CHUNKS], a[CHUNKS : 2 * CHUNKS], a[2 * CHUNKS :], scale),
+        [*kept, *given, *tiles],
+    )
+    return done, energy[0, 0]
 
 
 def xc_energy(electrons, grad_sq):
@@ -69,34 +674,34 @@
     return (jnp.cos(phase), jnp.sin(phase))
 
 
-def deriv_matrix(count):
+def plain_matrix(count):
     positions = jnp.arange(count, dtype=jnp.int32)
     cosine, sine = dft_tables(count, positions)
     waves = wavenum(positions, count)
-    first = jnp.dot(cosine.T * waves[None, :], sine, precision=highest)
-    second = jnp.dot(sine.T * waves[None, :], cosine, precision=highest)
+    first = jnp.dot(cosine.T * waves[None, :], sine, precision=lax.Precision.HIGHEST)
+    second = jnp.dot(sine.T * waves[None, :], cosine, precision=lax.Precision.HIGHEST)
     return (first - second) / float(count)
 
 
-def body(density):
+def plain_body(density):
     count_gx = lax.axis_size("gx")
     count_gy = lax.axis_size("gy")
     rows_x, rows_y, count_z = density.shape
     count_x = rows_x * count_gx
     count_y = rows_y * count_gy
-    deriv_x = deriv_matrix(count_x)
-    deriv_y = deriv_matrix(count_y)
-    deriv_z = deriv_matrix(count_z)
+    deriv_x = plain_matrix(count_x)
+    deriv_y = plain_matrix(count_y)
+    deriv_z = plain_matrix(count_z)
 
     def line_x(piece):
         flat = piece.reshape(piece.shape[0], piece.shape[1] * piece.shape[2])
-        result = jnp.dot(deriv_x, flat, precision=highest)
+        result = jnp.dot(deriv_x, flat, precision=lax.Precision.HIGHEST)
         return result.reshape(piece.shape)
 
     def line_y(piece):
         turned = jnp.swapaxes(piece, 0, 1)
         flat = turned.reshape(turned.shape[0], turned.shape[1] * turned.shape[2])
-        result = jnp.dot(deriv_y, flat, precision=highest).reshape(turned.shape)
+        result = jnp.dot(deriv_y, flat, precision=lax.Precision.HIGHEST).reshape(turned.shape)
         return jnp.swapaxes(result, 0, 1)
 
     def along_x(field):
@@ -109,7 +714,7 @@
 
     def along_z(field):
         flat = field.reshape(field.shape[0] * field.shape[1], field.shape[2])
-        result = jnp.dot(flat, deriv_z.T, precision=highest)
+        result = jnp.dot(flat, deriv_z.T, precision=lax.Precision.HIGHEST)
         return result.reshape(field.shape)
 
     gradients = [along_x(density), along_y(density), along_z(density)]
@@ -127,4 +732,18 @@
 def solution(mesh):
     in_specs = (P("gx", "gy", None),)
     out_specs = (P("gx", "gy", None), P())
-    return jax.shard_map(body, mesh=mesh, in_specs=in_specs, out_specs=out_specs, check_vma=False)
+
+    def run(density):
+        gx, gy = mesh.shape["gx"], mesh.shape["gy"]
+        x, y, z = density.shape
+        tiled = Plan.fits((x // gx, y // gy, z), gx, gy)
+        step = jax.shard_map(
+            body if tiled else plain_body,
+            mesh=mesh,
+            in_specs=in_specs,
+            out_specs=out_specs,
+            check_vma=False,
+        )
+        return step(density)
+
+    return run

time: 543 us -> 293 us (0.54); the launches traced: 537 us -> 293 us
  local copies, waits for them, and re-layouts: 230 us -> 1.62 us
  other arithmetic: 95 us -> 0 us
  waiting for transfers between devices: 56.8 us -> 138 us
  blocking collectives: 69.7 us -> 0 us
  starting transfers between devices: 37.4 us -> 105 us
  Pallas kernels: 0 us -> 46.3 us
  matrix products: 44.7 us -> 0 us
    ppermute x0 -> x59, waiting for transfers between devices: none -> 138 us  [the longest x38 85.8 us: move(): return lax.ppermute(array, 'gx', to)]
    ppermute x0 -> x59, starting transfers between devices: none -> 105 us  [the longest x38 72.1 us: move(): return lax.ppermute(array, 'gx', to)]
    unnamed x25 -> x10, local copies, waits for them, and re-layouts: 96 us -> 1.62 us
    all_to_all x15 -> x0, local copies, waits for them, and re-layouts: 80 us -> none  [the longest x4 24.6 us: along_y(): return lax.all_to_all(lines, 'gy', split_axis=1, concat_axis=2, tiled=True)]
    psum x1 -> x0, blocking collectives: 69.7 us -> none  [total_energy(): return lax.psum(energy_local, ('gx', 'gy')) / float(cells)]
    all_to_all x8 -> x0, other arithmetic: 67.5 us -> none  [the longest x2 18 us: along_y(): return lax.all_to_all(lines, 'gy', split_axis=1, concat_axis=2, tiled=True)]
    all_to_all x8 -> x0, waiting for transfers between devices: 56.8 us -> none  [the longest x2 26.2 us: along_y(): lax.all_to_all(field, 'gy', split_axis=2, concat_axis=1, tiled=True)]
    pallas_call x0 -> x35, Pallas kernels: none -> 46.3 us  [the longest x33 43.9 us: call(): pl.pallas_call(kernel, in_specs=[VMEM] * len(ins), out_specs=[VMEM] * len...]
  transfers between devices with their start and end apart: 8 -> 59, of which waited for: 5 -> 23; matrix products, arithmetic and copies ran while one was open for 44% -> 0% of each run, Pallas kernels for 0% -> 14%
where the time goes in v4:
time: 293 us
  waiting for transfers between devices  138 us (47%)
  starting transfers between devices  105 us (36%)
  Pallas kernels  46.3 us (16%)
    ppermute x38, waiting for transfers between devices, move(): return lax.ppermute(array, 'gx', to)  85.8 us
    ppermute x38, starting transfers between devices, move(): return lax.ppermute(array, 'gx', to)  72.1 us
    ppermute x21, waiting for transfers between devices, rotate(): arrived[size - t] = lax.ppermute(pieces[t], axis, to)  52.5 us
    pallas_call x33, Pallas kernels, call(): pl.pallas_call(kernel, in_specs=[VMEM] * len(ins), out_specs=[VMEM] * len...  43.9 us
    ppermute x21, starting transfers between devices, rotate(): arrived[size - t] = lax.ppermute(pieces[t], axis, to)  32.7 us
  transfers between devices with their start and end apart: 59, of which 23 were waited for; matrix products, arithmetic and copies ran while one was open for 0% of the time, Pallas kernels for 14%

profile of v4, /device:TPU:0, one launch (start us, length us, event | category | flops | bytes accessed | tf_op | source)
XLA Modules:
  0.0 292.5 jit_solution(1457374570800951426)
XLA Ops:
  1.2 4.0 %collective-permute-done.far_ref = f32[32,64,256]{2,1,0:T(8,128)S(1)} collective-permute-done((f32[32,64,256]{2,1,0:T(8,128)}, f32[32,64,256]{2,1,0:T(8,128)S(1)}, u32[]{:S(2)}, u32[]{:S(2)}) %collective-permute-start) | collective-permute-done | bytes 2097184 | tf_op jit(solution)/shard_map/ppermute | solution.py:183
  7.3 5.0 %collective-permute-start.7 = (f32[64,16,128]{2,1,0:T(8,128)S(1)}, f32[64,16,128]{2,1,0:T(8,128)S(1)}, u32[]{:S(2)}, u32[]{:S(2)}) collective-permute-start(f32[64,16,128]{2,1,0:T(8,128)S(1)} %get-tuple-element.345.refs_0_), channel_id=1, source_target_pairs={{0,8},{4,12},{24,16},{28,20},{1,9},{5,13},{25,17},{29,21},{2,10},{... | collective-permute-start | bytes 1572872 | tf_op jit(solution)/shard_map/ppermute | solution.py:183
  12.5 2.5 collective-permute-start.1
  16.8 7.0 %collective-permute-done.7 = f32[64,16,128]{2,1,0:T(8,128)S(1)} collective-permute-done((f32[64,16,128]{2,1,0:T(8,128)S(1)}, f32[64,16,128]{2,1,0:T(8,128)S(1)}, u32[]{:S(2)}, u32[]{:S(2)}) %collective-permute-start.7) | collective-permute-done | bytes 524320 | tf_op jit(solution)/shard_map/ppermute | solution.py:183
  27.3 12.3 %collective-permute-done.2.refs_2_ = f32[16,64,128]{2,1,0:T(8,128)S(1)} collective-permute-done((f32[16,64,128]{2,1,0:T(8,128)S(1)}, f32[16,64,128]{2,1,0:T(8,128)S(1)}, u32[]{:S(2)}, u32[]{:S(2)}) %collective-permute-start.2) | collective-permute-done | bytes 524320 | tf_op jit(solution)/shard_map/ppermute | solution.py:285
  43.8 1.6 shard_map.90
  47.5 8.6 %collective-permute-done.4.refs_3_ = f32[16,64,128]{2,1,0:T(8,128)S(1)} collective-permute-done((f32[16,64,128]{2,1,0:T(8,128)S(1)}, f32[16,64,128]{2,1,0:T(8,128)S(1)}, u32[]{:S(2)}, u32[]{:S(2)}) %collective-permute-start.4) | collective-permute-done | bytes 524320 | tf_op jit(solution)/shard_map/ppermute | solution.py:285
  56.7 9.2 %collective-permute-done.5.refs_4_ = f32[16,64,128]{2,1,0:T(8,128)S(1)} collective-permute-done((f32[16,64,128]{2,1,0:T(8,128)S(1)}, f32[16,64,128]{2,1,0:T(8,128)S(1)}, u32[]{:S(2)}, u32[]{:S(2)}) %collective-permute-start.5) | collective-permute-done | bytes 524320 | tf_op jit(solution)/shard_map/ppermute | solution.py:285
  66.7 2.9 %shard_map.91 = (f32[64,16,128]{2,1,0:T(8,128)S(1)}, f32[16,16,128]{2,1,0:T(8,128)S(1)}, f32[16,16,128]{2,1,0:T(8,128)S(1)}, f32[16,16,128]{2,1,0:T(8,128)S(1)},...) custom-call(f32[64,16,128]{2,1,0:T(8,128)S(1)} %get-tuple-element.34, ...), custom_call_target="tpu_custom_call" | custom-call | flops 1073741824 | bytes 6295552 | tf_op jit(solution)/shard_map/pallas_call | solution.py:130
  70.0 17.4 %collective-permute-start.11 = (f32[64,16,128]{2,1,0:T(8,128)S(1)}, f32[64,16,128]{2,1,0:T(8,128)S(1)}, u32[]{:S(2)}, u32[]{:S(2)}) collective-permute-start(f32[64,16,128]{2,1,0:T(8,128)S(1)} %get-tuple-element.379.refs_1_.refs_0_), channel_id=1, source_target_pairs={{0,8},{4,12},{24,16},{28,20},{1,9},{5,13},{25,17},{29,21},{2,10},{... | collective-permute-start | bytes 1572872 | tf_op jit(solution)/shard_map/ppermute | solution.py:183
  88.7 10.9 %collective-permute-done.11 = f32[64,16,128]{2,1,0:T(8,128)S(1)} collective-permute-done((f32[64,16,128]{2,1,0:T(8,128)S(1)}, f32[64,16,128]{2,1,0:T(8,128)S(1)}, u32[]{:S(2)}, u32[]{:S(2)}) %collective-permute-start.11) | collective-permute-done | bytes 524320 | tf_op jit(solution)/shard_map/ppermute | solution.py:183
  100.3 7.2 %collective-permute-start.21 = (f32[64,16,128]{2,1,0:T(8,128)S(1)}, f32[64,16,128]{2,1,0:T(8,128)S(1)}, u32[]{:S(2)}, u32[]{:S(2)}) collective-permute-start(f32[64,16,128]{2,1,0:T(8,128)S(1)} %get-tuple-element.442.refs_3_.refs_0_), channel_id=1, source_target_pairs={{0,8},{4,12},{24,16},{28,20},{1,9},{5,13},{25,17},{29,21},{2,10},{... | collective-permute-start | bytes 1572872 | tf_op jit(solution)/shard_map/ppermute | solution.py:183
  107.6 3.3 %collective-permute-done.17 = f32[64,16,128]{2,1,0:T(8,128)S(1)} collective-permute-done((f32[64,16,128]{2,1,0:T(8,128)S(1)}, f32[64,16,128]{2,1,0:T(8,128)S(1)}, u32[]{:S(2)}, u32[]{:S(2)}) %collective-permute-start.17) | collective-permute-done | bytes 524320 | tf_op jit(solution)/shard_map/ppermute | solution.py:183
  111.6 1.6 shard_map.93
  114.5 2.7 collective-permute-start.23
  117.2 4.4 %collective-permute-done.21 = f32[64,16,128]{2,1,0:T(8,128)S(1)} collective-permute-done((f32[64,16,128]{2,1,0:T(8,128)S(1)}, f32[64,16,128]{2,1,0:T(8,128)S(1)}, u32[]{:S(2)}, u32[]{:S(2)}) %collective-permute-start.21) | collective-permute-done | bytes 524320 | tf_op jit(solution)/shard_map/ppermute | solution.py:183
  121.6 4.4 %collective-permute-start.32 = (f32[64,16,128]{2,1,0:T(8,128)S(1)}, f32[64,16,128]{2,1,0:T(8,128)S(1)}, u32[]{:S(2)}, u32[]{:S(2)}) collective-permute-start(f32[64,16,128]{2,1,0:T(8,128)S(1)} %get-tuple-element.468), channel_id=1, source_target_pairs={{0,8},{4,12},{24,16},{28,20},{1,9},{5,13},{25,17},{29,21},{2,10},{... | collective-permute-start | bytes 1572872 | tf_op jit(solution)/shard_map/ppermute | solution.py:183
  127.2 3.5 %collective-permute-done.16.refs_7_ = f32[64,16,128]{2,1,0:T(8,128)S(1)} collective-permute-done((f32[64,16,128]{2,1,0:T(8,128)S(1)}, f32[64,16,128]{2,1,0:T(8,128)S(1)}, u32[]{:S(2)}, u32[]{:S(2)}) %collective-permute-start.16) | collective-permute-done | bytes 524320 | tf_op jit(solution)/shard_map/ppermute | solution.py:183
  130.7 2.3 collective-permute-start.25
  133.7 1.8 shard_map.94
  135.5 1.6 shard_map.95
  139.3 2.9 %shard_map.96 = (f32[64,16,128]{2,1,0:T(8,128)S(1)}, f32[16,16,128]{2,1,0:T(8,128)S(1)}, f32[16,16,128]{2,1,0:T(8,128)S(1)}, f32[16,16,128]{2,1,0:T(8,128)S(1)},...) custom-call(f32[64,16,128]{2,1,0:T(8,128)S(1)} %get-tuple-element.37, ...), custom_call_target="tpu_custom_call" | custom-call | flops 1073741824 | bytes 6299648 | tf_op jit(solution)/shard_map/pallas_call | solution.py:130
  142.3 8.3 %collective-permute-done.24.refs_2_ = f32[16,64,128]{2,1,0:T(8,128)S(1)} collective-permute-done((f32[16,64,128]{2,1,0:T(8,128)S(1)}, f32[16,64,128]{2,1,0:T(8,128)S(1)}, u32[]{:S(2)}, u32[]{:S(2)}) %collective-permute-start.24) | collective-permute-done | bytes 524320 | tf_op jit(solution)/shard_map/ppermute | solution.py:285
  152.1 1.6 shard_map.98
  155.1 4.6 %collective-permute-start.31 = (f32[64,16,128]{2,1,0:T(8,128)S(1)}, f32[64,16,128]{2,1,0:T(8,128)S(1)}, u32[]{:S(2)}, u32[]{:S(2)}) collective-permute-start(f32[64,16,128]{2,1,0:T(8,128)S(1)} %get-tuple-element.480), channel_id=1, source_target_pairs={{0,8},{4,12},{24,16},{28,20},{1,9},{5,13},{25,17},{29,21},{2,10},{... | collective-permute-start | bytes 1572872 | tf_op jit(solution)/shard_map/ppermute | solution.py:183
  160.9 2.9 shard_map.99
  165.2 2.8 collective-permute-done.26.refs_7_
  168.0 4.0 %collective-permute-done.31 = f32[64,16,128]{2,1,0:T(8,128)S(1)} collective-permute-done((f32[64,16,128]{2,1,0:T(8,128)S(1)}, f32[64,16,128]{2,1,0:T(8,128)S(1)}, u32[]{:S(2)}, u32[]{:S(2)}) %collective-permute-start.31) | collective-permute-done | bytes 524320 | tf_op jit(solution)/shard_map/ppermute | solution.py:183
  172.7 3.6 %shard_map.101 = (f32[64,16,128]{2,1,0:T(8,128)S(1)}, f32[17,16,128]{2,1,0:T(8,128)S(1)}, f32[17,16,128]{2,1,0:T(8,128)S(1)}, f32[17,16,128]{2,1,0:T(8,128)S(1)}...) custom-call(f32[64,16,128]{2,1,0:T(8,128)S(1)} %get-tuple-element.442., ...), custom_call_target="tpu_custom_call" | custom-call | flops 1073741824 | bytes 6332416 | tf_op jit(solution)/shard_map/pallas_call | solution.py:130
  177.5 2.9 %collective-permute-done.27 = f32[64,16,128]{2,1,0:T(8,128)S(1)} collective-permute-done((f32[64,16,128]{2,1,0:T(8,128)S(1)}, f32[64,16,128]{2,1,0:T(8,128)S(1)}, u32[]{:S(2)}, u32[]{:S(2)}) %collective-permute-start.27) | collective-permute-done | bytes 524320 | tf_op jit(solution)/shard_map/ppermute | solution.py:183
  181.1 3.7 %collective-permute-done.30.refs_5_ = f32[16,64,128]{2,1,0:T(8,128)S(1)} collective-permute-done((f32[16,64,128]{2,1,0:T(8,128)S(1)}, f32[16,64,128]{2,1,0:T(8,128)S(1)}, u32[]{:S(2)}, u32[]{:S(2)}) %collective-permute-start.30) | collective-permute-done | bytes 524320 | tf_op jit(solution)/shard_map/ppermute | solution.py:285
  184.8 2.5 collective-permute-start.36
  188.2 11.8 %collective-permute-start.40 = (f32[16,48,128]{2,1,0:T(8,128)S(1)}, f32[16,48,128]{2,1,0:T(8,128)S(1)}, u32[]{:S(2)}, u32[]{:S(2)}) collective-permute-start(f32[16,48,128]{2,1,0:T(8,128)S(1)} %get-tuple-element.497), channel_id=1, source_target_pairs={{0,1},{1,2},{2,3},{3,0},{4,5},{5,6},{6,7},{7,4},{8,9},{9,10},{10,1... | collective-permute-start | bytes 1179656 | tf_op jit(solution)/shard_map/ppermute | solution.py:285
  200.0 2.0 shard_map.102
  203.5 2.1 shard_map.104
  206.9 2.0 shard_map.106
  209.4 1.6 shard_map.107
  212.6 3.8 %collective-permute-start.43 = (f32[64,16,128]{2,1,0:T(8,128)S(1)}, f32[64,16,128]{2,1,0:T(8,128)S(1)}, u32[]{:S(2)}, u32[]{:S(2)}) collective-permute-start(f32[64,16,128]{2,1,0:T(8,128)S(1)} %get-tuple-element.533), channel_id=1, source_target_pairs={{0,8},{4,12},{24,16},{28,20},{1,9},{5,13},{25,17},{29,21},{2,10},{... | collective-permute-start | bytes 1572872 | tf_op jit(solution)/shard_map/ppermute | solution.py:183
  216.4 11.8 %collective-permute-done.43 = f32[64,16,128]{2,1,0:T(8,128)S(1)} collective-permute-done((f32[64,16,128]{2,1,0:T(8,128)S(1)}, f32[64,16,128]{2,1,0:T(8,128)S(1)}, u32[]{:S(2)}, u32[]{:S(2)}) %collective-permute-start.43) | collective-permute-done | bytes 524320 | tf_op jit(solution)/shard_map/ppermute | solution.py:183
  230.9 2.0 shard_map.110
  233.0 4.9 %collective-permute-start.50 = (f32[8,128]{1,0:T(8,128)S(1)}, f32[8,128]{1,0:T(8,128)S(1)}, u32[]{:S(2)}, u32[]{:S(2)}) collective-permute-start(f32[8,128]{1,0:T(8,128)S(1)} %shard_map.111.a_ref), channel_id=1, source_target_pairs={{0,8},{4,12},{8,0},{12,4},{16,24},{20,28},{24,16},{28,20},{1,9},{5... | collective-permute-start | bytes 12296 | tf_op jit(solution)/shard_map/ppermute | solution.py:183
  238.8 7.0 %collective-permute-done.49.refs_5_ = f32[64,16,128]{2,1,0:T(8,128)S(1)} collective-permute-done((f32[64,16,128]{2,1,0:T(8,128)S(1)}, f32[64,16,128]{2,1,0:T(8,128)S(1)}, u32[]{:S(2)}, u32[]{:S(2)}) %collective-permute-start.49) | collective-permute-done | bytes 524320 | tf_op jit(solution)/shard_map/ppermute | solution.py:183
  252.3 1.8 shard_map.113
  254.2 9.0 %collective-permute-done.47.refs_2_ = f32[16,64,128]{2,1,0:T(8,128)S(1)} collective-permute-done((f32[16,64,128]{2,1,0:T(8,128)S(1)}, f32[16,64,128]{2,1,0:T(8,128)S(1)}, u32[]{:S(2)}, u32[]{:S(2)}) %collective-permute-start.47) | collective-permute-done | bytes 524320 | tf_op jit(solution)/shard_map/ppermute | solution.py:285
  263.7 11.1 %collective-permute-done.52.refs_5_ = f32[64,16,128]{2,1,0:T(8,128)S(1)} collective-permute-done((f32[64,16,128]{2,1,0:T(8,128)S(1)}, f32[64,16,128]{2,1,0:T(8,128)S(1)}, u32[]{:S(2)}, u32[]{:S(2)}) %collective-permute-start.52) | collective-permute-done | bytes 524320 | tf_op jit(solution)/shard_map/ppermute | solution.py:183
  274.9 8.8 %collective-permute-done.53.refs_5_ = f32[64,16,128]{2,1,0:T(8,128)S(1)} collective-permute-done((f32[64,16,128]{2,1,0:T(8,128)S(1)}, f32[64,16,128]{2,1,0:T(8,128)S(1)}, u32[]{:S(2)}, u32[]{:S(2)}) %collective-permute-start.53) | collective-permute-done | bytes 524320 | tf_op jit(solution)/shard_map/ppermute | solution.py:183
  286.5 4.0 %collective-permute-done.58.refs_9_ = f32[8,128]{1,0:T(8,128)S(1)} collective-permute-done((f32[8,128]{1,0:T(8,128)S(1)}, f32[8,128]{1,0:T(8,128)S(1)}, u32[]{:S(2)}, u32[]{:S(2)}) %collective-permute-start.58) | collective-permute-done | bytes 4128 | tf_op jit(solution)/shard_map/ppermute | solution.py:183
  290.5 1.9 place.1
  (115 shorter events, 51.3 us)
Async XLA Ops:
  7.3 16.4 %collective-permute-start.7 = (f32[64,16,128]{2,1,0:T(8,128)S(1)}, f32[64,16,128]{2,1,0:T(8,128)S(1)}, u32[]{:S(2)}, u32[]{:S(2)}) collective-permute-start(f32[64,16,128]{2,1,0:T(8,128)S(1)} %get-tuple-element.345.refs_0_), channel_id=1, source_target_pairs={{0,8},{4,12},{24,16},{28,20},{1,9},{5,13},{25,17},{29,21},{2,10},{... | collective-permute-start | bytes 1572872 | tf_op jit(solution)/shard_map/ppermute | solution.py:183
  12.5 14.9 %collective-permute-start.1 = (f32[16,64,128]{2,1,0:T(8,128)S(1)}, f32[16,64,128]{2,1,0:T(8,128)S(1)}, u32[]{:S(2)}, u32[]{:S(2)}) collective-permute-start(f32[16,64,128]{2,1,0:T(8,128)S(1)} %get-tuple-element.321), channel_id=1, source_target_pairs={{0,3},{1,0},{2,1},{3,2},{4,7},{5,4},{6,5},{7,6},{8,11},{9,8},{10,9... | collective-permute-start | bytes 1572872 | tf_op jit(solution)/shard_map/ppermute | solution.py:285
  15.0 24.6 %collective-permute-start.2 = (f32[16,64,128]{2,1,0:T(8,128)S(1)}, f32[16,64,128]{2,1,0:T(8,128)S(1)}, u32[]{:S(2)}, u32[]{:S(2)}) collective-permute-start(f32[16,64,128]{2,1,0:T(8,128)S(1)} %get-tuple-element.322), channel_id=1, source_target_pairs={{0,2},{1,3},{2,0},{3,1},{4,6},{5,7},{6,4},{7,5},{8,10},{9,11},{10,... | collective-permute-start | bytes 1572872 | tf_op jit(solution)/shard_map/ppermute | solution.py:285
  15.5 24.1 %collective-permute-start.3 = (f32[16,64,128]{2,1,0:T(8,128)S(1)}, f32[16,64,128]{2,1,0:T(8,128)S(1)}, u32[]{:S(2)}, u32[]{:S(2)}) collective-permute-start(f32[16,64,128]{2,1,0:T(8,128)S(1)} %get-tuple-element.323), channel_id=1, source_target_pairs={{0,1},{1,2},{2,3},{3,0},{4,5},{5,6},{6,7},{7,4},{8,9},{9,10},{10,1... | collective-permute-start | bytes 1572872 | tf_op jit(solution)/shard_map/ppermute | solution.py:285
  16.1 27.7 %collective-permute-start.8 = (f32[64,16,128]{2,1,0:T(8,128)S(1)}, f32[64,16,128]{2,1,0:T(8,128)S(1)}, u32[]{:S(2)}, u32[]{:S(2)}) collective-permute-start(f32[64,16,128]{2,1,0:T(8,128)S(1)} %get-tuple-element.345.refs_0_), channel_id=1, source_target_pairs={{8,16},{12,20},{16,8},{20,12},{9,17},{13,21},{17,9},{21,13},{10,18... | collective-permute-start | bytes 1572872 | tf_op jit(solution)/shard_map/ppermute | solution.py:183
  23.8 20.0 %collective-permute-start.9 = (f32[64,16,128]{2,1,0:T(8,128)S(1)}, f32[64,16,128]{2,1,0:T(8,128)S(1)}, u32[]{:S(2)}, u32[]{:S(2)}) collective-permute-start(f32[64,16,128]{2,1,0:T(8,128)S(1)} %collective-permute-done.7), channel_id=1, source_target_pairs={{8,16},{12,20},{16,8},{20,12},{9,17},{13,21},{17,9},{21,13},{10,18... | collective-permute-start | bytes 1572872 | tf_op jit(solution)/shard_map/ppermute | solution.py:183
  41.2 14.8 %collective-permute-start.4 = (f32[16,64,128]{2,1,0:T(8,128)S(1)}, f32[16,64,128]{2,1,0:T(8,128)S(1)}, u32[]{:S(2)}, u32[]{:S(2)}) collective-permute-start(f32[16,64,128]{2,1,0:T(8,128)S(1)} %get-tuple-element.336), channel_id=1, source_target_pairs={{0,3},{1,0},{2,1},{3,2},{4,7},{5,4},{6,5},{7,6},{8,11},{9,8},{10,9... | collective-permute-start | bytes 1572872 | tf_op jit(solution)/shard_map/ppermute | solution.py:285
  41.8 24.2 %collective-permute-start.5 = (f32[16,64,128]{2,1,0:T(8,128)S(1)}, f32[16,64,128]{2,1,0:T(8,128)S(1)}, u32[]{:S(2)}, u32[]{:S(2)}) collective-permute-start(f32[16,64,128]{2,1,0:T(8,128)S(1)} %get-tuple-element.337), channel_id=1, source_target_pairs={{0,2},{1,3},{2,0},{3,1},{4,6},{5,7},{6,4},{7,5},{8,10},{9,11},{10,... | collective-permute-start | bytes 1572872 | tf_op jit(solution)/shard_map/ppermute | solution.py:285
  43.0 23.6 %collective-permute-start.6 = (f32[16,64,128]{2,1,0:T(8,128)S(1)}, f32[16,64,128]{2,1,0:T(8,128)S(1)}, u32[]{:S(2)}, u32[]{:S(2)}) collective-permute-start(f32[16,64,128]{2,1,0:T(8,128)S(1)} %get-tuple-element.338), channel_id=1, source_target_pairs={{0,1},{1,2},{2,3},{3,0},{4,5},{5,6},{6,7},{7,4},{8,9},{9,10},{10,1... | collective-permute-start | bytes 1572872 | tf_op jit(solution)/shard_map/ppermute | solution.py:285
  45.5 21.2 %collective-permute-start.10 = (f32[64,16,128]{2,1,0:T(8,128)S(1)}, f32[64,16,128]{2,1,0:T(8,128)S(1)}, u32[]{:S(2)}, u32[]{:S(2)}) collective-permute-start(f32[64,16,128]{2,1,0:T(8,128)S(1)} %bitcast.171), channel_id=1, source_target_pairs={{8,0},{12,4},{16,24},{20,28},{9,1},{13,5},{17,25},{21,29},{10,2},{... | collective-permute-start | bytes 1572872 | tf_op jit(solution)/shard_map/ppermute | solution.py:183
  46.8 22.9 %collective-permute-start.12 = (f32[64,16,128]{2,1,0:T(8,128)S(1)}, f32[64,16,128]{2,1,0:T(8,128)S(1)}, u32[]{:S(2)}, u32[]{:S(2)}) collective-permute-start(f32[64,16,128]{2,1,0:T(8,128)S(1)} %get-tuple-element.379.refs_1_.refs_0_), channel_id=1, source_target_pairs={{8,16},{12,20},{16,8},{20,12},{9,17},{13,21},{17,9},{21,13},{10,18... | collective-permute-start | bytes 1572872 | tf_op jit(solution)/shard_map/ppermute | solution.py:183
  56.1 13.6 %collective-permute-start.14 = (f32[64,16,128]{2,1,0:T(8,128)S(1)}, f32[64,16,128]{2,1,0:T(8,128)S(1)}, u32[]{:S(2)}, u32[]{:S(2)}) collective-permute-start(f32[64,16,128]{2,1,0:T(8,128)S(1)} %get-tuple-element.404.refs_2_.refs_0_), channel_id=1, source_target_pairs={{8,16},{12,20},{16,8},{20,12},{9,17},{13,21},{17,9},{21,13},{10,18... | collective-permute-start | bytes 1572872 | tf_op jit(solution)/shard_map/ppermute | solution.py:183
  69.9 63.1 %collective-permute-start.19 = (f32[4,64,16,128]{3,2,1,0:T(8,128)S(1)}, f32[4,64,16,128]{3,2,1,0:T(8,128)S(1)}, u32[]{:S(2)}, u32[]{:S(2)}) collective-permute-start(f32[4,64,16,128]{3,2,1,0:T(8,128)S(1)} %get-tuple-element.367), channel_id=1, source_target_pairs={{0,4},{4,0},{8,12},{12,8},{16,20},{20,16},{24,28},{28,24},{1,5},{5... | collective-permute-start | bytes 6291464 | tf_op jit(solution)/shard_map/ppermute | solution.py:183
  70.0 29.6 %collective-permute-start.11 = (f32[64,16,128]{2,1,0:T(8,128)S(1)}, f32[64,16,128]{2,1,0:T(8,128)S(1)}, u32[]{:S(2)}, u32[]{:S(2)}) collective-permute-start(f32[64,16,128]{2,1,0:T(8,128)S(1)} %get-tuple-element.379.refs_1_.refs_0_), channel_id=1, source_target_pairs={{0,8},{4,12},{24,16},{28,20},{1,9},{5,13},{25,17},{29,21},{2,10},{... | collective-permute-start | bytes 1572872 | tf_op jit(solution)/shard_map/ppermute | solution.py:183
  87.4 23.5 %collective-permute-start.17 = (f32[64,16,128]{2,1,0:T(8,128)S(1)}, f32[64,16,128]{2,1,0:T(8,128)S(1)}, u32[]{:S(2)}, u32[]{:S(2)}) collective-permute-start(f32[64,16,128]{2,1,0:T(8,128)S(1)} %get-tuple-element.404.refs_2_.refs_0_), channel_id=1, source_target_pairs={{0,8},{4,12},{24,16},{28,20},{1,9},{5,13},{25,17},{29,21},{2,10},{... | collective-permute-start | bytes 1572872 | tf_op jit(solution)/shard_map/ppermute | solution.py:183
  99.6 11.9 %collective-permute-start.13 = (f32[64,16,128]{2,1,0:T(8,128)S(1)}, f32[64,16,128]{2,1,0:T(8,128)S(1)}, u32[]{:S(2)}, u32[]{:S(2)}) collective-permute-start(f32[64,16,128]{2,1,0:T(8,128)S(1)} %collective-permute-done.11), channel_id=1, source_target_pairs={{8,16},{12,20},{16,8},{20,12},{9,17},{13,21},{17,9},{21,13},{10,18... | collective-permute-start | bytes 1572872 | tf_op jit(solution)/shard_map/ppermute | solution.py:183
  100.3 21.3 %collective-permute-start.21 = (f32[64,16,128]{2,1,0:T(8,128)S(1)}, f32[64,16,128]{2,1,0:T(8,128)S(1)}, u32[]{:S(2)}, u32[]{:S(2)}) collective-permute-start(f32[64,16,128]{2,1,0:T(8,128)S(1)} %get-tuple-element.442.refs_3_.refs_0_), channel_id=1, source_target_pairs={{0,8},{4,12},{24,16},{28,20},{1,9},{5,13},{25,17},{29,21},{2,10},{... | collective-permute-start | bytes 1572872 | tf_op jit(solution)/shard_map/ppermute | solution.py:183
  110.9 15.2 %collective-permute-start.18 = (f32[64,16,128]{2,1,0:T(8,128)S(1)}, f32[64,16,128]{2,1,0:T(8,128)S(1)}, u32[]{:S(2)}, u32[]{:S(2)}) collective-permute-start(f32[64,16,128]{2,1,0:T(8,128)S(1)} %collective-permute-done.17), channel_id=1, source_target_pairs={{8,16},{12,20},{16,8},{20,12},{9,17},{13,21},{17,9},{21,13},{10,18... | collective-permute-start | bytes 1572872 | tf_op jit(solution)/shard_map/ppermute | solution.py:183
  113.2 17.5 %collective-permute-start.16 = (f32[64,16,128]{2,1,0:T(8,128)S(1)}, f32[64,16,128]{2,1,0:T(8,128)S(1)}, u32[]{:S(2)}, u32[]{:S(2)}) collective-permute-start(f32[64,16,128]{2,1,0:T(8,128)S(1)} %bitcast.172), channel_id=1, source_target_pairs={{8,0},{12,4},{16,24},{20,28},{9,1},{13,5},{17,25},{21,29},{10,2},{... | collective-permute-start | bytes 1572872 | tf_op jit(solution)/shard_map/ppermute | solution.py:183
  114.5 22.6 %collective-permute-start.23 = (f32[16,64,128]{2,1,0:T(8,128)S(1)}, f32[16,64,128]{2,1,0:T(8,128)S(1)}, u32[]{:S(2)}, u32[]{:S(2)}) collective-permute-start(f32[16,64,128]{2,1,0:T(8,128)S(1)} %get-tuple-element.390), channel_id=1, source_target_pairs={{0,3},{1,0},{2,1},{3,2},{4,7},{5,4},{6,5},{7,6},{8,11},{9,8},{10,9... | collective-permute-start | bytes 1572872 | tf_op jit(solution)/shard_map/ppermute | solution.py:285
  121.6 16.8 %collective-permute-start.32 = (f32[64,16,128]{2,1,0:T(8,128)S(1)}, f32[64,16,128]{2,1,0:T(8,128)S(1)}, u32[]{:S(2)}, u32[]{:S(2)}) collective-permute-start(f32[64,16,128]{2,1,0:T(8,128)S(1)} %get-tuple-element.468), channel_id=1, source_target_pairs={{0,8},{4,12},{24,16},{28,20},{1,9},{5,13},{25,17},{29,21},{2,10},{... | collective-permute-start | bytes 1572872 | tf_op jit(solution)/shard_map/ppermute | solution.py:183
  126.1 24.5 %collective-permute-start.24 = (f32[16,64,128]{2,1,0:T(8,128)S(1)}, f32[16,64,128]{2,1,0:T(8,128)S(1)}, u32[]{:S(2)}, u32[]{:S(2)}) collective-permute-start(f32[16,64,128]{2,1,0:T(8,128)S(1)} %get-tuple-element.391), channel_id=1, source_target_pairs={{0,2},{1,3},{2,0},{3,1},{4,6},{5,7},{6,4},{7,5},{8,10},{9,11},{10,... | collective-permute-start | bytes 1572872 | tf_op jit(solution)/shard_map/ppermute | solution.py:285
  130.7 19.8 %collective-permute-start.25 = (f32[16,64,128]{2,1,0:T(8,128)S(1)}, f32[16,64,128]{2,1,0:T(8,128)S(1)}, u32[]{:S(2)}, u32[]{:S(2)}) collective-permute-start(f32[16,64,128]{2,1,0:T(8,128)S(1)} %get-tuple-element.392), channel_id=1, source_target_pairs={{0,1},{1,2},{2,3},{3,0},{4,5},{5,6},{6,7},{7,4},{8,9},{9,10},{10,1... | collective-permute-start | bytes 1572872 | tf_op jit(solution)/shard_map/ppermute | solution.py:285
  133.0 19.1 %collective-permute-start.22 = (f32[64,16,128]{2,1,0:T(8,128)S(1)}, f32[64,16,128]{2,1,0:T(8,128)S(1)}, u32[]{:S(2)}, u32[]{:S(2)}) collective-permute-start(f32[64,16,128]{2,1,0:T(8,128)S(1)} %collective-permute-done.21), channel_id=1, source_target_pairs={{8,16},{12,20},{16,8},{20,12},{9,17},{13,21},{17,9},{21,13},{10,18... | collective-permute-start | bytes 1572872 | tf_op jit(solution)/shard_map/ppermute | solution.py:183
  137.1 22.6 %collective-permute-start.20 = (f32[64,16,128]{2,1,0:T(8,128)S(1)}, f32[64,16,128]{2,1,0:T(8,128)S(1)}, u32[]{:S(2)}, u32[]{:S(2)}) collective-permute-start(f32[64,16,128]{2,1,0:T(8,128)S(1)} %bitcast.168), channel_id=1, source_target_pairs={{8,0},{12,4},{16,24},{20,28},{9,1},{13,5},{17,25},{21,29},{10,2},{... | collective-permute-start | bytes 1572872 | tf_op jit(solution)/shard_map/ppermute | solution.py:183
  138.4 25.4 %collective-permute-start.33 = (f32[64,16,128]{2,1,0:T(8,128)S(1)}, f32[64,16,128]{2,1,0:T(8,128)S(1)}, u32[]{:S(2)}, u32[]{:S(2)}) collective-permute-start(f32[64,16,128]{2,1,0:T(8,128)S(1)} %collective-permute-done.32), channel_id=1, source_target_pairs={{8,16},{12,20},{16,8},{20,12},{9,17},{13,21},{17,9},{21,13},{10,18... | collective-permute-start | bytes 1572872 | tf_op jit(solution)/shard_map/ppermute | solution.py:183
  153.8 14.2 %collective-permute-start.26 = (f32[64,16,128]{2,1,0:T(8,128)S(1)}, f32[64,16,128]{2,1,0:T(8,128)S(1)}, u32[]{:S(2)}, u32[]{:S(2)}) collective-permute-start(f32[64,16,128]{2,1,0:T(8,128)S(1)} %bitcast.170), channel_id=1, source_target_pairs={{8,0},{12,4},{16,24},{20,28},{9,1},{13,5},{17,25},{21,29},{10,2},{... | collective-permute-start | bytes 1572872 | tf_op jit(solution)/shard_map/ppermute | solution.py:183
  155.1 16.9 %collective-permute-start.31 = (f32[64,16,128]{2,1,0:T(8,128)S(1)}, f32[64,16,128]{2,1,0:T(8,128)S(1)}, u32[]{:S(2)}, u32[]{:S(2)}) collective-permute-start(f32[64,16,128]{2,1,0:T(8,128)S(1)} %get-tuple-element.480), channel_id=1, source_target_pairs={{0,8},{4,12},{24,16},{28,20},{1,9},{5,13},{25,17},{29,21},{2,10},{... | collective-permute-start | bytes 1572872 | tf_op jit(solution)/shard_map/ppermute | solution.py:183
  159.7 16.6 %collective-permute-start.28 = (f32[16,64,128]{2,1,0:T(8,128)S(1)}, f32[16,64,128]{2,1,0:T(8,128)S(1)}, u32[]{:S(2)}, u32[]{:S(2)}) collective-permute-start(f32[16,64,128]{2,1,0:T(8,128)S(1)} %get-tuple-element.453), channel_id=1, source_target_pairs={{0,3},{1,0},{2,1},{3,2},{4,7},{5,4},{6,5},{7,6},{8,11},{9,8},{10,9... | collective-permute-start | bytes 1572872 | tf_op jit(solution)/shard_map/ppermute | solution.py:285
  159.8 16.6 %collective-permute-start.29 = (f32[16,64,128]{2,1,0:T(8,128)S(1)}, f32[16,64,128]{2,1,0:T(8,128)S(1)}, u32[]{:S(2)}, u32[]{:S(2)}) collective-permute-start(f32[16,64,128]{2,1,0:T(8,128)S(1)} %get-tuple-element.454), channel_id=1, source_target_pairs={{0,2},{1,3},{2,0},{3,1},{4,6},{5,7},{6,4},{7,5},{8,10},{9,11},{10,... | collective-permute-start | bytes 1572872 | tf_op jit(solution)/shard_map/ppermute | solution.py:285
  163.8 16.6 %collective-permute-start.27 = (f32[64,16,128]{2,1,0:T(8,128)S(1)}, f32[64,16,128]{2,1,0:T(8,128)S(1)}, u32[]{:S(2)}, u32[]{:S(2)}) collective-permute-start(f32[64,16,128]{2,1,0:T(8,128)S(1)} %get-tuple-element.508), channel_id=1, source_target_pairs={{0,8},{4,12},{24,16},{28,20},{1,9},{5,13},{25,17},{29,21},{2,10},{... | collective-permute-start | bytes 1572872 | tf_op jit(solution)/shard_map/ppermute | solution.py:183
  168.0 16.8 %collective-permute-start.30 = (f32[16,64,128]{2,1,0:T(8,128)S(1)}, f32[16,64,128]{2,1,0:T(8,128)S(1)}, u32[]{:S(2)}, u32[]{:S(2)}) collective-permute-start(f32[16,64,128]{2,1,0:T(8,128)S(1)} %get-tuple-element.455), channel_id=1, source_target_pairs={{0,1},{1,2},{2,3},{3,0},{4,5},{5,6},{6,7},{7,4},{8,9},{9,10},{10,1... | collective-permute-start | bytes 1572872 | tf_op jit(solution)/shard_map/ppermute | solution.py:285
  171.9 31.4 %collective-permute-start.34 = (f32[64,16,128]{2,1,0:T(8,128)S(1)}, f32[64,16,128]{2,1,0:T(8,128)S(1)}, u32[]{:S(2)}, u32[]{:S(2)}) collective-permute-start(f32[64,16,128]{2,1,0:T(8,128)S(1)} %collective-permute-done.31), channel_id=1, source_target_pairs={{8,16},{12,20},{16,8},{20,12},{9,17},{13,21},{17,9},{21,13},{10,18... | collective-permute-start | bytes 1572872 | tf_op jit(solution)/shard_map/ppermute | solution.py:183
  176.3 11.9 %collective-permute-start.39 = (f32[17,16,128]{2,1,0:T(8,128)S(1)}, f32[17,16,128]{2,1,0:T(8,128)S(1)}, u32[]{:S(2)}, u32[]{:S(2)}) collective-permute-start(f32[17,16,128]{2,1,0:T(8,128)S(1)} %get-tuple-element.496), channel_id=1, source_target_pairs={{0,2},{1,3},{2,0},{3,1},{4,6},{5,7},{6,4},{7,5},{8,10},{9,11},{10,... | collective-permute-start | bytes 417800 | tf_op jit(solution)/shard_map/ppermute | solution.py:285
  180.4 30.6 %collective-permute-start.35 = (f32[64,16,128]{2,1,0:T(8,128)S(1)}, f32[64,16,128]{2,1,0:T(8,128)S(1)}, u32[]{:S(2)}, u32[]{:S(2)}) collective-permute-start(f32[64,16,128]{2,1,0:T(8,128)S(1)} %collective-permute-done.27), channel_id=1, source_target_pairs={{8,16},{12,20},{16,8},{20,12},{9,17},{13,21},{17,9},{21,13},{10,18... | collective-permute-start | bytes 1572872 | tf_op jit(solution)/shard_map/ppermute | solution.py:183
  184.8 24.6 %collective-permute-start.36 = (f32[16,48,128]{2,1,0:T(8,128)S(1)}, f32[16,48,128]{2,1,0:T(8,128)S(1)}, u32[]{:S(2)}, u32[]{:S(2)}) collective-permute-start(f32[16,48,128]{2,1,0:T(8,128)S(1)} %get-tuple-element.493), channel_id=1, source_target_pairs={{0,3},{1,0},{2,1},{3,2},{4,7},{5,4},{6,5},{7,6},{8,11},{9,8},{10,9... | collective-permute-start | bytes 1179656 | tf_op jit(solution)/shard_map/ppermute | solution.py:285
  187.3 22.1 %collective-permute-start.38 = (f32[16,48,128]{2,1,0:T(8,128)S(1)}, f32[16,48,128]{2,1,0:T(8,128)S(1)}, u32[]{:S(2)}, u32[]{:S(2)}) collective-permute-start(f32[16,48,128]{2,1,0:T(8,128)S(1)} %get-tuple-element.495), channel_id=1, source_target_pairs={{0,2},{1,3},{2,0},{3,1},{4,6},{5,7},{6,4},{7,5},{8,10},{9,11},{10,... | collective-permute-start | bytes 1179656 | tf_op jit(solution)/shard_map/ppermute | solution.py:285
  188.2 21.2 %collective-permute-start.40 = (f32[16,48,128]{2,1,0:T(8,128)S(1)}, f32[16,48,128]{2,1,0:T(8,128)S(1)}, u32[]{:S(2)}, u32[]{:S(2)}) collective-permute-start(f32[16,48,128]{2,1,0:T(8,128)S(1)} %get-tuple-element.497), channel_id=1, source_target_pairs={{0,1},{1,2},{2,3},{3,0},{4,5},{5,6},{6,7},{7,4},{8,9},{9,10},{10,1... | collective-permute-start | bytes 1179656 | tf_op jit(solution)/shard_map/ppermute | solution.py:285
  212.5 38.3 %collective-permute-start.42 = (f32[4,64,16,128]{3,2,1,0:T(8,128)S(1)}, f32[4,64,16,128]{3,2,1,0:T(8,128)S(1)}, u32[]{:S(2)}, u32[]{:S(2)}) collective-permute-start(f32[4,64,16,128]{3,2,1,0:T(8,128)S(1)} %shard_map.109), channel_id=1, source_target_pairs={{0,4},{4,0},{8,12},{12,8},{16,20},{20,16},{24,28},{28,24},{1,5},{5... | collective-permute-start | bytes 6291464 | tf_op jit(solution)/shard_map/ppermute | solution.py:183
  212.6 15.6 %collective-permute-start.43 = (f32[64,16,128]{2,1,0:T(8,128)S(1)}, f32[64,16,128]{2,1,0:T(8,128)S(1)}, u32[]{:S(2)}, u32[]{:S(2)}) collective-permute-start(f32[64,16,128]{2,1,0:T(8,128)S(1)} %get-tuple-element.533), channel_id=1, source_target_pairs={{0,8},{4,12},{24,16},{28,20},{1,9},{5,13},{25,17},{29,21},{2,10},{... | collective-permute-start | bytes 1572872 | tf_op jit(solution)/shard_map/ppermute | solution.py:183
  228.9 16.9 %collective-permute-start.49 = (f32[64,16,128]{2,1,0:T(8,128)S(1)}, f32[64,16,128]{2,1,0:T(8,128)S(1)}, u32[]{:S(2)}, u32[]{:S(2)}) collective-permute-start(f32[64,16,128]{2,1,0:T(8,128)S(1)} %bitcast.167), channel_id=1, source_target_pairs={{8,0},{12,4},{16,24},{20,28},{9,1},{13,5},{17,25},{21,29},{10,2},{... | collective-permute-start | bytes 1572872 | tf_op jit(solution)/shard_map/ppermute | solution.py:183
  230.2 16.7 %collective-permute-start.46 = (f32[16,64,128]{2,1,0:T(8,128)S(1)}, f32[16,64,128]{2,1,0:T(8,128)S(1)}, u32[]{:S(2)}, u32[]{:S(2)}) collective-permute-start(f32[16,64,128]{2,1,0:T(8,128)S(1)} %get-tuple-element.548), channel_id=1, source_target_pairs={{0,3},{1,0},{2,1},{3,2},{4,7},{5,4},{6,5},{7,6},{8,11},{9,8},{10,9... | collective-permute-start | bytes 1572872 | tf_op jit(solution)/shard_map/ppermute | solution.py:285
  233.0 15.2 %collective-permute-start.50 = (f32[8,128]{1,0:T(8,128)S(1)}, f32[8,128]{1,0:T(8,128)S(1)}, u32[]{:S(2)}, u32[]{:S(2)}) collective-permute-start(f32[8,128]{1,0:T(8,128)S(1)} %shard_map.111.a_ref), channel_id=1, source_target_pairs={{0,8},{4,12},{8,0},{12,4},{16,24},{20,28},{24,16},{28,20},{1,9},{5... | collective-permute-start | bytes 12296 | tf_op jit(solution)/shard_map/ppermute | solution.py:183
  237.9 25.3 %collective-permute-start.47 = (f32[16,64,128]{2,1,0:T(8,128)S(1)}, f32[16,64,128]{2,1,0:T(8,128)S(1)}, u32[]{:S(2)}, u32[]{:S(2)}) collective-permute-start(f32[16,64,128]{2,1,0:T(8,128)S(1)} %get-tuple-element.549), channel_id=1, source_target_pairs={{0,2},{1,3},{2,0},{3,1},{4,6},{5,7},{6,4},{7,5},{8,10},{9,11},{10,... | collective-permute-start | bytes 1572872 | tf_op jit(solution)/shard_map/ppermute | solution.py:285
  245.8 17.4 %collective-permute-start.48 = (f32[16,64,128]{2,1,0:T(8,128)S(1)}, f32[16,64,128]{2,1,0:T(8,128)S(1)}, u32[]{:S(2)}, u32[]{:S(2)}) collective-permute-start(f32[16,64,128]{2,1,0:T(8,128)S(1)} %get-tuple-element.550), channel_id=1, source_target_pairs={{0,1},{1,2},{2,3},{3,0},{4,5},{5,6},{6,7},{7,4},{8,9},{9,10},{10,1... | collective-permute-start | bytes 1572872 | tf_op jit(solution)/shard_map/ppermute | solution.py:285
  246.9 16.7 %collective-permute-start.51 = (f32[64,16,128]{2,1,0:T(8,128)S(1)}, f32[64,16,128]{2,1,0:T(8,128)S(1)}, u32[]{:S(2)}, u32[]{:S(2)}) collective-permute-start(f32[64,16,128]{2,1,0:T(8,128)S(1)} %bitcast.165), channel_id=1, source_target_pairs={{8,0},{12,4},{16,24},{20,28},{9,1},{13,5},{17,25},{21,29},{10,2},{... | collective-permute-start | bytes 1572872 | tf_op jit(solution)/shard_map/ppermute | solution.py:183
  248.2 26.6 %collective-permute-start.52 = (f32[64,16,128]{2,1,0:T(8,128)S(1)}, f32[64,16,128]{2,1,0:T(8,128)S(1)}, u32[]{:S(2)}, u32[]{:S(2)}) collective-permute-start(f32[64,16,128]{2,1,0:T(8,128)S(1)} %bitcast.166), channel_id=1, source_target_pairs={{8,0},{12,4},{16,24},{20,28},{9,1},{13,5},{17,25},{21,29},{10,2},{... | collective-permute-start | bytes 1572872 | tf_op jit(solution)/shard_map/ppermute | solution.py:183
  250.8 33.0 %collective-permute-start.53 = (f32[64,16,128]{2,1,0:T(8,128)S(1)}, f32[64,16,128]{2,1,0:T(8,128)S(1)}, u32[]{:S(2)}, u32[]{:S(2)}) collective-permute-start(f32[64,16,128]{2,1,0:T(8,128)S(1)} %bitcast.169), channel_id=1, source_target_pairs={{8,0},{12,4},{16,24},{20,28},{9,1},{13,5},{17,25},{21,29},{10,2},{... | collective-permute-start | bytes 1572872 | tf_op jit(solution)/shard_map/ppermute | solution.py:183
  (16 other events, 139.7 us)
